TPU v7x, 256 devices: a whole 4x4x8 slice. The times are simulated.
256 devices in a mesh: aux: 64 (over x, z, core), pair: 4 (over y).
Axes of the slice: x: 4, y: 4, z: 8, core: 2. Of those that a mesh axis runs over, the one named last changes fastest.
Arguments:
- three_centre: bfloat16 [16, 1280, 128, 128], P('pair', 'aux'), may hold values from -6 to 6
- block_mask: int32 [16], replicated, may hold values from 0 to 1, as said below
- block_owner: int32 [16], replicated, may hold values from 0 to 3, as said below
- block_index: int32 [2, 16], replicated, may hold values from 0 to 23
- active_orbitals: bfloat16 [24, 3072], replicated, may hold values from -0.5 to 0.5
- inactive_orbitals: bfloat16 [256, 3072], replicated, may hold values from -0.75 to 0.75
Outputs:
- fock_blocks: float32 [32, 128, 128], P('pair')
- active_integrals: float32 [576, 576], P('aux')
Inputs may be any that keep to these rules, and one draw needn't show every extreme that they name: `block_mask`: every index of pair holds at least 2 live slots. `block_owner`: among the 4 slots of one index of pair, live or not, at most 2 name any one owner; one owner is named by exactly 2 live slots of every index of pair, so it receives 8 live blocks.
All inputs are finite; a program needn't handle non-finite values.
Results may differ from a plain program's by a relative error of at most 0.0044.
Values may be sent and summed in bfloat16 or wider, within the bound.
No kernel may reach another device: no remote copies, remote signals or barrier semaphores. Data moves between devices by JAX's collectives and lax.ppermute only.
A program may use at most 64 MiB of HBM per device.

v0:
```python
import math

import jax
import jax.numpy as jnp
from jax import lax
from jax.experimental import pallas as pl
from jax.experimental.pallas import tpu as pltpu
from jax.sharding import Mesh, PartitionSpec as P

SLOTS = 4
ROWS = 20
BW = 128
ACT = 24
PAIRS = 576
GROUPS = 4
PER = 5
USED = PER * ACT
NX = 4
NZ = 8
CHIPS = NX * NZ
CORES = 2
OWNERS = 4
AUX = 1280
MSG = 24
F32 = jnp.float32
BF16 = jnp.bfloat16

HBM = pl.BlockSpec(memory_space=pltpu.HBM)
VMEM = pl.BlockSpec(memory_space=pltpu.VMEM)
SMEM = pl.BlockSpec(memory_space=pltpu.SMEM)


def limit(kib):
    return pltpu.CompilerParams(vmem_limit_bytes=kib << 10)


def nt(a, b):
    return lax.dot_general(a, b, (((1,), (1,)), ((), ())), preferred_element_type=F32)


def lanes(shape):
    return lax.broadcasted_iota(jnp.int32, shape, len(shape) - 1)


def sublanes(shape):
    return lax.broadcasted_iota(jnp.int32, shape, len(shape) - 2)


def contract_kernel(
    mask_hbm, index_hbm, blocks_hbm, active_hbm, inactive_hbm, out_ref, blocks,
    mask_ref, index_ref, act_row, act_col, ina_row, ina_col, wide, halves, sums,
    block_sem, ar_sem, ac_sem, ir_sem, ic_sem, int_sem,
):
    here = lax.axis_index("pair")
    ints = [
        pltpu.make_async_copy(index_hbm, index_ref, int_sem.at[0]),
        pltpu.make_async_copy(mask_hbm, mask_ref, int_sem.at[1]),
    ]
    for c in ints:
        c.start()
    whole = [
        pltpu.make_async_copy(blocks_hbm.at[g], blocks.at[g], block_sem.at[g]) for g in range(SLOTS)
    ]
    for c in whole:
        c.start()
    wide[...] = jnp.zeros_like(wide)
    for c in ints:
        c.wait()
    copies = []
    for g in range(SLOTS):
        slot = here * SLOTS + g
        row = pl.multiple_of(index_ref[0, slot] * BW, BW)
        col = pl.multiple_of(index_ref[1, slot] * BW, BW)
        group = [
            pltpu.make_async_copy(inactive_hbm.at[:, pl.ds(row, BW)], ina_row.at[g], ir_sem.at[g]),
            pltpu.make_async_copy(inactive_hbm.at[:, pl.ds(col, BW)], ina_col.at[g], ic_sem.at[g]),
            pltpu.make_async_copy(active_hbm.at[:, pl.ds(row, BW)], act_row.at[g], ar_sem.at[g]),
            pltpu.make_async_copy(active_hbm.at[:, pl.ds(col, BW)], act_col.at[g], ac_sem.at[g]),
        ]
        for c in group:
            c.start()
        copies.append(group + [whole[g]])
    for g in range(SLOTS):
        live = mask_ref[here * SLOTS + g].astype(F32)
        for c in copies[g]:
            c.wait()
        density = lax.dot_general(
            ina_row[g], ina_col[g], (((0,), (0,)), ((), ())), preferred_element_type=F32
        )
        density = density.astype(BF16).astype(F32) * live
        for p in range(ROWS):
            product = blocks[g, p].astype(F32) * density
            part = jnp.sum(product.reshape(BW // 8, 8, BW), axis=0)
            if g == 0:
                sums[p] = part
            else:
                sums[p] = sums[p] + part
        column = act_col[g].astype(F32)
        for p in range(PER):
            wide[pl.ds(ACT * p, ACT), pl.ds(BW * p, BW)] = column
        weights = wide[...].astype(BF16)
        for k in range(GROUPS):
            joined = jnp.concatenate([blocks[g, k * PER + p] for p in range(PER)], axis=1)
            half = nt(joined, weights)
            halves[pl.ds(g * BW, BW), pl.ds(k * BW, BW)] = half.astype(BF16)
    rows = jnp.concatenate(
        [
            act_row[g].astype(F32) * mask_ref[here * SLOTS + g].astype(F32)
            for g in range(SLOTS)
        ],
        axis=1,
    ).astype(BF16)
    fitted = jnp.dot(rows, halves[...], preferred_element_type=F32)
    coupling = jnp.sum(jnp.sum(sums[...], axis=1), axis=1, keepdims=True) * (1.0 / BW)
    coupling = jnp.concatenate([coupling, jnp.zeros((ACT - ROWS, 1), F32)], axis=0)
    high = coupling.astype(BF16).astype(F32)
    low = coupling - high
    spare = lanes((ACT, BW)) >= USED
    for k in range(GROUPS):
        tail = high if k == 0 else low if k == 1 else jnp.zeros_like(high)
        tile = jnp.where(spare, jnp.broadcast_to(tail, (ACT, BW)), fitted[:, k * BW : (k + 1) * BW])
        out_ref[:, pl.ds(k * BW, BW)] = tile.astype(BF16)


def expand_kernel(
    own_ref, one_ref, two_ref, three_ref, blocks, keep_ref, send_ref,
    coupling_ref, spread, left, coulomb, main, rest,
):
    here = lax.axis_index("pair")
    core = lax.axis_index("core")
    total = (own_ref[...].astype(F32) + two_ref[...].astype(F32)) + (
        one_ref[...].astype(F32) + three_ref[...].astype(F32)
    )
    both = total[:, :BW] + total[:, BW : 2 * BW]
    coupling = jnp.sum(jnp.where(lanes((ACT, BW)) == USED, both, 0.0), axis=1, keepdims=True)
    coupling_ref[...] = jnp.broadcast_to(coupling.astype(BF16).astype(F32), (ACT, BW))
    fitted = total.astype(BF16).astype(F32)
    offset = lanes((ACT, BW)) - sublanes((ACT, BW))
    keep = offset == 0
    for p in range(1, PER):
        keep = keep | (offset == ACT * p)
    keep = jnp.concatenate([keep.astype(F32)] * GROUPS, axis=1)
    for t in range(0, ACT, 2):
        pair = jnp.concatenate(
            [jnp.broadcast_to(fitted[t + d : t + d + 1, :], keep.shape) * keep for d in range(2)],
            axis=0,
        )
        spread[pl.ds(t * ACT, 2 * ACT), :] = pair.astype(BF16)
    shape = (GROUPS * BW, BW)
    lane = lanes(shape)
    group = (
        (lane >= PER).astype(jnp.int32)
        + (lane >= 2 * PER).astype(jnp.int32)
        + (lane >= 3 * PER).astype(jnp.int32)
    )
    start = group * BW + (lane - group * PER) * ACT
    position = sublanes(shape) - start
    pick = (position >= 0) & (position < ACT) & (lane < ROWS)
    folded = jnp.dot(
        spread[...], pick.astype(F32).astype(BF16), preferred_element_type=F32
    ).astype(BF16)
    left[...] = folded
    columns = left[pl.ds(pl.multiple_of(here * BW, BW), BW), :]
    tail = left[pl.ds(4 * BW, PAIRS - 4 * BW), :]
    main[...] = nt(folded, columns)
    rest[...] = nt(folded, jnp.concatenate([tail, tail], axis=0))
    for g in range(SLOTS):
        total_g = jnp.zeros((BW, BW), F32)
        for p in range(ROWS):
            factor = jnp.broadcast_to(coupling_ref[pl.ds(p, 1), :], (BW, BW))
            total_g = total_g + blocks[g, p].astype(F32) * factor
        coulomb[pl.ds(g * BW, BW), :] = total_g
    low_lane = lanes((CHIPS, BW)) < BW // 2
    for ref, which in ((keep_ref, core), (send_ref, 1 - core)):
        for x in range(NX):
            for z in range(NZ):
                row = pl.multiple_of(z // 2 * BW + 32 * x + 16 * which + 8 * (z % 2), 8)
                ref[pl.ds((x * NZ + z) * MSG, 8), :] = coulomb[pl.ds(row, 8), :]
        for s in range(9):
            ref[pl.ds(8 + s, CHIPS, stride=MSG), :] = main[pl.ds(9 * which + s, CHIPS, stride=18), :]
        for s in range(7):
            value = rest[pl.ds(9 * which + s, CHIPS, stride=18), :]
            if s < 2:
                other = rest[pl.ds(9 * which + 7 + s, CHIPS, stride=18), :]
                value = jnp.where(low_lane, value, other)
            ref[pl.ds(17 + s, CHIPS, stride=MSG), :] = value


def along_x_kernel(parts_ref, out_ref):
    total = jnp.sum(parts_ref[...].astype(F32), axis=0)
    pieces = [total[z * MSG : (z + 1) * MSG] for z in range(NZ)]
    fock = jnp.concatenate([p[0:8] for p in pieces], axis=0).astype(BF16)
    for z in range(NZ):
        out_ref[z, 0:64, :] = fock
        out_ref[z, 64:80, :] = pieces[z][8:MSG].astype(BF16)


def route_kernel(mask_ref, owner_ref, parts_ref, out_ref, tile):
    here = lax.axis_index("pair")
    total = jnp.sum(parts_ref[...].astype(F32), axis=0)
    gram = total[64:80] * (1.0 / AUX)
    high = gram.astype(BF16)
    low = (gram - high.astype(F32)).astype(BF16)
    scaled = total[0:64] * (1.0 / math.sqrt(AUX))
    tile[...] = jnp.zeros_like(tile)
    for o in range(OWNERS):
        place = jnp.int32(0)
        for g in range(SLOTS):
            slot = here * SLOTS + g
            chosen = (mask_ref[slot] == 1) & (owner_ref[slot] == o)

            @pl.when(chosen & (place < 2))
            def _(o=o, g=g, place=place):
                tile[o, pl.ds(pl.multiple_of(16 * place, 16), 16), :] = scaled[16 * g : 16 * g + 16]

            place = place + chosen.astype(jnp.int32)
    for o in range(OWNERS):
        piece = tile[o].astype(BF16)
        for x in range(NX):
            out_ref[o * NX + x, 0:32, :] = piece
            out_ref[o * NX + x, 32:48, :] = high
            out_ref[o * NX + x, 48:64, :] = low


def place_kernel(mask_ref, owner_ref, own_ref, other_ref, fock_ref, gram_ref):
    here = lax.axis_index("pair")
    core = lax.axis_index("core")
    along = lax.axis_index("x")
    fock_ref[...] = jnp.zeros_like(fock_ref)
    rank = jnp.int32(0)
    for q in range(OWNERS):
        place = jnp.int32(0)
        for g in range(SLOTS):
            slot = q * SLOTS + g
            chosen = (mask_ref[slot] == 1) & (owner_ref[slot] == here)

            @pl.when(chosen & (place < 2))
            def _(q=q, rank=rank, place=place):
                source = pl.ds(pl.multiple_of(16 * place, 16), 16)
                for n, ref in enumerate((own_ref, other_ref)):
                    which = core if n == 0 else 1 - core
                    for x in range(NX):
                        row = pl.multiple_of(rank * BW + 32 * x + 16 * which, 16)
                        fock_ref[pl.ds(row, 16), :] = ref[q * NX + x, source, :].astype(F32)

            place = place + chosen.astype(jnp.int32)
            rank = rank + chosen.astype(jnp.int32)
    for q in range(OWNERS):
        high = own_ref[q * NX + along, 32:48, :].astype(F32)
        low = own_ref[q * NX + along, 48:64, :].astype(F32)
        gram = high + low
        gram_ref[:, q * BW : (q + 1) * BW] = gram[0:9]
        if q == 0:
            gram_ref[0:7, 4 * BW : PAIRS] = gram[9:16, 0 : BW // 2]
            gram_ref[7:9, 4 * BW : PAIRS] = gram[9:11, BW // 2 : BW]


def from_others(x):
    return [
        lax.ppermute(x, "pair", [(i, (i + s) % OWNERS) for i in range(OWNERS)])
        for s in range(1, OWNERS)
    ]


def shards(three_centre, block_mask, block_owner, block_index, active_orbitals, inactive_orbitals):
    dma = pltpu.SemaphoreType.DMA
    pinned = [
        pltpu.with_memory_space_constraint(a, pltpu.HBM)
        for a in (block_mask, block_index, three_centre, active_orbitals, inactive_orbitals)
    ]
    message, blocks = pl.pallas_call(
        contract_kernel,
        out_shape=[
            pltpu.VMEM((ACT, GROUPS * BW), BF16),
            pltpu.VMEM((SLOTS, ROWS, BW, BW), BF16),
        ],
        in_specs=[HBM] * 5,
        out_specs=[VMEM, VMEM],
        scratch_shapes=[
            pltpu.SMEM((16,), jnp.int32),
            pltpu.SMEM((2, 16), jnp.int32),
            pltpu.VMEM((SLOTS, ACT, BW), BF16),
            pltpu.VMEM((SLOTS, ACT, BW), BF16),
            pltpu.VMEM((SLOTS, 256, BW), BF16),
            pltpu.VMEM((SLOTS, 256, BW), BF16),
            pltpu.VMEM((BW, PER * BW), F32),
            pltpu.VMEM((SLOTS * BW, GROUPS * BW), BF16),
            pltpu.VMEM((ROWS, 8, BW), F32),
            dma((SLOTS,)), dma((SLOTS,)), dma((SLOTS,)), dma((SLOTS,)), dma((SLOTS,)), dma((2,)),
        ],
        compiler_params=limit(8192),
        name="contract",
    )(*pinned)
    one, two, three = from_others(message)
    rows = CHIPS * MSG
    keep, send = pl.pallas_call(
        expand_kernel,
        out_shape=[pltpu.VMEM((rows, BW), F32)] * 2,
        in_specs=[VMEM] * 5,
        out_specs=[VMEM, VMEM],
        scratch_shapes=[
            pltpu.VMEM((ACT, BW), F32),
            pltpu.VMEM((PAIRS, GROUPS * BW), BF16),
            pltpu.VMEM((PAIRS, BW), BF16),
            pltpu.VMEM((SLOTS * BW, BW), F32),
            pltpu.VMEM((PAIRS, BW), F32),
            pltpu.VMEM((PAIRS, BW), F32),
        ],
        compiler_params=limit(8192),
        name="expand",
    )(message, one, two, three, blocks)
    swap = [(0, 1), (1, 0)]
    chip_sum = (keep + lax.ppermute(send, "core", swap)).astype(BF16)
    along_x = lax.all_to_all(chip_sum.reshape(NX, NZ * MSG, BW), "x", 0, 0, tiled=True)
    pieces = pl.pallas_call(
        along_x_kernel,
        out_shape=pltpu.VMEM((NZ, 80, BW), BF16),
        in_specs=[VMEM],
        out_specs=VMEM,
        compiler_params=limit(4096),
        name="along_x",
    )(along_x)
    along_z = lax.all_to_all(pieces, "z", 0, 0, tiled=True)
    pieces = pl.pallas_call(
        route_kernel,
        out_shape=pltpu.VMEM((OWNERS * NX, 64, BW), BF16),
        in_specs=[SMEM, SMEM, VMEM],
        out_specs=VMEM,
        scratch_shapes=[pltpu.VMEM((OWNERS, 32, BW), F32)],
        compiler_params=limit(4096),
        name="route",
    )(block_mask, block_owner, along_z)
    received = lax.all_to_all(pieces, ("pair", "x"), 0, 0, tiled=True)
    partner = lax.ppermute(received, "core", swap)
    fock, integrals = pl.pallas_call(
        place_kernel,
        out_shape=[
            jax.ShapeDtypeStruct((8 * BW, BW), F32),
            jax.ShapeDtypeStruct((9, PAIRS), F32),
        ],
        in_specs=[SMEM, SMEM, VMEM, VMEM],
        out_specs=[VMEM, VMEM],
        compiler_params=limit(4096),
        name="place",
    )(block_mask, block_owner, received, partner)
    return (fock.reshape(8, BW, BW), integrals)


def solution(mesh):
    split = Mesh(mesh.devices.reshape(NX, NZ, CORES, OWNERS), ("x", "z", "core", "pair"))
    aux = ("x", "z", "core")
    return jax.shard_map(
        shards,
        mesh=split,
        in_specs=(P("pair", aux, None, None), P(), P(), P(), P(), P()),
        out_specs=(P("pair", None, None), P(aux, None)),
        check_vma=False,
    )
```

profile of v0, /device:TPU:1, one launch (start us, length us, event | category | flops | bytes accessed | tf_op | source)
XLA Modules:
  0.0 61.9 jit_solution(3653241215340701022)
XLA Ops:
  0.6 4.0 %contract.1 = (bf16[24,512]{1,0:T(8,128)(2,1)S(1)}, bf16[4,20,128,128]{3,2,1,0:T(8,128)(2,1)S(1)}) custom-call(s32[16]{0:T(128)} %mask_ref.3, s32[2,16]{1,0:T(2,128)} %index_hbm.1, bf16[4,20,128,128]{3,2,1,0:T(8,128)(2,1)} %blocks_hbm.1, bf16[24,3072]{1,0:T(8,128)(2,1)} %active_hbm.1, bf16[256,3072]{1,0:T(8,128)(2,1)} %inactive_hbm.1), custom_call_target="tpu_custom_call" | custom-call | tf_op jit(solution)/shard_map/contract/pallas_call | solution.py:271
  4.6 0.0 copy-start
  4.6 0.0 copy-start.1
  4.6 3.6 %collective-permute-start.2 = (bf16[24,512]{1,0:T(8,128)(2,1)S(1)}, bf16[24,512]{1,0:T(8,128)(2,1)S(1)}, u32[]{:S(2)}, u32[]{:S(2)}) collective-permute-start(bf16[24,512]{1,0:T(8,128)(2,1)S(1)} %get-tuple-element.8.own_ref), channel_id=1, source_target_pairs={{0,3},{1,0},{2,1},{3,2},{4,7},{5,4},{6,5},{7,6},{8,11},{9,8},{10,9... | collective-permute-start | bytes 73736 | tf_op jit(solution)/shard_map/ppermute | solution.py:260
  8.3 0.3 collective-permute-start.1
  8.6 0.7 %collective-permute-start = (bf16[24,512]{1,0:T(8,128)(2,1)S(1)}, bf16[24,512]{1,0:T(8,128)(2,1)S(1)}, u32[]{:S(2)}, u32[]{:S(2)}) collective-permute-start(bf16[24,512]{1,0:T(8,128)(2,1)S(1)} %get-tuple-element.8.own_ref), channel_id=1, source_target_pairs={{0,1},{1,2},{2,3},{3,0},{4,5},{5,6},{6,7},{7,4},{8,9},{9,10},{10,1... | collective-permute-start | bytes 73736 | tf_op jit(solution)/shard_map/ppermute | solution.py:260
  9.3 0.0 collective-permute-done.2.three_ref
  9.3 3.2 %collective-permute-done.1.two_ref = bf16[24,512]{1,0:T(8,128)(2,1)S(1)} collective-permute-done((bf16[24,512]{1,0:T(8,128)(2,1)S(1)}, bf16[24,512]{1,0:T(8,128)(2,1)S(1)}, u32[]{:S(2)}, u32[]{:S(2)}) %collective-permute-start.1) | collective-permute-done | bytes 24608 | tf_op jit(solution)/shard_map/ppermute | solution.py:260
  12.5 0.2 collective-permute-done.one_ref
  12.7 1.4 %expand.1 = (f32[768,128]{1,0:T(8,128)S(1)}, f32[768,128]{1,0:T(8,128)S(1)}) custom-call(bf16[24,512]{1,0:T(8,128)(2,1)S(1)} %get-tuple-element.8.own_ref, bf16[24,512]{1,0:T(8,128)(2,1)S(1)} %collective-permute-done.one_ref, bf16[24,512]{1,0:T(8,128)(2,1)S(1)} %collective-permute-done.1.two_ref, bf16[24,512]{1,0:T(8,128)(2,1)S(1)} %collective-permute-done.2.three_ref, ...), custom_call_target="tpu_custom_call" | custom-call | tf_op jit(solution)/shard_map/expand/pallas_call | solution.py:296
  14.1 2.3 %collective-permute-start.3 = (f32[768,128]{1,0:T(8,128)S(1)}, f32[768,128]{1,0:T(8,128)S(1)}, u32[]{:S(2)}, u32[]{:S(2)}) collective-permute-start(f32[768,128]{1,0:T(8,128)S(1)} %get-tuple-element.11), channel_id=1, source_target_pairs={{0,4},{4,0},{1,5},{5,1},{2,6},{6,2},{3,7},{7,3},{8,12},{12,8},{9,1... | collective-permute-start | bytes 1179656 | tf_op jit(solution)/shard_map/ppermute | solution.py:313
  16.4 1.3 %collective-permute-done.3 = f32[768,128]{1,0:T(8,128)S(1)} collective-permute-done((f32[768,128]{1,0:T(8,128)S(1)}, f32[768,128]{1,0:T(8,128)S(1)}, u32[]{:S(2)}, u32[]{:S(2)}) %collective-permute-start.3) | collective-permute-done | bytes 393248 | tf_op jit(solution)/shard_map/ppermute | solution.py:313
  17.7 0.1 add_convert_fusion
  17.8 9.1 %all_to_all.15.parts_ref = bf16[4,192,128]{2,1,0:T(8,128)(2,1)S(1)} all-to-all(bf16[4,192,128]{2,1,0:T(8,128)(2,1)S(1)} %bitcast.2), channel_id=1, replica_groups=mesh['x'=4,'z'=8,'core'=2,'pair'=4] {'x'}, dimensions={0} | all-to-all | bytes 393216 | tf_op jit(solution)/shard_map/all_to_all | solution.py:314
  26.9 16.3 %all_to_all.16.parts_ref = bf16[8,80,128]{2,1,0:T(8,128)(2,1)S(1)} all-to-all(bf16[8,80,128]{2,1,0:T(8,128)(2,1)S(1)} %along_x.1), channel_id=1, replica_groups=mesh['x'=4,'z'=8,'core'=2,'pair'=4] {'z'}, dimensions={0} | all-to-all | bytes 327680 | tf_op jit(solution)/shard_map/all_to_all | solution.py:323
  43.2 0.0 copy-done
  43.2 0.0 copy-done.1
  43.2 0.7 %route.1 = bf16[16,64,128]{2,1,0:T(8,128)(2,1)S(1)} custom-call(s32[16]{0:T(128)S(1)} %copy-done, s32[16]{0:T(128)S(1)} %copy-done.1, bf16[8,80,128]{2,1,0:T(8,128)(2,1)S(1)} %all_to_all.16.parts_ref), custom_call_target="tpu_custom_call" | custom-call | tf_op jit(solution)/shard_map/route/pallas_call | solution.py:324
  43.9 10.8 %all_to_all.17.own_ref = bf16[16,64,128]{2,1,0:T(8,128)(2,1)S(1)} all-to-all(bf16[16,64,128]{2,1,0:T(8,128)(2,1)S(1)} %route.1), channel_id=1, replica_groups=mesh['x'=4,'z'=8,'core'=2,'pair'=4] {'pair','x'}, dimensions={0} | all-to-all | bytes 524288 | tf_op jit(solution)/shard_map/all_to_all | solution.py:333
  54.7 4.5 %collective-permute-start.4 = (bf16[16,64,128]{2,1,0:T(8,128)(2,1)S(1)}, bf16[16,64,128]{2,1,0:T(8,128)(2,1)S(1)}, u32[]{:S(2)}, u32[]{:S(2)}) collective-permute-start(bf16[16,64,128]{2,1,0:T(8,128)(2,1)S(1)} %all_to_all.17.own_ref), channel_id=1, source_target_pairs={{0,4},{4,0},{1,5},{5,1},{2,6},{6,2},{3,7},{7,3},{8,12},{12,8},{9,1... | collective-permute-start | bytes 786440 | tf_op jit(solution)/shard_map/ppermute | solution.py:334
  59.2 1.2 %collective-permute-done.4.other_ref = bf16[16,64,128]{2,1,0:T(8,128)(2,1)S(1)} collective-permute-done((bf16[16,64,128]{2,1,0:T(8,128)(2,1)S(1)}, bf16[16,64,128]{2,1,0:T(8,128)(2,1)S(1)}, u32[]{:S(2)}, u32[]{:S(2)}) %collective-permute-start.4) | collective-permute-done | bytes 262176 | tf_op jit(solution)/shard_map/ppermute | solution.py:334
  60.4 1.5 %place.1 = (f32[1024,128]{1,0:T(8,128)}, f32[9,576]{1,0:T(8,128)}) custom-call(s32[16]{0:T(128)S(1)} %copy-done, s32[16]{0:T(128)S(1)} %copy-done.1, bf16[16,64,128]{2,1,0:T(8,128)(2,1)S(1)} %all_to_all.17.own_ref, bf16[16,64,128]{2,1,0:T(8,128)(2,1)S(1)} %collective-permute-done.4.other_ref), custom_call_target="tpu_custom_call" | custom-call | tf_op jit(solution)/shard_map/place/pallas_call | solution.py:335
  (1 shorter events, 0.0 us)
Async XLA Ops:
  4.6 38.6 %copy-start = (s32[16]{0:T(128)S(1)}, s32[16]{0:T(128)}, u32[]{:S(2)}) copy-start(s32[16]{0:T(128)} %mask_ref.3) | copy-start | bytes 196
  4.6 38.5 %copy-start.1 = (s32[16]{0:T(128)S(1)}, s32[16]{0:T(128)}, u32[]{:S(2)}) copy-start(s32[16]{0:T(128)} %owner_ref.3) | copy-start | bytes 196
  4.6 4.7 %collective-permute-start.2 = (bf16[24,512]{1,0:T(8,128)(2,1)S(1)}, bf16[24,512]{1,0:T(8,128)(2,1)S(1)}, u32[]{:S(2)}, u32[]{:S(2)}) collective-permute-start(bf16[24,512]{1,0:T(8,128)(2,1)S(1)} %get-tuple-element.8.own_ref), channel_id=1, source_target_pairs={{0,3},{1,0},{2,1},{3,2},{4,7},{5,4},{6,5},{7,6},{8,11},{9,8},{10,9... | collective-permute-start | bytes 73736 | tf_op jit(solution)/shard_map/ppermute | solution.py:260
  8.3 4.2 %collective-permute-start.1 = (bf16[24,512]{1,0:T(8,128)(2,1)S(1)}, bf16[24,512]{1,0:T(8,128)(2,1)S(1)}, u32[]{:S(2)}, u32[]{:S(2)}) collective-permute-start(bf16[24,512]{1,0:T(8,128)(2,1)S(1)} %get-tuple-element.8.own_ref), channel_id=1, source_target_pairs={{0,2},{1,3},{2,0},{3,1},{4,6},{5,7},{6,4},{7,5},{8,10},{9,11},{10,... | collective-permute-start | bytes 73736 | tf_op jit(solution)/shard_map/ppermute | solution.py:260
  8.6 4.1 %collective-permute-start = (bf16[24,512]{1,0:T(8,128)(2,1)S(1)}, bf16[24,512]{1,0:T(8,128)(2,1)S(1)}, u32[]{:S(2)}, u32[]{:S(2)}) collective-permute-start(bf16[24,512]{1,0:T(8,128)(2,1)S(1)} %get-tuple-element.8.own_ref), channel_id=1, source_target_pairs={{0,1},{1,2},{2,3},{3,0},{4,5},{5,6},{6,7},{7,4},{8,9},{9,10},{10,1... | collective-permute-start | bytes 73736 | tf_op jit(solution)/shard_map/ppermute | solution.py:260
  14.1 3.6 %collective-permute-start.3 = (f32[768,128]{1,0:T(8,128)S(1)}, f32[768,128]{1,0:T(8,128)S(1)}, u32[]{:S(2)}, u32[]{:S(2)}) collective-permute-start(f32[768,128]{1,0:T(8,128)S(1)} %get-tuple-element.11), channel_id=1, source_target_pairs={{0,4},{4,0},{1,5},{5,1},{2,6},{6,2},{3,7},{7,3},{8,12},{12,8},{9,1... | collective-permute-start | bytes 1179656 | tf_op jit(solution)/shard_map/ppermute | solution.py:313
  54.7 5.7 %collective-permute-start.4 = (bf16[16,64,128]{2,1,0:T(8,128)(2,1)S(1)}, bf16[16,64,128]{2,1,0:T(8,128)(2,1)S(1)}, u32[]{:S(2)}, u32[]{:S(2)}) collective-permute-start(bf16[16,64,128]{2,1,0:T(8,128)(2,1)S(1)} %all_to_all.17.own_ref), channel_id=1, source_target_pairs={{0,4},{4,0},{1,5},{5,1},{2,6},{6,2},{3,7},{7,3},{8,12},{12,8},{9,1... | collective-permute-start | bytes 786440 | tf_op jit(solution)/shard_map/ppermute | solution.py:334
where the time goes:
time: 62.1 us; the launch traced here: 61.9 us
  blocking collectives  36.2 us (58%)
  starting transfers between devices  11.4 us (18%)
  Pallas kernels  7.65 us (12%)
  waiting for transfers between devices  5.91 us (10%)
  between operations  0.68 us (1%)
    all_to_all x1, blocking collectives, shards(): along_z = lax.all_to_all(pieces, 'z', 0, 0, tiled=True)  16.3 us
    all_to_all x1, blocking collectives, shards(): received = lax.all_to_all(pieces, ('pair', 'x'), 0, 0, tiled=True)  10.8 us
    all_to_all x1, blocking collectives, shards(): lax.all_to_all(chip_sum.reshape(NX, NZ * MSG, BW), 'x', 0, 0, tiled=True)  9.1 us
    ppermute x3, starting transfers between devices, from_others(): lax.ppermute(x, 'pair', [(i, (i + s) % OWNERS) for i in range(OWNERS)])  4.67 us
    ppermute x1, starting transfers between devices, shards(): partner = lax.ppermute(received, 'core', swap)  4.5 us
    pallas_call x1, Pallas kernels, shards(): pl.pallas_call(contract_kernel, out_shape=[pltpu.VMEM((ACT, GROUPS * BW),...  3.98 us
    ppermute x3, waiting for transfers between devices, from_others(): lax.ppermute(x, 'pair', [(i, (i + s) % OWNERS) for i in range(OWNERS)])  3.4 us
    ppermute x1, starting transfers between devices, shards(): chip_sum = (keep + lax.ppermute(send, 'core', swap)).astype(BF16)  2.26 us
  transfers between devices with their start and end apart: 5, of which 4 were waited for; matrix products, arithmetic and copies ran while one was open for 0% of the time, Pallas kernels for 0%

commit v1 on v0

v1 whole, which is shorter than its diff:
```python
import math

import jax
import jax.numpy as jnp
from jax import lax
from jax.experimental import pallas as pl
from jax.experimental.pallas import tpu as pltpu
from jax.sharding import Mesh, PartitionSpec as P

SLOTS = 4
ROWS = 20
BW = 128
ACT = 24
PAIRS = 576
GROUPS = 4
PER = 5
USED = PER * ACT
NX = 4
NZ = 8
CHIPS = NX * NZ
CORES = 2
OWNERS = 4
AUX = 1280
NIN = 256
NAO = 3072
MSG = 24
F32 = jnp.float32
BF16 = jnp.bfloat16

HBM = pl.BlockSpec(memory_space=pltpu.HBM)
VMEM = pl.BlockSpec(memory_space=pltpu.VMEM)


def limit(kib):
    return pltpu.CompilerParams(vmem_limit_bytes=kib << 10)


def nt(a, b):
    return lax.dot_general(a, b, (((1,), (1,)), ((), ())), preferred_element_type=F32)


def lanes(shape):
    return lax.broadcasted_iota(jnp.int32, shape, len(shape) - 1)


def sublanes(shape):
    return lax.broadcasted_iota(jnp.int32, shape, len(shape) - 2)


def contract_kernel(
    mask_hbm, owner_hbm, index_hbm, blocks_hbm, active_hbm, inactive_hbm,
    out_ref, blocks, route_ref, place_ref,
    mask_ref, owner_ref, index_ref, active, inactive, wide, halves, density, sums,
    int_sem, ina_sem, act_sem, block_sem,
):
    here = lax.axis_index("pair")
    ints = [
        pltpu.make_async_copy(index_hbm, index_ref, int_sem.at[0]),
        pltpu.make_async_copy(mask_hbm, mask_ref, int_sem.at[1]),
        pltpu.make_async_copy(owner_hbm, owner_ref, int_sem.at[2]),
    ]
    part = NIN // SLOTS
    inactives = [
        pltpu.make_async_copy(
            inactive_hbm.at[pl.ds(n * part, part)], inactive.at[pl.ds(n * part, part)], ina_sem.at[n]
        )
        for n in range(SLOTS)
    ]
    actives = [pltpu.make_async_copy(active_hbm, active, act_sem.at[0])]
    whole = [
        pltpu.make_async_copy(blocks_hbm.at[g], blocks.at[g], block_sem.at[g]) for g in range(SLOTS)
    ]
    for c in ints + inactives + actives + whole:
        c.start()
    wide[...] = jnp.zeros_like(wide)
    for c in ints:
        c.wait()
    lives = [mask_ref[here * SLOTS + g] for g in range(SLOTS)]
    owners = [owner_ref[here * SLOTS + g] for g in range(SLOTS)]
    rows = [pl.multiple_of(index_ref[0, here * SLOTS + g] * BW, BW) for g in range(SLOTS)]
    cols = [pl.multiple_of(index_ref[1, here * SLOTS + g] * BW, BW) for g in range(SLOTS)]
    col = lanes((1, BW))
    at = sublanes((BW, BW))
    target = jnp.full((1, BW), -BW, jnp.int32)
    for g in range(SLOTS):
        place = jnp.int32(0)
        for h in range(g):
            place = place + jnp.where((lives[h] == 1) & (owners[h] == owners[g]), 1, 0)
        first = jnp.where(lives[g] == 1, 16 * (2 * owners[g] + place), -BW)
        inside = (col >= 16 * g) & (col < 16 * (g + 1))
        target = jnp.where(inside, first + col - 16 * g, target)
    route_ref[...] = (at == target).astype(F32).astype(BF16)
    target = jnp.full((1, BW), -BW, jnp.int32)
    rank = jnp.int32(0)
    for q in range(OWNERS):
        place = jnp.int32(0)
        firsts = [jnp.int32(-BW)] * 2
        for g in range(SLOTS):
            slot = q * SLOTS + g
            chosen = (mask_ref[slot] == 1) & (owner_ref[slot] == here)
            firsts = [jnp.where(chosen & (place == k), 16 * rank, f) for k, f in enumerate(firsts)]
            place = place + jnp.where(chosen, 1, 0)
            rank = rank + jnp.where(chosen, 1, 0)
        for k in range(2):
            begin = 16 * (2 * q + k)
            inside = (col >= begin) & (col < begin + 16)
            target = jnp.where(inside, firsts[k] + col - begin, target)
    place_ref[...] = (at == target).astype(F32).astype(BF16)
    for c in inactives:
        c.wait()
    for g in range(SLOTS):
        square = lax.dot_general(
            inactive[:, pl.ds(rows[g], BW)],
            inactive[:, pl.ds(cols[g], BW)],
            (((0,), (0,)), ((), ())),
            preferred_element_type=F32,
        )
        density[g] = square.astype(BF16).astype(F32) * lives[g].astype(F32)
    actives[0].wait()
    for g in range(SLOTS):
        column = active[:, pl.ds(cols[g], BW)].astype(F32)
        for p in range(PER):
            wide[pl.ds(ACT * p, ACT), pl.ds(BW * p, BW)] = column
        weights = wide[...].astype(BF16)
        whole[g].wait()
        for k in range(GROUPS):
            joined = jnp.concatenate([blocks[g, k * PER + p] for p in range(PER)], axis=1)
            half = nt(joined, weights)
            halves[pl.ds(g * BW, BW), pl.ds(k * BW, BW)] = half.astype(BF16)
        square = density[g]
        for p in range(ROWS):
            product = blocks[g, p].astype(F32) * square
            part_sum = jnp.sum(product.reshape(BW // 8, 8, BW), axis=0)
            if g == 0:
                sums[p] = part_sum
            else:
                sums[p] = sums[p] + part_sum
    left_side = jnp.concatenate(
        [active[:, pl.ds(rows[g], BW)].astype(F32) * lives[g].astype(F32) for g in range(SLOTS)],
        axis=1,
    ).astype(BF16)
    fitted = jnp.dot(left_side, halves[...], preferred_element_type=F32)
    coupling = jnp.sum(jnp.sum(sums[...], axis=1), axis=1, keepdims=True) * (1.0 / BW)
    coupling = jnp.concatenate([coupling, jnp.zeros((ACT - ROWS, 1), F32)], axis=0)
    high = coupling.astype(BF16).astype(F32)
    low = coupling - high
    spare = lanes((ACT, BW)) >= USED
    for k in range(GROUPS):
        tail = high if k == 0 else low if k == 1 else jnp.zeros_like(high)
        tile = jnp.where(spare, jnp.broadcast_to(tail, (ACT, BW)), fitted[:, k * BW : (k + 1) * BW])
        out_ref[:, pl.ds(k * BW, BW)] = tile.astype(BF16)


def expand_kernel(
    own_ref, one_ref, two_ref, three_ref, blocks, keep_ref, send_ref,
    coupling_ref, spread, left, coulomb, main, rest,
):
    here = lax.axis_index("pair")
    core = lax.axis_index("core")
    along = lax.axis_index("x")
    total = (own_ref[...].astype(F32) + two_ref[...].astype(F32)) + (
        one_ref[...].astype(F32) + three_ref[...].astype(F32)
    )
    both = total[:, :BW] + total[:, BW : 2 * BW]
    coupling = jnp.sum(jnp.where(lanes((ACT, BW)) == USED, both, 0.0), axis=1, keepdims=True)
    coupling_ref[...] = jnp.broadcast_to(coupling.astype(BF16).astype(F32), (ACT, BW))
    fitted = total.astype(BF16).astype(F32)
    offset = lanes((ACT, BW)) - sublanes((ACT, BW))
    keep = offset == 0
    for p in range(1, PER):
        keep = keep | (offset == ACT * p)
    keep = jnp.concatenate([keep.astype(F32)] * GROUPS, axis=1)
    for t in range(0, ACT, 2):
        pair = jnp.concatenate(
            [jnp.broadcast_to(fitted[t + d : t + d + 1, :], keep.shape) * keep for d in range(2)],
            axis=0,
        )
        spread[pl.ds(t * ACT, 2 * ACT), :] = pair.astype(BF16)
    shape = (GROUPS * BW, BW)
    lane = lanes(shape)
    group = (
        (lane >= PER).astype(jnp.int32)
        + (lane >= 2 * PER).astype(jnp.int32)
        + (lane >= 3 * PER).astype(jnp.int32)
    )
    start = group * BW + (lane - group * PER) * ACT
    position = sublanes(shape) - start
    pick = (position >= 0) & (position < ACT) & (lane < ROWS)
    folded = jnp.dot(
        spread[...], pick.astype(F32).astype(BF16), preferred_element_type=F32
    ).astype(BF16)
    left[...] = folded
    columns = left[pl.ds(pl.multiple_of(here * BW, BW), BW), :]
    tail = left[pl.ds(4 * BW, PAIRS - 4 * BW), :]
    main[...] = nt(folded, columns)
    rest[...] = nt(folded, jnp.concatenate([tail, tail], axis=0))
    for g in range(SLOTS):
        total_g = jnp.zeros((BW, BW), F32)
        for p in range(ROWS):
            factor = jnp.broadcast_to(coupling_ref[pl.ds(p, 1), :], (BW, BW))
            total_g = total_g + blocks[g, p].astype(F32) * factor
        coulomb[pl.ds(g * BW, BW), :] = total_g
    low_lane = lanes((NZ, BW)) < BW // 2
    for ref, which in ((keep_ref, core), (send_ref, 1 - core)):
        for step in range(NX):
            x = lax.rem(along + step, NX)
            base = step * NZ * MSG
            for z in range(NZ):
                row = pl.multiple_of(z // 2 * BW + 32 * x + 16 * which + 8 * (z % 2), 8)
                ref[pl.ds(base + z * MSG, 8), :] = coulomb[pl.ds(row, 8), :]
            first = 144 * x + 9 * which
            for s in range(9):
                ref[pl.ds(base + 8 + s, NZ, stride=MSG), :] = main[pl.ds(first + s, NZ, stride=18), :]
            for s in range(7):
                value = rest[pl.ds(first + s, NZ, stride=18), :]
                if s < 2:
                    other = rest[pl.ds(first + 7 + s, NZ, stride=18), :]
                    value = jnp.where(low_lane, value, other)
                ref[pl.ds(base + 17 + s, NZ, stride=MSG), :] = value


def along_x_kernel(own_ref, one_ref, two_ref, three_ref, out_ref):
    total = own_ref[...]
    for ref in (one_ref, two_ref, three_ref):
        total = total + ref[...].astype(F32)
    pieces = [total[z * MSG : (z + 1) * MSG] for z in range(NZ)]
    fock = jnp.concatenate([p[0:8] for p in pieces], axis=0).astype(BF16)
    for z in range(NZ):
        out_ref[z, 0:64, :] = fock
        out_ref[z, 64:80, :] = pieces[z][8:MSG].astype(BF16)


def route_kernel(route_ref, parts_ref, out_ref):
    total = jnp.sum(parts_ref[...].astype(F32), axis=0)
    gram = (total[64:80] * (1.0 / AUX)).astype(BF16)
    scaled = total[0:64] * (1.0 / math.sqrt(AUX))
    scaled = jnp.concatenate([scaled, jnp.zeros_like(scaled)], axis=0).astype(BF16)
    chosen = jnp.dot(route_ref[...], scaled, preferred_element_type=F32).astype(BF16)
    for o in range(OWNERS):
        for x in range(NX):
            out_ref[o * NX + x, 0:32, :] = chosen[32 * o : 32 * (o + 1)]
            out_ref[o * NX + x, 32:48, :] = gram


def place_kernel(place_ref, own_ref, other_ref, fock_ref, gram_ref):
    core = lax.axis_index("core")
    along = lax.axis_index("x")
    table = place_ref[...]
    for n, ref in enumerate((own_ref, other_ref)):
        which = core if n == 0 else 1 - core
        for x in range(NX):
            pieces = jnp.concatenate([ref[q * NX + x, 0:32, :] for q in range(OWNERS)], axis=0)
            placed = jnp.dot(table, pieces, preferred_element_type=F32)
            for rank in range(8):
                row = pl.multiple_of(rank * BW + 32 * x + 16 * which, 16)
                fock_ref[pl.ds(row, 16), :] = placed[16 * rank : 16 * (rank + 1)]
    for q in range(OWNERS):
        gram = own_ref[q * NX + along, 32:48, :].astype(F32)
        gram_ref[:, q * BW : (q + 1) * BW] = gram[0:9]
        if q == 0:
            gram_ref[0:7, 4 * BW : PAIRS] = gram[9:16, 0 : BW // 2]
            gram_ref[7:9, 4 * BW : PAIRS] = gram[9:11, BW // 2 : BW]


def from_others(x, axis="pair"):
    return [
        lax.ppermute(x if axis == "pair" else x[s], axis, [(i, (i + s) % 4) for i in range(4)])
        for s in range(1, 4)
    ]


def shards(three_centre, block_mask, block_owner, block_index, active_orbitals, inactive_orbitals):
    dma = pltpu.SemaphoreType.DMA
    inputs = (
        block_mask, block_owner, block_index, three_centre, active_orbitals, inactive_orbitals
    )
    pinned = [pltpu.with_memory_space_constraint(a, pltpu.HBM) for a in inputs]
    message, blocks, routes, places = pl.pallas_call(
        contract_kernel,
        out_shape=[
            pltpu.VMEM((ACT, GROUPS * BW), BF16),
            pltpu.VMEM((SLOTS, ROWS, BW, BW), BF16),
            pltpu.VMEM((BW, BW), BF16),
            pltpu.VMEM((BW, BW), BF16),
        ],
        in_specs=[HBM] * 6,
        out_specs=[VMEM] * 4,
        scratch_shapes=[
            pltpu.SMEM((16,), jnp.int32),
            pltpu.SMEM((16,), jnp.int32),
            pltpu.SMEM((2, 16), jnp.int32),
            pltpu.VMEM((ACT, NAO), BF16),
            pltpu.VMEM((NIN, NAO), BF16),
            pltpu.VMEM((BW, PER * BW), F32),
            pltpu.VMEM((SLOTS * BW, GROUPS * BW), BF16),
            pltpu.VMEM((SLOTS, BW, BW), F32),
            pltpu.VMEM((ROWS, 8, BW), F32),
            dma((3,)), dma((SLOTS,)), dma((1,)), dma((SLOTS,)),
        ],
        compiler_params=limit(8192),
        name="contract",
    )(*pinned)
    one, two, three = from_others(message)
    rows = CHIPS * MSG
    keep, send = pl.pallas_call(
        expand_kernel,
        out_shape=[pltpu.VMEM((rows, BW), F32)] * 2,
        in_specs=[VMEM] * 5,
        out_specs=[VMEM, VMEM],
        scratch_shapes=[
            pltpu.VMEM((ACT, BW), F32),
            pltpu.VMEM((PAIRS, GROUPS * BW), BF16),
            pltpu.VMEM((PAIRS, BW), BF16),
            pltpu.VMEM((SLOTS * BW, BW), F32),
            pltpu.VMEM((PAIRS, BW), F32),
            pltpu.VMEM((PAIRS, BW), F32),
        ],
        compiler_params=limit(8192),
        name="expand",
    )(message, one, two, three, blocks)
    swap = [(0, 1), (1, 0)]
    chip_sum = (keep + lax.ppermute(send, "core", swap)).reshape(NX, NZ * MSG, BW)
    one, two, three = from_others(chip_sum.astype(BF16), "x")
    pieces = pl.pallas_call(
        along_x_kernel,
        out_shape=pltpu.VMEM((NZ, 80, BW), BF16),
        in_specs=[VMEM] * 4,
        out_specs=VMEM,
        compiler_params=limit(4096),
        name="along_x",
    )(chip_sum[0], one, two, three)
    along_z = lax.all_to_all(pieces, "z", 0, 0, tiled=True)
    pieces = pl.pallas_call(
        route_kernel,
        out_shape=pltpu.VMEM((OWNERS * NX, 48, BW), BF16),
        in_specs=[VMEM] * 2,
        out_specs=VMEM,
        compiler_params=limit(4096),
        name="route",
    )(routes, along_z)
    received = lax.all_to_all(pieces, ("pair", "x"), 0, 0, tiled=True)
    partner = lax.ppermute(received, "core", swap)
    fock, integrals = pl.pallas_call(
        place_kernel,
        out_shape=[
            jax.ShapeDtypeStruct((8 * BW, BW), F32),
            jax.ShapeDtypeStruct((9, PAIRS), F32),
        ],
        in_specs=[VMEM] * 3,
        out_specs=[VMEM, VMEM],
        compiler_params=limit(4096),
        name="place",
    )(places, received, partner)
    return (fock.reshape(8, BW, BW), integrals)


def solution(mesh):
    split = Mesh(mesh.devices.reshape(NX, NZ, CORES, OWNERS), ("x", "z", "core", "pair"))
    aux = ("x", "z", "core")
    return jax.shard_map(
        shards,
        mesh=split,
        in_specs=(P("pair", aux, None, None), P(), P(), P(), P(), P()),
        out_specs=(P("pair", None, None), P(aux, None)),
        check_vma=False,
    )
```

time: 62.1 us -> 59.3 us (0.955)
  blocking collectives: 36.2 us -> 27.3 us
  waiting for transfers between devices: 5.91 us -> 9.66 us
  starting transfers between devices: 11.4 us -> 15 us
  Pallas kernels: 7.65 us -> 6.49 us
    all_to_all x1 -> x0, blocking collectives: 9.1 us -> none  [shards(): lax.all_to_all(chip_sum.reshape(NX, NZ * MSG, BW), 'x', 0, 0, tiled=True)]
    ppermute x4 -> x7, waiting for transfers between devices: 4.75 us -> 8.59 us  [the longest x6 7.24 us: from_others(): lax.ppermute(x if axis == 'pair' else x[s], axis, [(i, (i + s) % 4) for i...]
    ppermute x4 -> x7, starting transfers between devices: 6.93 us -> 10.6 us  [the longest x6 8.35 us: from_others(): lax.ppermute(x if axis == 'pair' else x[s], axis, [(i, (i + s) % 4) for i...]
  transfers between devices with their start and end apart: 5 -> 8, of which waited for: 4 -> 6; matrix products, arithmetic and copies ran while one was open for 0% -> 0% of each run, Pallas kernels for 0% -> 0%
where the time goes in v1:
time: 59.3 us; the launch traced here: 59.2 us
  blocking collectives  27.3 us (46%)
  starting transfers between devices  15 us (25%)
  waiting for transfers between devices  9.66 us (16%)
  Pallas kernels  6.49 us (11%)
  between operations  0.68 us (1%)
    all_to_all x1, blocking collectives, shards(): along_z = lax.all_to_all(pieces, 'z', 0, 0, tiled=True)  16.4 us
    all_to_all x1, blocking collectives, shards(): received = lax.all_to_all(pieces, ('pair', 'x'), 0, 0, tiled=True)  10.9 us
    ppermute x6, starting transfers between devices, from_others(): lax.ppermute(x if axis == 'pair' else x[s], axis, [(i, (i + s) % 4) for i...  8.35 us
    ppermute x6, waiting for transfers between devices, from_others(): lax.ppermute(x if axis == 'pair' else x[s], axis, [(i, (i + s) % 4) for i...  7.24 us
    ppermute x1, starting transfers between devices, shards(): partner = lax.ppermute(received, 'core', swap)  4.38 us
    pallas_call x1, Pallas kernels, shards(): pl.pallas_call(contract_kernel, out_shape=[pltpu.VMEM((ACT, GROUPS * BW),...  3.93 us
    ppermute x1, starting transfers between devices, shards(): lax.ppermute(send, 'core', swap)  2.26 us
    pallas_call x1, Pallas kernels, shards(): pl.pallas_call(expand_kernel, out_shape=[pltpu.VMEM((rows, BW), F32)] * 2...  1.38 us
  transfers between devices with their start and end apart: 8, of which 6 were waited for; matrix products, arithmetic and copies ran while one was open for 0% of the time, Pallas kernels for 0%

profile of v1, /device:TPU:1, one launch (start us, length us, event | category | flops | bytes accessed | tf_op | source)
XLA Modules:
  0.0 59.2 jit_solution(2992890508819242430)
XLA Ops:
  0.6 3.9 %contract.1 = (bf16[24,512]{1,0:T(8,128)(2,1)S(1)}, bf16[4,20,128,128]{3,2,1,0:T(8,128)(2,1)S(1)}, bf16[128,128]{1,0:T(8,128)(2,1)S(1)}, bf16[128,128]{1,0:T(8,128)(2,1)S(1)}) custom-call(s32[16]{0:T(128)} %mask_hbm.1, s32[16]{0:T(128)} %owner_hbm.1, s32[2,16]{1,0:T(2,128)} %index_hbm.1, bf16[4,20,128,128]{3,2,1,0:T(8,128)(2,1)} %blocks_hbm.1, ...), custom_call_target="tpu_custom_call" | custom-call | tf_op jit(solution)/shard_map/contract/pallas_call | solution.py:278
  4.6 3.6 %collective-permute-start.2 = (bf16[24,512]{1,0:T(8,128)(2,1)S(1)}, bf16[24,512]{1,0:T(8,128)(2,1)S(1)}, u32[]{:S(2)}, u32[]{:S(2)}) collective-permute-start(bf16[24,512]{1,0:T(8,128)(2,1)S(1)} %get-tuple-element.12.own_ref), channel_id=1, source_target_pairs={{0,3},{1,0},{2,1},{3,2},{4,7},{5,4},{6,5},{7,6},{8,11},{9,8},{10,9... | collective-permute-start | bytes 73736 | tf_op jit(solution)/shard_map/ppermute | solution.py:267
  8.2 0.3 collective-permute-start.1
  8.5 0.7 %collective-permute-start = (bf16[24,512]{1,0:T(8,128)(2,1)S(1)}, bf16[24,512]{1,0:T(8,128)(2,1)S(1)}, u32[]{:S(2)}, u32[]{:S(2)}) collective-permute-start(bf16[24,512]{1,0:T(8,128)(2,1)S(1)} %get-tuple-element.12.own_ref), channel_id=1, source_target_pairs={{0,1},{1,2},{2,3},{3,0},{4,5},{5,6},{6,7},{7,4},{8,9},{9,10},{10,1... | collective-permute-start | bytes 73736 | tf_op jit(solution)/shard_map/ppermute | solution.py:267
  9.2 0.0 collective-permute-done.2.three_ref
  9.2 3.2 %collective-permute-done.1.two_ref = bf16[24,512]{1,0:T(8,128)(2,1)S(1)} collective-permute-done((bf16[24,512]{1,0:T(8,128)(2,1)S(1)}, bf16[24,512]{1,0:T(8,128)(2,1)S(1)}, u32[]{:S(2)}, u32[]{:S(2)}) %collective-permute-start.1) | collective-permute-done | bytes 24608 | tf_op jit(solution)/shard_map/ppermute | solution.py:267
  12.4 0.2 collective-permute-done.one_ref
  12.6 1.4 %expand.1 = (f32[768,128]{1,0:T(8,128)S(1)}, f32[768,128]{1,0:T(8,128)S(1)}) custom-call(bf16[24,512]{1,0:T(8,128)(2,1)S(1)} %get-tuple-element.12.own_ref, bf16[24,512]{1,0:T(8,128)(2,1)S(1)} %collective-permute-done.one_ref, bf16[24,512]{1,0:T(8,128)(2,1)S(1)} %collective-permute-done.1.two_ref, bf16[24,512]{1,0:T(8,128)(2,1)S(1)} %collective-permute-done.2.three_ref, ...), custom_call_target="tpu_custom_call" | custom-call | tf_op jit(solution)/shard_map/expand/pallas_call | solution.py:305
  14.0 2.3 %collective-permute-start.3 = (f32[768,128]{1,0:T(8,128)S(1)}, f32[768,128]{1,0:T(8,128)S(1)}, u32[]{:S(2)}, u32[]{:S(2)}) collective-permute-start(f32[768,128]{1,0:T(8,128)S(1)} %get-tuple-element.15), channel_id=1, source_target_pairs={{0,4},{4,0},{1,5},{5,1},{2,6},{6,2},{3,7},{7,3},{8,12},{12,8},{9,1... | collective-permute-start | bytes 1179656 | tf_op jit(solution)/shard_map/ppermute | solution.py:322
  16.3 1.3 %collective-permute-done.3 = f32[768,128]{1,0:T(8,128)S(1)} collective-permute-done((f32[768,128]{1,0:T(8,128)S(1)}, f32[768,128]{1,0:T(8,128)S(1)}, u32[]{:S(2)}, u32[]{:S(2)}) %collective-permute-start.3) | collective-permute-done | bytes 393248 | tf_op jit(solution)/shard_map/ppermute | solution.py:322
  17.6 0.1 fusion
  17.7 2.6 %collective-permute-start.6 = (bf16[192,128]{1,0:T(8,128)(2,1)S(1)}, bf16[192,128]{1,0:T(8,128)(2,1)S(1)}, u32[]{:S(2)}, u32[]{:S(2)}) collective-permute-start(bf16[192,128]{1,0:T(8,128)(2,1)S(1)} %get-tuple-element.20), channel_id=1, source_target_pairs={{0,192},{64,0},{128,64},{192,128},{1,193},{65,1},{129,65},{193,129... | collective-permute-start | bytes 147464 | tf_op jit(solution)/shard_map/ppermute | solution.py:267
  20.3 0.5 collective-permute-start.5
  20.8 0.6 %collective-permute-start.4 = (bf16[192,128]{1,0:T(8,128)(2,1)S(1)}, bf16[192,128]{1,0:T(8,128)(2,1)S(1)}, u32[]{:S(2)}, u32[]{:S(2)}) collective-permute-start(bf16[192,128]{1,0:T(8,128)(2,1)S(1)} %get-tuple-element.22), channel_id=1, source_target_pairs={{0,64},{64,128},{128,192},{192,0},{1,65},{65,129},{129,193},{193,1... | collective-permute-start | bytes 147464 | tf_op jit(solution)/shard_map/ppermute | solution.py:267
  21.4 0.0 collective-permute-done.6.three_ref
  21.5 3.3 %collective-permute-done.5.two_ref = bf16[192,128]{1,0:T(8,128)(2,1)S(1)} collective-permute-done((bf16[192,128]{1,0:T(8,128)(2,1)S(1)}, bf16[192,128]{1,0:T(8,128)(2,1)S(1)}, u32[]{:S(2)}, u32[]{:S(2)}) %collective-permute-start.5) | collective-permute-done | bytes 49184 | tf_op jit(solution)/shard_map/ppermute | solution.py:267
  24.8 0.5 collective-permute-done.4.one_ref
  25.3 16.4 %all_to_all.10.parts_ref = bf16[8,80,128]{2,1,0:T(8,128)(2,1)S(1)} all-to-all(bf16[8,80,128]{2,1,0:T(8,128)(2,1)S(1)} %along_x.1), channel_id=1, replica_groups=mesh['x'=4,'z'=8,'core'=2,'pair'=4] {'z'}, dimensions={0} | all-to-all | bytes 327680 | tf_op jit(solution)/shard_map/all_to_all | solution.py:332
  41.6 0.1 route.1
  41.8 10.9 %all_to_all.11.own_ref = bf16[16,48,128]{2,1,0:T(8,128)(2,1)S(1)} all-to-all(bf16[16,48,128]{2,1,0:T(8,128)(2,1)S(1)} %route.1), channel_id=1, replica_groups=mesh['x'=4,'z'=8,'core'=2,'pair'=4] {'pair','x'}, dimensions={0} | all-to-all | bytes 393216 | tf_op jit(solution)/shard_map/all_to_all | solution.py:341
  52.7 4.4 %collective-permute-start.7 = (bf16[16,48,128]{2,1,0:T(8,128)(2,1)S(1)}, bf16[16,48,128]{2,1,0:T(8,128)(2,1)S(1)}, u32[]{:S(2)}, u32[]{:S(2)}) collective-permute-start(bf16[16,48,128]{2,1,0:T(8,128)(2,1)S(1)} %all_to_all.11.own_ref), channel_id=1, source_target_pairs={{0,4},{4,0},{1,5},{5,1},{2,6},{6,2},{3,7},{7,3},{8,12},{12,8},{9,1... | collective-permute-start | bytes 589832 | tf_op jit(solution)/shard_map/ppermute | solution.py:342
  57.1 1.1 %collective-permute-done.7.other_ref = bf16[16,48,128]{2,1,0:T(8,128)(2,1)S(1)} collective-permute-done((bf16[16,48,128]{2,1,0:T(8,128)(2,1)S(1)}, bf16[16,48,128]{2,1,0:T(8,128)(2,1)S(1)}, u32[]{:S(2)}, u32[]{:S(2)}) %collective-permute-start.7) | collective-permute-done | bytes 196640 | tf_op jit(solution)/shard_map/ppermute | solution.py:342
  58.2 1.0 %place.1 = (f32[1024,128]{1,0:T(8,128)}, f32[9,576]{1,0:T(8,128)}) custom-call(bf16[128,128]{1,0:T(8,128)(2,1)S(1)} %get-tuple-element.10.place_ref, bf16[16,48,128]{2,1,0:T(8,128)(2,1)S(1)} %all_to_all.11.own_ref, bf16[16,48,128]{2,1,0:T(8,128)(2,1)S(1)} %collective-permute-done.7.other_ref), custom_call_target="tpu_custom_call" | custom-call | tf_op jit(solution)/shard_map/place/pallas_call | solution.py:343
  (3 shorter events, 0.0 us)
Async XLA Ops:
  4.6 4.7 %collective-permute-start.2 = (bf16[24,512]{1,0:T(8,128)(2,1)S(1)}, bf16[24,512]{1,0:T(8,128)(2,1)S(1)}, u32[]{:S(2)}, u32[]{:S(2)}) collective-permute-start(bf16[24,512]{1,0:T(8,128)(2,1)S(1)} %get-tuple-element.12.own_ref), channel_id=1, source_target_pairs={{0,3},{1,0},{2,1},{3,2},{4,7},{5,4},{6,5},{7,6},{8,11},{9,8},{10,9... | collective-permute-start | bytes 73736 | tf_op jit(solution)/shard_map/ppermute | solution.py:267
  8.2 4.2 %collective-permute-start.1 = (bf16[24,512]{1,0:T(8,128)(2,1)S(1)}, bf16[24,512]{1,0:T(8,128)(2,1)S(1)}, u32[]{:S(2)}, u32[]{:S(2)}) collective-permute-start(bf16[24,512]{1,0:T(8,128)(2,1)S(1)} %get-tuple-element.12.own_ref), channel_id=1, source_target_pairs={{0,2},{1,3},{2,0},{3,1},{4,6},{5,7},{6,4},{7,5},{8,10},{9,11},{10,... | collective-permute-start | bytes 73736 | tf_op jit(solution)/shard_map/ppermute | solution.py:267
  8.5 4.1 %collective-permute-start = (bf16[24,512]{1,0:T(8,128)(2,1)S(1)}, bf16[24,512]{1,0:T(8,128)(2,1)S(1)}, u32[]{:S(2)}, u32[]{:S(2)}) collective-permute-start(bf16[24,512]{1,0:T(8,128)(2,1)S(1)} %get-tuple-element.12.own_ref), channel_id=1, source_target_pairs={{0,1},{1,2},{2,3},{3,0},{4,5},{5,6},{6,7},{7,4},{8,9},{9,10},{10,1... | collective-permute-start | bytes 73736 | tf_op jit(solution)/shard_map/ppermute | solution.py:267
  14.0 3.6 %collective-permute-start.3 = (f32[768,128]{1,0:T(8,128)S(1)}, f32[768,128]{1,0:T(8,128)S(1)}, u32[]{:S(2)}, u32[]{:S(2)}) collective-permute-start(f32[768,128]{1,0:T(8,128)S(1)} %get-tuple-element.15), channel_id=1, source_target_pairs={{0,4},{4,0},{1,5},{5,1},{2,6},{6,2},{3,7},{7,3},{8,12},{12,8},{9,1... | collective-permute-start | bytes 1179656 | tf_op jit(solution)/shard_map/ppermute | solution.py:322
  17.7 3.7 %collective-permute-start.6 = (bf16[192,128]{1,0:T(8,128)(2,1)S(1)}, bf16[192,128]{1,0:T(8,128)(2,1)S(1)}, u32[]{:S(2)}, u32[]{:S(2)}) collective-permute-start(bf16[192,128]{1,0:T(8,128)(2,1)S(1)} %get-tuple-element.20), channel_id=1, source_target_pairs={{0,192},{64,0},{128,64},{192,128},{1,193},{65,1},{129,65},{193,129... | collective-permute-start | bytes 147464 | tf_op jit(solution)/shard_map/ppermute | solution.py:267
  20.3 4.5 %collective-permute-start.5 = (bf16[192,128]{1,0:T(8,128)(2,1)S(1)}, bf16[192,128]{1,0:T(8,128)(2,1)S(1)}, u32[]{:S(2)}, u32[]{:S(2)}) collective-permute-start(bf16[192,128]{1,0:T(8,128)(2,1)S(1)} %get-tuple-element.21), channel_id=1, source_target_pairs={{0,128},{64,192},{128,0},{192,64},{1,129},{65,193},{129,1},{193,65... | collective-permute-start | bytes 147464 | tf_op jit(solution)/shard_map/ppermute | solution.py:267
  20.8 4.5 %collective-permute-start.4 = (bf16[192,128]{1,0:T(8,128)(2,1)S(1)}, bf16[192,128]{1,0:T(8,128)(2,1)S(1)}, u32[]{:S(2)}, u32[]{:S(2)}) collective-permute-start(bf16[192,128]{1,0:T(8,128)(2,1)S(1)} %get-tuple-element.22), channel_id=1, source_target_pairs={{0,64},{64,128},{128,192},{192,0},{1,65},{65,129},{129,193},{193,1... | collective-permute-start | bytes 147464 | tf_op jit(solution)/shard_map/ppermute | solution.py:267
  52.7 5.5 %collective-permute-start.7 = (bf16[16,48,128]{2,1,0:T(8,128)(2,1)S(1)}, bf16[16,48,128]{2,1,0:T(8,128)(2,1)S(1)}, u32[]{:S(2)}, u32[]{:S(2)}) collective-permute-start(bf16[16,48,128]{2,1,0:T(8,128)(2,1)S(1)} %all_to_all.11.own_ref), channel_id=1, source_target_pairs={{0,4},{4,0},{1,5},{5,1},{2,6},{6,2},{3,7},{7,3},{8,12},{12,8},{9,1... | collective-permute-start | bytes 589832 | tf_op jit(solution)/shard_map/ppermute | solution.py:342

commit v2 on v1

--- a/solution.py
+++ b/solution.py
@@ -49,7 +49,7 @@
 
 def contract_kernel(
     mask_hbm, owner_hbm, index_hbm, blocks_hbm, active_hbm, inactive_hbm,
-    out_ref, blocks, route_ref, place_ref,
+    out_ref, blocks, route_ref, place_ref, keep_mask, pick_mask,
     mask_ref, owner_ref, index_ref, active, inactive, wide, halves, density, sums,
     int_sem, ina_sem, act_sem, block_sem,
 ):
@@ -70,9 +70,28 @@
     whole = [
         pltpu.make_async_copy(blocks_hbm.at[g], blocks.at[g], block_sem.at[g]) for g in range(SLOTS)
     ]
-    for c in ints + inactives + actives + whole:
+    for c in ints + inactives + actives:
         c.start()
+    for c in whole:
+        c.start(priority=1)
     wide[...] = jnp.zeros_like(wide)
+    offset = lanes((ACT, BW)) - sublanes((ACT, BW))
+    keep = offset == 0
+    for p in range(1, PER):
+        keep = keep | (offset == ACT * p)
+    keep = jnp.concatenate([keep.astype(F32)] * GROUPS, axis=1)
+    keep_mask[...] = keep
+    shape = (GROUPS * BW, BW)
+    lane = lanes(shape)
+    group = (
+        (lane >= PER).astype(jnp.int32)
+        + (lane >= 2 * PER).astype(jnp.int32)
+        + (lane >= 3 * PER).astype(jnp.int32)
+    )
+    start = group * BW + (lane - group * PER) * ACT
+    position = sublanes(shape) - start
+    pick = (position >= 0) & (position < ACT) & (lane < ROWS)
+    pick_mask[...] = pick.astype(F32).astype(BF16)
     for c in ints:
         c.wait()
     lives = [mask_ref[here * SLOTS + g] for g in range(SLOTS)]
@@ -152,8 +171,8 @@
 
 
 def expand_kernel(
-    own_ref, one_ref, two_ref, three_ref, blocks, keep_ref, send_ref,
-    coupling_ref, spread, left, coulomb, main, rest,
+    own_ref, one_ref, two_ref, three_ref, blocks, keep_mask, pick_mask, keep_ref, send_ref,
+    coupling_ref, spread, left, coulomb, main, rest, scaled_eye,
 ):
     here = lax.axis_index("pair")
     core = lax.axis_index("core")
@@ -165,36 +184,32 @@
     coupling = jnp.sum(jnp.where(lanes((ACT, BW)) == USED, both, 0.0), axis=1, keepdims=True)
     coupling_ref[...] = jnp.broadcast_to(coupling.astype(BF16).astype(F32), (ACT, BW))
     fitted = total.astype(BF16).astype(F32)
-    offset = lanes((ACT, BW)) - sublanes((ACT, BW))
-    keep = offset == 0
-    for p in range(1, PER):
-        keep = keep | (offset == ACT * p)
-    keep = jnp.concatenate([keep.astype(F32)] * GROUPS, axis=1)
+    keep = keep_mask[...]
     for t in range(0, ACT, 2):
         pair = jnp.concatenate(
             [jnp.broadcast_to(fitted[t + d : t + d + 1, :], keep.shape) * keep for d in range(2)],
             axis=0,
         )
         spread[pl.ds(t * ACT, 2 * ACT), :] = pair.astype(BF16)
-    shape = (GROUPS * BW, BW)
-    lane = lanes(shape)
-    group = (
-        (lane >= PER).astype(jnp.int32)
-        + (lane >= 2 * PER).astype(jnp.int32)
-        + (lane >= 3 * PER).astype(jnp.int32)
-    )
-    start = group * BW + (lane - group * PER) * ACT
-    position = sublanes(shape) - start
-    pick = (position >= 0) & (position < ACT) & (lane < ROWS)
     folded = jnp.dot(
-        spread[...], pick.astype(F32).astype(BF16), preferred_element_type=F32
+        spread[...], pick_mask[...], preferred_element_type=F32
     ).astype(BF16)
     left[...] = folded
     columns = left[pl.ds(pl.multiple_of(here * BW, BW), BW), :]
     tail = left[pl.ds(4 * BW, PAIRS - 4 * BW), :]
     main[...] = nt(folded, columns)
     rest[...] = nt(folded, jnp.concatenate([tail, tail], axis=0))
-    for g in range(SLOTS):
+    eye = (lanes((BW, BW)) == sublanes((BW, BW))).astype(F32)
+    for p in range(ROWS):
+        factor = jnp.broadcast_to(coupling_ref[pl.ds(p, 1), :], (BW, BW))
+        scaled_eye[pl.ds(p * BW, BW), :] = (eye * factor).astype(BF16)
+    joined = jnp.concatenate(
+        [jnp.concatenate([blocks[g, p] for p in range(ROWS)], axis=1) for g in (0, 1, 2)], axis=0
+    )
+    coulomb[pl.ds(0 * BW, 3 * BW), :] = jnp.dot(
+        joined, scaled_eye[...], preferred_element_type=F32
+    )
+    for g in (3,):
         total_g = jnp.zeros((BW, BW), F32)
         for p in range(ROWS):
             factor = jnp.broadcast_to(coupling_ref[pl.ds(p, 1), :], (BW, BW))
@@ -275,16 +290,18 @@
         block_mask, block_owner, block_index, three_centre, active_orbitals, inactive_orbitals
     )
     pinned = [pltpu.with_memory_space_constraint(a, pltpu.HBM) for a in inputs]
-    message, blocks, routes, places = pl.pallas_call(
+    message, blocks, routes, places, keep_mask, pick_mask = pl.pallas_call(
         contract_kernel,
         out_shape=[
             pltpu.VMEM((ACT, GROUPS * BW), BF16),
             pltpu.VMEM((SLOTS, ROWS, BW, BW), BF16),
             pltpu.VMEM((BW, BW), BF16),
             pltpu.VMEM((BW, BW), BF16),
+            pltpu.VMEM((ACT, GROUPS * BW), F32),
+            pltpu.VMEM((GROUPS * BW, BW), BF16),
         ],
         in_specs=[HBM] * 6,
-        out_specs=[VMEM] * 4,
+        out_specs=[VMEM] * 6,
         scratch_shapes=[
             pltpu.SMEM((16,), jnp.int32),
             pltpu.SMEM((16,), jnp.int32),
@@ -305,7 +322,7 @@
     keep, send = pl.pallas_call(
         expand_kernel,
         out_shape=[pltpu.VMEM((rows, BW), F32)] * 2,
-        in_specs=[VMEM] * 5,
+        in_specs=[VMEM] * 7,
         out_specs=[VMEM, VMEM],
         scratch_shapes=[
             pltpu.VMEM((ACT, BW), F32),
@@ -314,10 +331,11 @@
             pltpu.VMEM((SLOTS * BW, BW), F32),
             pltpu.VMEM((PAIRS, BW), F32),
             pltpu.VMEM((PAIRS, BW), F32),
+            pltpu.VMEM((ROWS * BW, BW), BF16),
         ],
         compiler_params=limit(8192),
         name="expand",
-    )(message, one, two, three, blocks)
+    )(message, one, two, three, blocks, keep_mask, pick_mask)
     swap = [(0, 1), (1, 0)]
     chip_sum = (keep + lax.ppermute(send, "core", swap)).reshape(NX, NZ * MSG, BW)
     one, two, three = from_others(chip_sum.astype(BF16), "x")

time: 59.3 us -> 58.8 us (level)
    pallas_call x1, Pallas kernels: 3.93 us -> 3.29 us  [shards(): pl.pallas_call(contract_kernel, out_shape=[pltpu.VMEM((ACT, GROUPS * BW),...]
where the time goes in v2:
time: 58.8 us; the launch traced here: 58.6 us
  blocking collectives  27.3 us (46%)
  starting transfers between devices  15 us (26%)
  waiting for transfers between devices  9.65 us (16%)
  Pallas kernels  5.97 us (10%)
  between operations  0.68 us (1%)
    all_to_all x1, blocking collectives, shards(): along_z = lax.all_to_all(pieces, 'z', 0, 0, tiled=True)  16.4 us
    all_to_all x1, blocking collectives, shards(): received = lax.all_to_all(pieces, ('pair', 'x'), 0, 0, tiled=True)  10.9 us
    ppermute x6, starting transfers between devices, from_others(): lax.ppermute(x if axis == 'pair' else x[s], axis, [(i, (i + s) % 4) for i...  8.35 us
    ppermute x6, waiting for transfers between devices, from_others(): lax.ppermute(x if axis == 'pair' else x[s], axis, [(i, (i + s) % 4) for i...  7.23 us
    ppermute x1, starting transfers between devices, shards(): partner = lax.ppermute(received, 'core', swap)  4.38 us
    pallas_call x1, Pallas kernels, shards(): pl.pallas_call(contract_kernel, out_shape=[pltpu.VMEM((ACT, GROUPS * BW),...  3.29 us
    ppermute x1, starting transfers between devices, shards(): lax.ppermute(send, 'core', swap)  2.27 us
    pallas_call x1, Pallas kernels, shards(): pl.pallas_call(expand_kernel, out_shape=[pltpu.VMEM((rows, BW), F32)] * 2...  1.49 us
  transfers between devices with their start and end apart: 8, of which 6 were waited for; matrix products, arithmetic and copies ran while one was open for 0% of the time, Pallas kernels for 0%

profile of v2, /device:TPU:1, one launch (start us, length us, event | category | flops | bytes accessed | tf_op | source)
XLA Modules:
  0.0 58.6 jit_solution(6001255833358331735)
XLA Ops:
  0.6 3.3 %contract.1 = (bf16[24,512]{1,0:T(8,128)(2,1)S(1)}, bf16[4,20,128,128]{3,2,1,0:T(8,128)(2,1)S(1)}, bf16[128,128]{1,0:T(8,128)(2,1)S(1)}, bf16[128,128]{1,0:T(8,1...) custom-call(s32[16]{0:T(128)} %mask_hbm.1, s32[16]{0:T(128)} %owner_hbm.1, s32[2,16]{1,0:T(2,128)} %index_hbm.1, ...), custom_call_target="tpu_custom_call" | custom-call | tf_op jit(solution)/shard_map/contract/pallas_call | solution.py:293
  3.9 3.6 %collective-permute-start.2 = (bf16[24,512]{1,0:T(8,128)(2,1)S(1)}, bf16[24,512]{1,0:T(8,128)(2,1)S(1)}, u32[]{:S(2)}, u32[]{:S(2)}) collective-permute-start(bf16[24,512]{1,0:T(8,128)(2,1)S(1)} %get-tuple-element.14.own_ref), channel_id=1, source_target_pairs={{0,3},{1,0},{2,1},{3,2},{4,7},{5,4},{6,5},{7,6},{8,11},{9,8},{10,9... | collective-permute-start | bytes 73736 | tf_op jit(solution)/shard_map/ppermute | solution.py:282
  7.6 0.4 collective-permute-start.1
  7.9 0.7 %collective-permute-start = (bf16[24,512]{1,0:T(8,128)(2,1)S(1)}, bf16[24,512]{1,0:T(8,128)(2,1)S(1)}, u32[]{:S(2)}, u32[]{:S(2)}) collective-permute-start(bf16[24,512]{1,0:T(8,128)(2,1)S(1)} %get-tuple-element.14.own_ref), channel_id=1, source_target_pairs={{0,1},{1,2},{2,3},{3,0},{4,5},{5,6},{6,7},{7,4},{8,9},{9,10},{10,1... | collective-permute-start | bytes 73736 | tf_op jit(solution)/shard_map/ppermute | solution.py:282
  8.6 0.0 collective-permute-done.2.three_ref
  8.6 3.2 %collective-permute-done.1.two_ref = bf16[24,512]{1,0:T(8,128)(2,1)S(1)} collective-permute-done((bf16[24,512]{1,0:T(8,128)(2,1)S(1)}, bf16[24,512]{1,0:T(8,128)(2,1)S(1)}, u32[]{:S(2)}, u32[]{:S(2)}) %collective-permute-start.1) | collective-permute-done | bytes 24608 | tf_op jit(solution)/shard_map/ppermute | solution.py:282
  11.8 0.2 collective-permute-done.one_ref
  12.0 1.5 %expand.1 = (f32[768,128]{1,0:T(8,128)S(1)}, f32[768,128]{1,0:T(8,128)S(1)}) custom-call(bf16[24,512]{1,0:T(8,128)(2,1)S(1)} %get-tuple-element.14.own_ref, bf16[24,512]{1,0:T(8,128)(2,1)S(1)} %collective-permute-done.one_ref, bf16[24,512]{1,0:T(8,128)(2,1)S(1)} %collective-permute-done.1.two_ref, bf16[24,512]{1,0:T(8,128)(2,1)S(1)} %collective-permute-done.2.three_ref, ...), custom_call_target="tpu_custom_call" | custom-call | tf_op jit(solution)/shard_map/expand/pallas_call | solution.py:322
  13.5 2.3 %collective-permute-start.3 = (f32[768,128]{1,0:T(8,128)S(1)}, f32[768,128]{1,0:T(8,128)S(1)}, u32[]{:S(2)}, u32[]{:S(2)}) collective-permute-start(f32[768,128]{1,0:T(8,128)S(1)} %get-tuple-element.19), channel_id=1, source_target_pairs={{0,4},{4,0},{1,5},{5,1},{2,6},{6,2},{3,7},{7,3},{8,12},{12,8},{9,1... | collective-permute-start | bytes 1179656 | tf_op jit(solution)/shard_map/ppermute | solution.py:340
  15.8 1.3 %collective-permute-done.3 = f32[768,128]{1,0:T(8,128)S(1)} collective-permute-done((f32[768,128]{1,0:T(8,128)S(1)}, f32[768,128]{1,0:T(8,128)S(1)}, u32[]{:S(2)}, u32[]{:S(2)}) %collective-permute-start.3) | collective-permute-done | bytes 393248 | tf_op jit(solution)/shard_map/ppermute | solution.py:340
  17.1 0.1 fusion
  17.2 2.6 %collective-permute-start.6 = (bf16[192,128]{1,0:T(8,128)(2,1)S(1)}, bf16[192,128]{1,0:T(8,128)(2,1)S(1)}, u32[]{:S(2)}, u32[]{:S(2)}) collective-permute-start(bf16[192,128]{1,0:T(8,128)(2,1)S(1)} %get-tuple-element.24), channel_id=1, source_target_pairs={{0,192},{64,0},{128,64},{192,128},{1,193},{65,1},{129,65},{193,129... | collective-permute-start | bytes 147464 | tf_op jit(solution)/shard_map/ppermute | solution.py:282
  19.8 0.5 collective-permute-start.5
  20.3 0.6 %collective-permute-start.4 = (bf16[192,128]{1,0:T(8,128)(2,1)S(1)}, bf16[192,128]{1,0:T(8,128)(2,1)S(1)}, u32[]{:S(2)}, u32[]{:S(2)}) collective-permute-start(bf16[192,128]{1,0:T(8,128)(2,1)S(1)} %get-tuple-element.26), channel_id=1, source_target_pairs={{0,64},{64,128},{128,192},{192,0},{1,65},{65,129},{129,193},{193,1... | collective-permute-start | bytes 147464 | tf_op jit(solution)/shard_map/ppermute | solution.py:282
  20.9 0.0 collective-permute-done.6.three_ref
  20.9 3.3 %collective-permute-done.5.two_ref = bf16[192,128]{1,0:T(8,128)(2,1)S(1)} collective-permute-done((bf16[192,128]{1,0:T(8,128)(2,1)S(1)}, bf16[192,128]{1,0:T(8,128)(2,1)S(1)}, u32[]{:S(2)}, u32[]{:S(2)}) %collective-permute-start.5) | collective-permute-done | bytes 49184 | tf_op jit(solution)/shard_map/ppermute | solution.py:282
  24.2 0.5 collective-permute-done.4.one_ref
  24.8 16.4 %all_to_all.10.parts_ref = bf16[8,80,128]{2,1,0:T(8,128)(2,1)S(1)} all-to-all(bf16[8,80,128]{2,1,0:T(8,128)(2,1)S(1)} %along_x.1), channel_id=1, replica_groups=mesh['x'=4,'z'=8,'core'=2,'pair'=4] {'z'}, dimensions={0} | all-to-all | bytes 327680 | tf_op jit(solution)/shard_map/all_to_all | solution.py:350
  41.1 0.1 route.1
  41.3 10.9 %all_to_all.11.own_ref = bf16[16,48,128]{2,1,0:T(8,128)(2,1)S(1)} all-to-all(bf16[16,48,128]{2,1,0:T(8,128)(2,1)S(1)} %route.1), channel_id=1, replica_groups=mesh['x'=4,'z'=8,'core'=2,'pair'=4] {'pair','x'}, dimensions={0} | all-to-all | bytes 393216 | tf_op jit(solution)/shard_map/all_to_all | solution.py:359
  52.2 4.4 %collective-permute-start.7 = (bf16[16,48,128]{2,1,0:T(8,128)(2,1)S(1)}, bf16[16,48,128]{2,1,0:T(8,128)(2,1)S(1)}, u32[]{:S(2)}, u32[]{:S(2)}) collective-permute-start(bf16[16,48,128]{2,1,0:T(8,128)(2,1)S(1)} %all_to_all.11.own_ref), channel_id=1, source_target_pairs={{0,4},{4,0},{1,5},{5,1},{2,6},{6,2},{3,7},{7,3},{8,12},{12,8},{9,1... | collective-permute-start | bytes 589832 | tf_op jit(solution)/shard_map/ppermute | solution.py:360
  56.5 1.1 %collective-permute-done.7.other_ref = bf16[16,48,128]{2,1,0:T(8,128)(2,1)S(1)} collective-permute-done((bf16[16,48,128]{2,1,0:T(8,128)(2,1)S(1)}, bf16[16,48,128]{2,1,0:T(8,128)(2,1)S(1)}, u32[]{:S(2)}, u32[]{:S(2)}) %collective-permute-start.7) | collective-permute-done | bytes 196640 | tf_op jit(solution)/shard_map/ppermute | solution.py:360
  57.6 1.0 %place.1 = (f32[1024,128]{1,0:T(8,128)}, f32[9,576]{1,0:T(8,128)}) custom-call(bf16[128,128]{1,0:T(8,128)(2,1)S(1)} %get-tuple-element.12.place_ref, bf16[16,48,128]{2,1,0:T(8,128)(2,1)S(1)} %all_to_all.11.own_ref, bf16[16,48,128]{2,1,0:T(8,128)(2,1)S(1)} %collective-permute-done.7.other_ref), custom_call_target="tpu_custom_call" | custom-call | tf_op jit(solution)/shard_map/place/pallas_call | solution.py:361
  (3 shorter events, 0.0 us)
Async XLA Ops:
  3.9 4.7 %collective-permute-start.2 = (bf16[24,512]{1,0:T(8,128)(2,1)S(1)}, bf16[24,512]{1,0:T(8,128)(2,1)S(1)}, u32[]{:S(2)}, u32[]{:S(2)}) collective-permute-start(bf16[24,512]{1,0:T(8,128)(2,1)S(1)} %get-tuple-element.14.own_ref), channel_id=1, source_target_pairs={{0,3},{1,0},{2,1},{3,2},{4,7},{5,4},{6,5},{7,6},{8,11},{9,8},{10,9... | collective-permute-start | bytes 73736 | tf_op jit(solution)/shard_map/ppermute | solution.py:282
  7.6 4.2 %collective-permute-start.1 = (bf16[24,512]{1,0:T(8,128)(2,1)S(1)}, bf16[24,512]{1,0:T(8,128)(2,1)S(1)}, u32[]{:S(2)}, u32[]{:S(2)}) collective-permute-start(bf16[24,512]{1,0:T(8,128)(2,1)S(1)} %get-tuple-element.14.own_ref), channel_id=1, source_target_pairs={{0,2},{1,3},{2,0},{3,1},{4,6},{5,7},{6,4},{7,5},{8,10},{9,11},{10,... | collective-permute-start | bytes 73736 | tf_op jit(solution)/shard_map/ppermute | solution.py:282
  7.9 4.1 %collective-permute-start = (bf16[24,512]{1,0:T(8,128)(2,1)S(1)}, bf16[24,512]{1,0:T(8,128)(2,1)S(1)}, u32[]{:S(2)}, u32[]{:S(2)}) collective-permute-start(bf16[24,512]{1,0:T(8,128)(2,1)S(1)} %get-tuple-element.14.own_ref), channel_id=1, source_target_pairs={{0,1},{1,2},{2,3},{3,0},{4,5},{5,6},{6,7},{7,4},{8,9},{9,10},{10,1... | collective-permute-start | bytes 73736 | tf_op jit(solution)/shard_map/ppermute | solution.py:282
  13.5 3.6 %collective-permute-start.3 = (f32[768,128]{1,0:T(8,128)S(1)}, f32[768,128]{1,0:T(8,128)S(1)}, u32[]{:S(2)}, u32[]{:S(2)}) collective-permute-start(f32[768,128]{1,0:T(8,128)S(1)} %get-tuple-element.19), channel_id=1, source_target_pairs={{0,4},{4,0},{1,5},{5,1},{2,6},{6,2},{3,7},{7,3},{8,12},{12,8},{9,1... | collective-permute-start | bytes 1179656 | tf_op jit(solution)/shard_map/ppermute | solution.py:340
  17.2 3.7 %collective-permute-start.6 = (bf16[192,128]{1,0:T(8,128)(2,1)S(1)}, bf16[192,128]{1,0:T(8,128)(2,1)S(1)}, u32[]{:S(2)}, u32[]{:S(2)}) collective-permute-start(bf16[192,128]{1,0:T(8,128)(2,1)S(1)} %get-tuple-element.24), channel_id=1, source_target_pairs={{0,192},{64,0},{128,64},{192,128},{1,193},{65,1},{129,65},{193,129... | collective-permute-start | bytes 147464 | tf_op jit(solution)/shard_map/ppermute | solution.py:282
  19.8 4.5 %collective-permute-start.5 = (bf16[192,128]{1,0:T(8,128)(2,1)S(1)}, bf16[192,128]{1,0:T(8,128)(2,1)S(1)}, u32[]{:S(2)}, u32[]{:S(2)}) collective-permute-start(bf16[192,128]{1,0:T(8,128)(2,1)S(1)} %get-tuple-element.25), channel_id=1, source_target_pairs={{0,128},{64,192},{128,0},{192,64},{1,129},{65,193},{129,1},{193,65... | collective-permute-start | bytes 147464 | tf_op jit(solution)/shard_map/ppermute | solution.py:282
  20.3 4.4 %collective-permute-start.4 = (bf16[192,128]{1,0:T(8,128)(2,1)S(1)}, bf16[192,128]{1,0:T(8,128)(2,1)S(1)}, u32[]{:S(2)}, u32[]{:S(2)}) collective-permute-start(bf16[192,128]{1,0:T(8,128)(2,1)S(1)} %get-tuple-element.26), channel_id=1, source_target_pairs={{0,64},{64,128},{128,192},{192,0},{1,65},{65,129},{129,193},{193,1... | collective-permute-start | bytes 147464 | tf_op jit(solution)/shard_map/ppermute | solution.py:282
  52.2 5.5 %collective-permute-start.7 = (bf16[16,48,128]{2,1,0:T(8,128)(2,1)S(1)}, bf16[16,48,128]{2,1,0:T(8,128)(2,1)S(1)}, u32[]{:S(2)}, u32[]{:S(2)}) collective-permute-start(bf16[16,48,128]{2,1,0:T(8,128)(2,1)S(1)} %all_to_all.11.own_ref), channel_id=1, source_target_pairs={{0,4},{4,0},{1,5},{5,1},{2,6},{6,2},{3,7},{7,3},{8,12},{12,8},{9,1... | collective-permute-start | bytes 589832 | tf_op jit(solution)/shard_map/ppermute | solution.py:360

commit v3 on v2

--- a/solution.py
+++ b/solution.py
@@ -23,7 +23,7 @@
 AUX = 1280
 NIN = 256
 NAO = 3072
-MSG = 24
+MSG = 48
 F32 = jnp.float32
 BF16 = jnp.bfloat16
 
@@ -171,11 +171,10 @@
 
 
 def expand_kernel(
-    own_ref, one_ref, two_ref, three_ref, blocks, keep_mask, pick_mask, keep_ref, send_ref,
-    coupling_ref, spread, left, coulomb, main, rest, scaled_eye,
+    own_ref, one_ref, two_ref, three_ref, blocks, keep_mask, pick_mask, own_out, send_out,
+    coupling_ref, spread, left, coulomb, main, rest,
 ):
     here = lax.axis_index("pair")
-    core = lax.axis_index("core")
     along = lax.axis_index("x")
     total = (own_ref[...].astype(F32) + two_ref[...].astype(F32)) + (
         one_ref[...].astype(F32) + three_ref[...].astype(F32)
@@ -199,39 +198,36 @@
     tail = left[pl.ds(4 * BW, PAIRS - 4 * BW), :]
     main[...] = nt(folded, columns)
     rest[...] = nt(folded, jnp.concatenate([tail, tail], axis=0))
-    eye = (lanes((BW, BW)) == sublanes((BW, BW))).astype(F32)
-    for p in range(ROWS):
-        factor = jnp.broadcast_to(coupling_ref[pl.ds(p, 1), :], (BW, BW))
-        scaled_eye[pl.ds(p * BW, BW), :] = (eye * factor).astype(BF16)
-    joined = jnp.concatenate(
-        [jnp.concatenate([blocks[g, p] for p in range(ROWS)], axis=1) for g in (0, 1, 2)], axis=0
-    )
-    coulomb[pl.ds(0 * BW, 3 * BW), :] = jnp.dot(
-        joined, scaled_eye[...], preferred_element_type=F32
-    )
-    for g in (3,):
+    def one(g, carry):
         total_g = jnp.zeros((BW, BW), F32)
         for p in range(ROWS):
             factor = jnp.broadcast_to(coupling_ref[pl.ds(p, 1), :], (BW, BW))
             total_g = total_g + blocks[g, p].astype(F32) * factor
-        coulomb[pl.ds(g * BW, BW), :] = total_g
+        coulomb[pl.ds(pl.multiple_of(g * BW, BW), BW), :] = total_g
+        return carry
+
+    lax.fori_loop(0, SLOTS, one, 0)
     low_lane = lanes((NZ, BW)) < BW // 2
-    for ref, which in ((keep_ref, core), (send_ref, 1 - core)):
-        for step in range(NX):
-            x = lax.rem(along + step, NX)
-            base = step * NZ * MSG
-            for z in range(NZ):
-                row = pl.multiple_of(z // 2 * BW + 32 * x + 16 * which + 8 * (z % 2), 8)
-                ref[pl.ds(base + z * MSG, 8), :] = coulomb[pl.ds(row, 8), :]
-            first = 144 * x + 9 * which
+    for step in range(NX):
+        x = lax.rem(along + step, NX)
+        base = step * NZ * MSG
+        for z in range(NZ):
+            row = pl.multiple_of(z // 2 * BW + 32 * x + 16 * (z % 2), 16)
+            own_out[pl.ds(base + z * MSG, 16), :] = coulomb[pl.ds(row, 16), :]
+        for c in range(CORES):
+            first = 144 * x + 9 * c
+            start = base + 16 + 16 * c
             for s in range(9):
-                ref[pl.ds(base + 8 + s, NZ, stride=MSG), :] = main[pl.ds(first + s, NZ, stride=18), :]
+                own_out[pl.ds(start + s, NZ, stride=MSG), :] = main[
+                    pl.ds(first + s, NZ, stride=18), :
+                ]
             for s in range(7):
                 value = rest[pl.ds(first + s, NZ, stride=18), :]
                 if s < 2:
                     other = rest[pl.ds(first + 7 + s, NZ, stride=18), :]
                     value = jnp.where(low_lane, value, other)
-                ref[pl.ds(base + 17 + s, NZ, stride=MSG), :] = value
+                own_out[pl.ds(start + 9 + s, NZ, stride=MSG), :] = value
+    send_out[...] = own_out[...].astype(BF16)
 
 
 def along_x_kernel(own_ref, one_ref, two_ref, three_ref, out_ref):
@@ -239,48 +235,71 @@
     for ref in (one_ref, two_ref, three_ref):
         total = total + ref[...].astype(F32)
     pieces = [total[z * MSG : (z + 1) * MSG] for z in range(NZ)]
-    fock = jnp.concatenate([p[0:8] for p in pieces], axis=0).astype(BF16)
+    fock = jnp.concatenate([p[0:16] for p in pieces], axis=0).astype(BF16)
     for z in range(NZ):
-        out_ref[z, 0:64, :] = fock
-        out_ref[z, 64:80, :] = pieces[z][8:MSG].astype(BF16)
+        out_ref[z, 0:128, :] = fock
+        out_ref[z, 128:160, :] = pieces[z][16:MSG].astype(BF16)
 
 
 def route_kernel(route_ref, parts_ref, out_ref):
     total = jnp.sum(parts_ref[...].astype(F32), axis=0)
-    gram = (total[64:80] * (1.0 / AUX)).astype(BF16)
-    scaled = total[0:64] * (1.0 / math.sqrt(AUX))
-    scaled = jnp.concatenate([scaled, jnp.zeros_like(scaled)], axis=0).astype(BF16)
-    chosen = jnp.dot(route_ref[...], scaled, preferred_element_type=F32).astype(BF16)
+    gram = (total[128:160] * (1.0 / AUX)).astype(BF16)
+    scaled = total[0:128] * (1.0 / math.sqrt(AUX))
+    halves = []
+    for h in range(2):
+        rows = [scaled[32 * g + 16 * h : 32 * g + 16 * h + 16] for g in range(SLOTS)]
+        halves.append(jnp.concatenate(rows + [jnp.zeros((64, BW), F32)], axis=0))
+    source = jnp.concatenate(halves, axis=1).astype(BF16)
+    chosen = jnp.dot(route_ref[...], source, preferred_element_type=F32).astype(BF16)
     for o in range(OWNERS):
         for x in range(NX):
-            out_ref[o * NX + x, 0:32, :] = chosen[32 * o : 32 * (o + 1)]
-            out_ref[o * NX + x, 32:48, :] = gram
+            for h in range(2):
+                out_ref[o * NX + x, 32 * h : 32 * (h + 1), :] = chosen[
+                    32 * o : 32 * (o + 1), h * BW : (h + 1) * BW
+                ]
+            out_ref[o * NX + x, 64:96, :] = gram
 
 
 def place_kernel(place_ref, own_ref, other_ref, fock_ref, gram_ref):
     core = lax.axis_index("core")
     along = lax.axis_index("x")
-    table = place_ref[...]
-    for n, ref in enumerate((own_ref, other_ref)):
-        which = core if n == 0 else 1 - core
-        for x in range(NX):
-            pieces = jnp.concatenate([ref[q * NX + x, 0:32, :] for q in range(OWNERS)], axis=0)
-            placed = jnp.dot(table, pieces, preferred_element_type=F32)
-            for rank in range(8):
-                row = pl.multiple_of(rank * BW + 32 * x + 16 * which, 16)
-                fock_ref[pl.ds(row, 16), :] = placed[16 * rank : 16 * (rank + 1)]
-    for q in range(OWNERS):
-        gram = own_ref[q * NX + along, 32:48, :].astype(F32)
-        gram_ref[:, q * BW : (q + 1) * BW] = gram[0:9]
-        if q == 0:
-            gram_ref[0:7, 4 * BW : PAIRS] = gram[9:16, 0 : BW // 2]
-            gram_ref[7:9, 4 * BW : PAIRS] = gram[9:11, BW // 2 : BW]
-
-
-def from_others(x, axis="pair"):
+    for c, ref in enumerate((other_ref, own_ref)):
+
+        @pl.when(core == c)
+        def _(c=c, ref=ref):
+            table = place_ref[...]
+            for x in range(NX):
+                for h in range(2):
+                    pieces = jnp.concatenate(
+                        [ref[q * NX + x, 32 * h : 32 * (h + 1), :] for q in range(OWNERS)], axis=0
+                    )
+                    placed = jnp.dot(table, pieces, preferred_element_type=F32)
+                    for rank in range(8):
+                        row = rank * BW + 32 * x + 16 * h
+                        fock_ref[row : row + 16, :] = placed[16 * rank : 16 * (rank + 1)]
+            for q in range(OWNERS):
+                gram = ref[q * NX + along, 64 + 16 * c : 80 + 16 * c, :].astype(F32)
+                gram_ref[:, q * BW : (q + 1) * BW] = gram[0:9]
+                if q == 0:
+                    gram_ref[0:7, 4 * BW : PAIRS] = gram[9:16, 0 : BW // 2]
+                    gram_ref[7:9, 4 * BW : PAIRS] = gram[9:11, BW // 2 : BW]
+
+
+def from_others(x):
     return [
-        lax.ppermute(x if axis == "pair" else x[s], axis, [(i, (i + s) % 4) for i in range(4)])
-        for s in range(1, 4)
+        lax.ppermute(x, "pair", [(i, (i + s) % OWNERS) for i in range(OWNERS)])
+        for s in range(1, OWNERS)
+    ]
+
+
+def from_north(pieces):
+    return [
+        lax.ppermute(
+            pieces[s],
+            ("x", "core"),
+            [(CORES * i + 1, CORES * ((i + s) % NX) + 1) for i in range(NX)],
+        )
+        for s in range(1, NX)
     ]
 
 
@@ -318,10 +337,10 @@
         name="contract",
     )(*pinned)
     one, two, three = from_others(message)
-    rows = CHIPS * MSG
-    keep, send = pl.pallas_call(
+    rows = NX * NZ * MSG
+    own, send = pl.pallas_call(
         expand_kernel,
-        out_shape=[pltpu.VMEM((rows, BW), F32)] * 2,
+        out_shape=[pltpu.VMEM((rows, BW), F32), pltpu.VMEM((rows, BW), BF16)],
         in_specs=[VMEM] * 7,
         out_specs=[VMEM, VMEM],
         scratch_shapes=[
@@ -331,17 +350,16 @@
             pltpu.VMEM((SLOTS * BW, BW), F32),
             pltpu.VMEM((PAIRS, BW), F32),
             pltpu.VMEM((PAIRS, BW), F32),
-            pltpu.VMEM((ROWS * BW, BW), BF16),
         ],
         compiler_params=limit(8192),
         name="expand",
     )(message, one, two, three, blocks, keep_mask, pick_mask)
-    swap = [(0, 1), (1, 0)]
-    chip_sum = (keep + lax.ppermute(send, "core", swap)).reshape(NX, NZ * MSG, BW)
-    one, two, three = from_others(chip_sum.astype(BF16), "x")
+    chip_sum = own + lax.ppermute(send, "core", [(0, 1)]).astype(F32)
+    chip_sum = chip_sum.reshape(NX, NZ * MSG, BW)
+    one, two, three = from_north(chip_sum.astype(BF16))
     pieces = pl.pallas_call(
         along_x_kernel,
-        out_shape=pltpu.VMEM((NZ, 80, BW), BF16),
+        out_shape=pltpu.VMEM((NZ, 160, BW), BF16),
         in_specs=[VMEM] * 4,
         out_specs=VMEM,
         compiler_params=limit(4096),
@@ -350,14 +368,14 @@
     along_z = lax.all_to_all(pieces, "z", 0, 0, tiled=True)
     pieces = pl.pallas_call(
         route_kernel,
-        out_shape=pltpu.VMEM((OWNERS * NX, 48, BW), BF16),
+        out_shape=pltpu.VMEM((OWNERS * NX, 96, BW), BF16),
         in_specs=[VMEM] * 2,
         out_specs=VMEM,
         compiler_params=limit(4096),
         name="route",
     )(routes, along_z)
     received = lax.all_to_all(pieces, ("pair", "x"), 0, 0, tiled=True)
-    partner = lax.ppermute(received, "core", swap)
+    partner = lax.ppermute(received, "core", [(1, 0)])
     fock, integrals = pl.pallas_call(
         place_kernel,
         out_shape=[

time: 58.8 us -> 65.9 us (1.12)
  blocking collectives: 27.3 us -> 30.1 us
  waiting for transfers between devices: 9.65 us -> 12.1 us
  starting transfers between devices: 15 us -> 16.6 us
    ppermute x8, waiting for transfers between devices: 9.65 us -> 12.1 us  [the longest x3 4.01 us: from_north(): lax.ppermute(pieces[s], ('x', 'core'), [(CORES * i + 1, CORES * ((i + s)...]
    all_to_all x1, blocking collectives: 16.4 us -> 18.3 us  [shards(): along_z = lax.all_to_all(pieces, 'z', 0, 0, tiled=True)]
    ppermute x8, starting transfers between devices: 15 us -> 16.6 us  [the longest x3 9.33 us: from_north(): lax.ppermute(pieces[s], ('x', 'core'), [(CORES * i + 1, CORES * ((i + s)...]
    all_to_all x1, blocking collectives: 10.9 us -> 11.8 us  [shards(): received = lax.all_to_all(pieces, ('pair', 'x'), 0, 0, tiled=True)]
where the time goes in v3:
time: 65.9 us; the launch traced here: 65.6 us
  blocking collectives  30.1 us (46%)
  starting transfers between devices  16.6 us (25%)
  waiting for transfers between devices  12.1 us (18%)
  Pallas kernels  5.93 us (9%)
  between operations  0.73 us (1%)
    all_to_all x1, blocking collectives, shards(): along_z = lax.all_to_all(pieces, 'z', 0, 0, tiled=True)  18.3 us
    all_to_all x1, blocking collectives, shards(): received = lax.all_to_all(pieces, ('pair', 'x'), 0, 0, tiled=True)  11.8 us
    ppermute x3, starting transfers between devices, from_north(): lax.ppermute(pieces[s], ('x', 'core'), [(CORES * i + 1, CORES * ((i + s)...  9.33 us
    ppermute x3, starting transfers between devices, from_others(): lax.ppermute(x, 'pair', [(i, (i + s) % OWNERS) for i in range(OWNERS)])  4.67 us
    ppermute x3, waiting for transfers between devices, from_north(): lax.ppermute(pieces[s], ('x', 'core'), [(CORES * i + 1, CORES * ((i + s)...  4.01 us
    ppermute x3, waiting for transfers between devices, from_others(): lax.ppermute(x, 'pair', [(i, (i + s) % OWNERS) for i in range(OWNERS)])  3.4 us
    ppermute x1, waiting for transfers between devices, shards(): chip_sum = own + lax.ppermute(send, 'core', [(0, 1)]).astype(F32)  3.37 us
    pallas_call x1, Pallas kernels, shards(): pl.pallas_call(contract_kernel, out_shape=[pltpu.VMEM((ACT, GROUPS * BW),...  3.29 us
  transfers between devices with their start and end apart: 8, of which 6 were waited for; matrix products, arithmetic and copies ran while one was open for 0% of the time, Pallas kernels for 0%

profile of v3, /device:TPU:1, one launch (start us, length us, event | category | flops | bytes accessed | tf_op | source)
XLA Modules:
  0.0 65.6 jit_solution(7531347260865957435)
XLA Ops:
  0.6 3.3 %contract.1 = (bf16[24,512]{1,0:T(8,128)(2,1)S(1)}, bf16[4,20,128,128]{3,2,1,0:T(8,128)(2,1)S(1)}, bf16[128,128]{1,0:T(8,128)(2,1)S(1)}, bf16[128,128]{1,0:T(8,1...) custom-call(s32[16]{0:T(128)} %mask_hbm.1, s32[16]{0:T(128)} %owner_hbm.1, s32[2,16]{1,0:T(2,128)} %index_hbm.1, ...), custom_call_target="tpu_custom_call" | custom-call | tf_op jit(solution)/shard_map/contract/pallas_call | solution.py:312
  3.9 3.6 %collective-permute-start.2 = (bf16[24,512]{1,0:T(8,128)(2,1)S(1)}, bf16[24,512]{1,0:T(8,128)(2,1)S(1)}, u32[]{:S(2)}, u32[]{:S(2)}) collective-permute-start(bf16[24,512]{1,0:T(8,128)(2,1)S(1)} %get-tuple-element.14.own_ref), channel_id=1, source_target_pairs={{0,3},{1,0},{2,1},{3,2},{4,7},{5,4},{6,5},{7,6},{8,11},{9,8},{10,9... | collective-permute-start | bytes 73736 | tf_op jit(solution)/shard_map/ppermute | solution.py:290
  7.6 0.4 collective-permute-start.1
  7.9 0.7 %collective-permute-start = (bf16[24,512]{1,0:T(8,128)(2,1)S(1)}, bf16[24,512]{1,0:T(8,128)(2,1)S(1)}, u32[]{:S(2)}, u32[]{:S(2)}) collective-permute-start(bf16[24,512]{1,0:T(8,128)(2,1)S(1)} %get-tuple-element.14.own_ref), channel_id=1, source_target_pairs={{0,1},{1,2},{2,3},{3,0},{4,5},{5,6},{6,7},{7,4},{8,9},{9,10},{10,1... | collective-permute-start | bytes 73736 | tf_op jit(solution)/shard_map/ppermute | solution.py:290
  8.6 0.0 collective-permute-done.2.three_ref
  8.6 3.2 %collective-permute-done.1.two_ref = bf16[24,512]{1,0:T(8,128)(2,1)S(1)} collective-permute-done((bf16[24,512]{1,0:T(8,128)(2,1)S(1)}, bf16[24,512]{1,0:T(8,128)(2,1)S(1)}, u32[]{:S(2)}, u32[]{:S(2)}) %collective-permute-start.1) | collective-permute-done | bytes 24608 | tf_op jit(solution)/shard_map/ppermute | solution.py:290
  11.8 0.2 collective-permute-done.one_ref
  12.0 1.4 %expand.1 = (f32[1536,128]{1,0:T(8,128)S(1)}, bf16[1536,128]{1,0:T(8,128)(2,1)S(1)}) custom-call(bf16[24,512]{1,0:T(8,128)(2,1)S(1)} %get-tuple-element.14.own_ref, bf16[24,512]{1,0:T(8,128)(2,1)S(1)} %collective-permute-done.one_ref, bf16[24,512]{1,0:T(8,128)(2,1)S(1)} %collective-permute-done.1.two_ref, ...), custom_call_target="tpu_custom_call" | custom-call | tf_op jit(solution)/shard_map/expand/pallas_call | solution.py:341
  13.4 1.3 %collective-permute-start.3 = (bf16[1536,128]{1,0:T(8,128)(2,1)S(1)}, bf16[1536,128]{1,0:T(8,128)(2,1)S(1)}, u32[]{:S(2)}, u32[]{:S(2)}) collective-permute-start(bf16[1536,128]{1,0:T(8,128)(2,1)S(1)} %get-tuple-element.19), channel_id=1, source_target_pairs={{0,4},{1,5},{2,6},{3,7},{8,12},{9,13},{10,14},{11,15},{16,20},{17,... | collective-permute-start | bytes 1179656 | tf_op jit(solution)/shard_map/ppermute | solution.py:357
  14.7 3.4 %collective-permute-done.3 = bf16[1536,128]{1,0:T(8,128)(2,1)S(1)} collective-permute-done((bf16[1536,128]{1,0:T(8,128)(2,1)S(1)}, bf16[1536,128]{1,0:T(8,128)(2,1)S(1)}, u32[]{:S(2)}, u32[]{:S(2)}) %collective-permute-start.3) | collective-permute-done | bytes 393248 | tf_op jit(solution)/shard_map/ppermute | solution.py:357
  18.1 0.1 fusion
  18.2 4.4 %collective-permute-start.6 = (bf16[384,128]{1,0:T(8,128)(2,1)S(1)}, bf16[384,128]{1,0:T(8,128)(2,1)S(1)}, u32[]{:S(2)}, u32[]{:S(2)}) collective-permute-start(bf16[384,128]{1,0:T(8,128)(2,1)S(1)} %get-tuple-element.24), channel_id=1, source_target_pairs={{4,196},{68,4},{132,68},{196,132},{5,197},{69,5},{133,69},{197,133... | collective-permute-start | bytes 294920 | tf_op jit(solution)/shard_map/ppermute | solution.py:297
  22.6 2.4 %collective-permute-start.5 = (bf16[384,128]{1,0:T(8,128)(2,1)S(1)}, bf16[384,128]{1,0:T(8,128)(2,1)S(1)}, u32[]{:S(2)}, u32[]{:S(2)}) collective-permute-start(bf16[384,128]{1,0:T(8,128)(2,1)S(1)} %get-tuple-element.25), channel_id=1, source_target_pairs={{4,132},{68,196},{132,4},{196,68},{5,133},{69,197},{133,5},{197,69... | collective-permute-start | bytes 294920 | tf_op jit(solution)/shard_map/ppermute | solution.py:297
  25.1 2.5 %collective-permute-start.4 = (bf16[384,128]{1,0:T(8,128)(2,1)S(1)}, bf16[384,128]{1,0:T(8,128)(2,1)S(1)}, u32[]{:S(2)}, u32[]{:S(2)}) collective-permute-start(bf16[384,128]{1,0:T(8,128)(2,1)S(1)} %get-tuple-element.26), channel_id=1, source_target_pairs={{4,68},{68,132},{132,196},{196,4},{5,69},{69,133},{133,197},{197,5... | collective-permute-start | bytes 294920 | tf_op jit(solution)/shard_map/ppermute | solution.py:297
  27.6 0.0 collective-permute-done.6.three_ref
  27.6 1.9 %collective-permute-done.5.two_ref = bf16[384,128]{1,0:T(8,128)(2,1)S(1)} collective-permute-done((bf16[384,128]{1,0:T(8,128)(2,1)S(1)}, bf16[384,128]{1,0:T(8,128)(2,1)S(1)}, u32[]{:S(2)}, u32[]{:S(2)}) %collective-permute-start.5) | collective-permute-done | bytes 98336 | tf_op jit(solution)/shard_map/ppermute | solution.py:297
  29.5 2.1 %collective-permute-done.4.one_ref = bf16[384,128]{1,0:T(8,128)(2,1)S(1)} collective-permute-done((bf16[384,128]{1,0:T(8,128)(2,1)S(1)}, bf16[384,128]{1,0:T(8,128)(2,1)S(1)}, u32[]{:S(2)}, u32[]{:S(2)}) %collective-permute-start.4) | collective-permute-done | bytes 98336 | tf_op jit(solution)/shard_map/ppermute | solution.py:297
  31.7 18.3 %all_to_all.10.parts_ref = bf16[8,160,128]{2,1,0:T(8,128)(2,1)S(1)} all-to-all(bf16[8,160,128]{2,1,0:T(8,128)(2,1)S(1)} %along_x.1), channel_id=1, replica_groups=mesh['x'=4,'z'=8,'core'=2,'pair'=4] {'z'}, dimensions={0} | all-to-all | bytes 655360 | tf_op jit(solution)/shard_map/all_to_all | solution.py:368
  50.0 0.2 route.1
  50.2 11.8 %all_to_all.11.own_ref = bf16[16,96,128]{2,1,0:T(8,128)(2,1)S(1)} all-to-all(bf16[16,96,128]{2,1,0:T(8,128)(2,1)S(1)} %route.1), channel_id=1, replica_groups=mesh['x'=4,'z'=8,'core'=2,'pair'=4] {'pair','x'}, dimensions={0} | all-to-all | bytes 786432 | tf_op jit(solution)/shard_map/all_to_all | solution.py:377
  62.0 1.3 %collective-permute-start.7 = (bf16[16,96,128]{2,1,0:T(8,128)(2,1)S(1)}, bf16[16,96,128]{2,1,0:T(8,128)(2,1)S(1)}, u32[]{:S(2)}, u32[]{:S(2)}) collective-permute-start(bf16[16,96,128]{2,1,0:T(8,128)(2,1)S(1)} %all_to_all.11.own_ref), channel_id=1, source_target_pairs={{4,0},{5,1},{6,2},{7,3},{12,8},{13,9},{14,10},{15,11},{20,16},{21,... | collective-permute-start | bytes 1179656 | tf_op jit(solution)/shard_map/ppermute | solution.py:378
  63.3 1.3 %collective-permute-done.7.other_ref = bf16[16,96,128]{2,1,0:T(8,128)(2,1)S(1)} collective-permute-done((bf16[16,96,128]{2,1,0:T(8,128)(2,1)S(1)}, bf16[16,96,128]{2,1,0:T(8,128)(2,1)S(1)}, u32[]{:S(2)}, u32[]{:S(2)}) %collective-permute-start.7) | collective-permute-done | bytes 393248 | tf_op jit(solution)/shard_map/ppermute | solution.py:378
  64.6 1.0 %place.1 = (f32[1024,128]{1,0:T(8,128)}, f32[9,576]{1,0:T(8,128)}) custom-call(bf16[128,128]{1,0:T(8,128)(2,1)S(1)} %get-tuple-element.12.place_ref, bf16[16,96,128]{2,1,0:T(8,128)(2,1)S(1)} %all_to_all.11.own_ref, bf16[16,96,128]{2,1,0:T(8,128)(2,1)S(1)} %collective-permute-done.7.other_ref), custom_call_target="tpu_custom_call" | custom-call | tf_op jit(solution)/shard_map/place/pallas_call | solution.py:379
  (3 shorter events, 0.1 us)
Async XLA Ops:
  3.9 4.7 %collective-permute-start.2 = (bf16[24,512]{1,0:T(8,128)(2,1)S(1)}, bf16[24,512]{1,0:T(8,128)(2,1)S(1)}, u32[]{:S(2)}, u32[]{:S(2)}) collective-permute-start(bf16[24,512]{1,0:T(8,128)(2,1)S(1)} %get-tuple-element.14.own_ref), channel_id=1, source_target_pairs={{0,3},{1,0},{2,1},{3,2},{4,7},{5,4},{6,5},{7,6},{8,11},{9,8},{10,9... | collective-permute-start | bytes 73736 | tf_op jit(solution)/shard_map/ppermute | solution.py:290
  7.6 4.2 %collective-permute-start.1 = (bf16[24,512]{1,0:T(8,128)(2,1)S(1)}, bf16[24,512]{1,0:T(8,128)(2,1)S(1)}, u32[]{:S(2)}, u32[]{:S(2)}) collective-permute-start(bf16[24,512]{1,0:T(8,128)(2,1)S(1)} %get-tuple-element.14.own_ref), channel_id=1, source_target_pairs={{0,2},{1,3},{2,0},{3,1},{4,6},{5,7},{6,4},{7,5},{8,10},{9,11},{10,... | collective-permute-start | bytes 73736 | tf_op jit(solution)/shard_map/ppermute | solution.py:290
  7.9 4.1 %collective-permute-start = (bf16[24,512]{1,0:T(8,128)(2,1)S(1)}, bf16[24,512]{1,0:T(8,128)(2,1)S(1)}, u32[]{:S(2)}, u32[]{:S(2)}) collective-permute-start(bf16[24,512]{1,0:T(8,128)(2,1)S(1)} %get-tuple-element.14.own_ref), channel_id=1, source_target_pairs={{0,1},{1,2},{2,3},{3,0},{4,5},{5,6},{6,7},{7,4},{8,9},{9,10},{10,1... | collective-permute-start | bytes 73736 | tf_op jit(solution)/shard_map/ppermute | solution.py:290
  13.4 4.7 %collective-permute-start.3 = (bf16[1536,128]{1,0:T(8,128)(2,1)S(1)}, bf16[1536,128]{1,0:T(8,128)(2,1)S(1)}, u32[]{:S(2)}, u32[]{:S(2)}) collective-permute-start(bf16[1536,128]{1,0:T(8,128)(2,1)S(1)} %get-tuple-element.19), channel_id=1, source_target_pairs={{0,4},{1,5},{2,6},{3,7},{8,12},{9,13},{10,14},{11,15},{16,20},{17,... | collective-permute-start | bytes 1179656 | tf_op jit(solution)/shard_map/ppermute | solution.py:357
  18.2 9.4 %collective-permute-start.6 = (bf16[384,128]{1,0:T(8,128)(2,1)S(1)}, bf16[384,128]{1,0:T(8,128)(2,1)S(1)}, u32[]{:S(2)}, u32[]{:S(2)}) collective-permute-start(bf16[384,128]{1,0:T(8,128)(2,1)S(1)} %get-tuple-element.24), channel_id=1, source_target_pairs={{4,196},{68,4},{132,68},{196,132},{5,197},{69,5},{133,69},{197,133... | collective-permute-start | bytes 294920 | tf_op jit(solution)/shard_map/ppermute | solution.py:297
  22.6 6.9 %collective-permute-start.5 = (bf16[384,128]{1,0:T(8,128)(2,1)S(1)}, bf16[384,128]{1,0:T(8,128)(2,1)S(1)}, u32[]{:S(2)}, u32[]{:S(2)}) collective-permute-start(bf16[384,128]{1,0:T(8,128)(2,1)S(1)} %get-tuple-element.25), channel_id=1, source_target_pairs={{4,132},{68,196},{132,4},{196,68},{5,133},{69,197},{133,5},{197,69... | collective-permute-start | bytes 294920 | tf_op jit(solution)/shard_map/ppermute | solution.py:297
  25.1 6.6 %collective-permute-start.4 = (bf16[384,128]{1,0:T(8,128)(2,1)S(1)}, bf16[384,128]{1,0:T(8,128)(2,1)S(1)}, u32[]{:S(2)}, u32[]{:S(2)}) collective-permute-start(bf16[384,128]{1,0:T(8,128)(2,1)S(1)} %get-tuple-element.26), channel_id=1, source_target_pairs={{4,68},{68,132},{132,196},{196,4},{5,69},{69,133},{133,197},{197,5... | collective-permute-start | bytes 294920 | tf_op jit(solution)/shard_map/ppermute | solution.py:297
  62.0 2.6 %collective-permute-start.7 = (bf16[16,96,128]{2,1,0:T(8,128)(2,1)S(1)}, bf16[16,96,128]{2,1,0:T(8,128)(2,1)S(1)}, u32[]{:S(2)}, u32[]{:S(2)}) collective-permute-start(bf16[16,96,128]{2,1,0:T(8,128)(2,1)S(1)} %all_to_all.11.own_ref), channel_id=1, source_target_pairs={{4,0},{5,1},{6,2},{7,3},{12,8},{13,9},{14,10},{15,11},{20,16},{21,... | collective-permute-start | bytes 1179656 | tf_op jit(solution)/shard_map/ppermute | solution.py:378

commit v4 on v2

--- a/solution.py
+++ b/solution.py
@@ -172,7 +172,7 @@
 
 def expand_kernel(
     own_ref, one_ref, two_ref, three_ref, blocks, keep_mask, pick_mask, keep_ref, send_ref,
-    coupling_ref, spread, left, coulomb, main, rest, scaled_eye,
+    coupling_ref, spread, left, coulomb, main, rest, staged,
 ):
     here = lax.axis_index("pair")
     core = lax.axis_index("core")
@@ -199,24 +199,17 @@
     tail = left[pl.ds(4 * BW, PAIRS - 4 * BW), :]
     main[...] = nt(folded, columns)
     rest[...] = nt(folded, jnp.concatenate([tail, tail], axis=0))
-    eye = (lanes((BW, BW)) == sublanes((BW, BW))).astype(F32)
-    for p in range(ROWS):
-        factor = jnp.broadcast_to(coupling_ref[pl.ds(p, 1), :], (BW, BW))
-        scaled_eye[pl.ds(p * BW, BW), :] = (eye * factor).astype(BF16)
-    joined = jnp.concatenate(
-        [jnp.concatenate([blocks[g, p] for p in range(ROWS)], axis=1) for g in (0, 1, 2)], axis=0
-    )
-    coulomb[pl.ds(0 * BW, 3 * BW), :] = jnp.dot(
-        joined, scaled_eye[...], preferred_element_type=F32
-    )
-    for g in (3,):
+    def one(g, carry):
         total_g = jnp.zeros((BW, BW), F32)
         for p in range(ROWS):
             factor = jnp.broadcast_to(coupling_ref[pl.ds(p, 1), :], (BW, BW))
             total_g = total_g + blocks[g, p].astype(F32) * factor
-        coulomb[pl.ds(g * BW, BW), :] = total_g
+        coulomb[pl.ds(pl.multiple_of(g * BW, BW), BW), :] = total_g
+        return carry
+
+    lax.fori_loop(0, SLOTS, one, 0)
     low_lane = lanes((NZ, BW)) < BW // 2
-    for ref, which in ((keep_ref, core), (send_ref, 1 - core)):
+    for ref, which in ((staged, 1 - core), (keep_ref, core)):
         for step in range(NX):
             x = lax.rem(along + step, NX)
             base = step * NZ * MSG
@@ -232,6 +225,7 @@
                     other = rest[pl.ds(first + 7 + s, NZ, stride=18), :]
                     value = jnp.where(low_lane, value, other)
                 ref[pl.ds(base + 17 + s, NZ, stride=MSG), :] = value
+    send_ref[...] = staged[...].astype(BF16)
 
 
 def along_x_kernel(own_ref, one_ref, two_ref, three_ref, out_ref):
@@ -321,7 +315,7 @@
     rows = CHIPS * MSG
     keep, send = pl.pallas_call(
         expand_kernel,
-        out_shape=[pltpu.VMEM((rows, BW), F32)] * 2,
+        out_shape=[pltpu.VMEM((rows, BW), F32), pltpu.VMEM((rows, BW), BF16)],
         in_specs=[VMEM] * 7,
         out_specs=[VMEM, VMEM],
         scratch_shapes=[
@@ -331,13 +325,13 @@
             pltpu.VMEM((SLOTS * BW, BW), F32),
             pltpu.VMEM((PAIRS, BW), F32),
             pltpu.VMEM((PAIRS, BW), F32),
-            pltpu.VMEM((ROWS * BW, BW), BF16),
+            pltpu.VMEM((rows, BW), F32),
         ],
         compiler_params=limit(8192),
         name="expand",
     )(message, one, two, three, blocks, keep_mask, pick_mask)
     swap = [(0, 1), (1, 0)]
-    chip_sum = (keep + lax.ppermute(send, "core", swap)).reshape(NX, NZ * MSG, BW)
+    chip_sum = (keep + lax.ppermute(send, "core", swap).astype(F32)).reshape(NX, NZ * MSG, BW)
     one, two, three = from_others(chip_sum.astype(BF16), "x")
     pieces = pl.pallas_call(
         along_x_kernel,

time: 58.8 us -> 58.3 us (level)
  no operation moved by 1% of the time
where the time goes in v4:
time: 58.3 us; the launch traced here: 58.2 us
  blocking collectives  27.3 us (47%)
  starting transfers between devices  15 us (26%)
  waiting for transfers between devices  9.38 us (16%)
  Pallas kernels  5.8 us (10%)
  between operations  0.68 us (1%)
    all_to_all x1, blocking collectives, shards(): along_z = lax.all_to_all(pieces, 'z', 0, 0, tiled=True)  16.4 us
    all_to_all x1, blocking collectives, shards(): received = lax.all_to_all(pieces, ('pair', 'x'), 0, 0, tiled=True)  10.9 us
    ppermute x6, starting transfers between devices, from_others(): lax.ppermute(x if axis == 'pair' else x[s], axis, [(i, (i + s) % 4) for i...  8.35 us
    ppermute x6, waiting for transfers between devices, from_others(): lax.ppermute(x if axis == 'pair' else x[s], axis, [(i, (i + s) % 4) for i...  7.24 us
    ppermute x1, starting transfers between devices, shards(): partner = lax.ppermute(received, 'core', swap)  4.37 us
    pallas_call x1, Pallas kernels, shards(): pl.pallas_call(contract_kernel, out_shape=[pltpu.VMEM((ACT, GROUPS * BW),...  3.29 us
    ppermute x1, starting transfers between devices, shards(): lax.ppermute(send, 'core', swap).astype(F32)  2.27 us
    pallas_call x1, Pallas kernels, shards(): pl.pallas_call(expand_kernel, out_shape=[pltpu.VMEM((rows, BW), F32), plt...  1.33 us
  transfers between devices with their start and end apart: 8, of which 6 were waited for; matrix products, arithmetic and copies ran while one was open for 0% of the time, Pallas kernels for 0%

profile of v4, /device:TPU:1, one launch (start us, length us, event | category | flops | bytes accessed | tf_op | source)
XLA Modules:
  0.0 58.2 jit_solution(17780506446751589922)
XLA Ops:
  0.6 3.3 %contract.1 = (bf16[24,512]{1,0:T(8,128)(2,1)S(1)}, bf16[4,20,128,128]{3,2,1,0:T(8,128)(2,1)S(1)}, bf16[128,128]{1,0:T(8,128)(2,1)S(1)}, bf16[128,128]{1,0:T(8,1...) custom-call(s32[16]{0:T(128)} %mask_hbm.1, s32[16]{0:T(128)} %owner_hbm.1, s32[2,16]{1,0:T(2,128)} %index_hbm.1, ...), custom_call_target="tpu_custom_call" | custom-call | tf_op jit(solution)/shard_map/contract/pallas_call | solution.py:287
  3.9 3.6 %collective-permute-start.2 = (bf16[24,512]{1,0:T(8,128)(2,1)S(1)}, bf16[24,512]{1,0:T(8,128)(2,1)S(1)}, u32[]{:S(2)}, u32[]{:S(2)}) collective-permute-start(bf16[24,512]{1,0:T(8,128)(2,1)S(1)} %get-tuple-element.14.own_ref), channel_id=1, source_target_pairs={{0,3},{1,0},{2,1},{3,2},{4,7},{5,4},{6,5},{7,6},{8,11},{9,8},{10,9... | collective-permute-start | bytes 73736 | tf_op jit(solution)/shard_map/ppermute | solution.py:276
  7.6 0.4 collective-permute-start.1
  7.9 0.7 %collective-permute-start = (bf16[24,512]{1,0:T(8,128)(2,1)S(1)}, bf16[24,512]{1,0:T(8,128)(2,1)S(1)}, u32[]{:S(2)}, u32[]{:S(2)}) collective-permute-start(bf16[24,512]{1,0:T(8,128)(2,1)S(1)} %get-tuple-element.14.own_ref), channel_id=1, source_target_pairs={{0,1},{1,2},{2,3},{3,0},{4,5},{5,6},{6,7},{7,4},{8,9},{9,10},{10,1... | collective-permute-start | bytes 73736 | tf_op jit(solution)/shard_map/ppermute | solution.py:276
  8.6 0.0 collective-permute-done.2.three_ref
  8.6 3.2 %collective-permute-done.1.two_ref = bf16[24,512]{1,0:T(8,128)(2,1)S(1)} collective-permute-done((bf16[24,512]{1,0:T(8,128)(2,1)S(1)}, bf16[24,512]{1,0:T(8,128)(2,1)S(1)}, u32[]{:S(2)}, u32[]{:S(2)}) %collective-permute-start.1) | collective-permute-done | bytes 24608 | tf_op jit(solution)/shard_map/ppermute | solution.py:276
  11.8 0.2 collective-permute-done.one_ref
  12.0 1.3 %expand.1 = (f32[768,128]{1,0:T(8,128)S(1)}, bf16[768,128]{1,0:T(8,128)(2,1)S(1)}) custom-call(bf16[24,512]{1,0:T(8,128)(2,1)S(1)} %get-tuple-element.14.own_ref, bf16[24,512]{1,0:T(8,128)(2,1)S(1)} %collective-permute-done.one_ref, bf16[24,512]{1,0:T(8,128)(2,1)S(1)} %collective-permute-done.1.two_ref, ...), custom_call_target="tpu_custom_call" | custom-call | tf_op jit(solution)/shard_map/expand/pallas_call | solution.py:316
  13.3 2.3 %collective-permute-start.3 = (bf16[768,128]{1,0:T(8,128)(2,1)S(1)}, bf16[768,128]{1,0:T(8,128)(2,1)S(1)}, u32[]{:S(2)}, u32[]{:S(2)}) collective-permute-start(bf16[768,128]{1,0:T(8,128)(2,1)S(1)} %get-tuple-element.19), channel_id=1, source_target_pairs={{0,4},{4,0},{1,5},{5,1},{2,6},{6,2},{3,7},{7,3},{8,12},{12,8},{9,1... | collective-permute-start | bytes 589832 | tf_op jit(solution)/shard_map/ppermute | solution.py:334
  15.6 1.1 %collective-permute-done.3 = bf16[768,128]{1,0:T(8,128)(2,1)S(1)} collective-permute-done((bf16[768,128]{1,0:T(8,128)(2,1)S(1)}, bf16[768,128]{1,0:T(8,128)(2,1)S(1)}, u32[]{:S(2)}, u32[]{:S(2)}) %collective-permute-start.3) | collective-permute-done | bytes 196640 | tf_op jit(solution)/shard_map/ppermute | solution.py:334
  16.7 0.1 fusion
  16.7 2.6 %collective-permute-start.6 = (bf16[192,128]{1,0:T(8,128)(2,1)S(1)}, bf16[192,128]{1,0:T(8,128)(2,1)S(1)}, u32[]{:S(2)}, u32[]{:S(2)}) collective-permute-start(bf16[192,128]{1,0:T(8,128)(2,1)S(1)} %get-tuple-element.24), channel_id=1, source_target_pairs={{0,192},{64,0},{128,64},{192,128},{1,193},{65,1},{129,65},{193,129... | collective-permute-start | bytes 147464 | tf_op jit(solution)/shard_map/ppermute | solution.py:276
  19.3 0.5 collective-permute-start.5
  19.8 0.6 %collective-permute-start.4 = (bf16[192,128]{1,0:T(8,128)(2,1)S(1)}, bf16[192,128]{1,0:T(8,128)(2,1)S(1)}, u32[]{:S(2)}, u32[]{:S(2)}) collective-permute-start(bf16[192,128]{1,0:T(8,128)(2,1)S(1)} %get-tuple-element.26), channel_id=1, source_target_pairs={{0,64},{64,128},{128,192},{192,0},{1,65},{65,129},{129,193},{193,1... | collective-permute-start | bytes 147464 | tf_op jit(solution)/shard_map/ppermute | solution.py:276
  20.4 0.0 collective-permute-done.6.three_ref
  20.5 3.3 %collective-permute-done.5.two_ref = bf16[192,128]{1,0:T(8,128)(2,1)S(1)} collective-permute-done((bf16[192,128]{1,0:T(8,128)(2,1)S(1)}, bf16[192,128]{1,0:T(8,128)(2,1)S(1)}, u32[]{:S(2)}, u32[]{:S(2)}) %collective-permute-start.5) | collective-permute-done | bytes 49184 | tf_op jit(solution)/shard_map/ppermute | solution.py:276
  23.8 0.5 collective-permute-done.4.one_ref
  24.3 16.4 %all_to_all.10.parts_ref = bf16[8,80,128]{2,1,0:T(8,128)(2,1)S(1)} all-to-all(bf16[8,80,128]{2,1,0:T(8,128)(2,1)S(1)} %along_x.1), channel_id=1, replica_groups=mesh['x'=4,'z'=8,'core'=2,'pair'=4] {'z'}, dimensions={0} | all-to-all | bytes 327680 | tf_op jit(solution)/shard_map/all_to_all | solution.py:344
  40.7 0.1 route.1
  40.8 10.9 %all_to_all.11.own_ref = bf16[16,48,128]{2,1,0:T(8,128)(2,1)S(1)} all-to-all(bf16[16,48,128]{2,1,0:T(8,128)(2,1)S(1)} %route.1), channel_id=1, replica_groups=mesh['x'=4,'z'=8,'core'=2,'pair'=4] {'pair','x'}, dimensions={0} | all-to-all | bytes 393216 | tf_op jit(solution)/shard_map/all_to_all | solution.py:353
  51.7 4.4 %collective-permute-start.7 = (bf16[16,48,128]{2,1,0:T(8,128)(2,1)S(1)}, bf16[16,48,128]{2,1,0:T(8,128)(2,1)S(1)}, u32[]{:S(2)}, u32[]{:S(2)}) collective-permute-start(bf16[16,48,128]{2,1,0:T(8,128)(2,1)S(1)} %all_to_all.11.own_ref), channel_id=1, source_target_pairs={{0,4},{4,0},{1,5},{5,1},{2,6},{6,2},{3,7},{7,3},{8,12},{12,8},{9,1... | collective-permute-start | bytes 589832 | tf_op jit(solution)/shard_map/ppermute | solution.py:354
  56.1 1.1 %collective-permute-done.7.other_ref = bf16[16,48,128]{2,1,0:T(8,128)(2,1)S(1)} collective-permute-done((bf16[16,48,128]{2,1,0:T(8,128)(2,1)S(1)}, bf16[16,48,128]{2,1,0:T(8,128)(2,1)S(1)}, u32[]{:S(2)}, u32[]{:S(2)}) %collective-permute-start.7) | collective-permute-done | bytes 196640 | tf_op jit(solution)/shard_map/ppermute | solution.py:354
  57.2 1.0 %place.1 = (f32[1024,128]{1,0:T(8,128)}, f32[9,576]{1,0:T(8,128)}) custom-call(bf16[128,128]{1,0:T(8,128)(2,1)S(1)} %get-tuple-element.12.place_ref, bf16[16,48,128]{2,1,0:T(8,128)(2,1)S(1)} %all_to_all.11.own_ref, bf16[16,48,128]{2,1,0:T(8,128)(2,1)S(1)} %collective-permute-done.7.other_ref), custom_call_target="tpu_custom_call" | custom-call | tf_op jit(solution)/shard_map/place/pallas_call | solution.py:355
  (3 shorter events, 0.0 us)
Async XLA Ops:
  3.9 4.7 %collective-permute-start.2 = (bf16[24,512]{1,0:T(8,128)(2,1)S(1)}, bf16[24,512]{1,0:T(8,128)(2,1)S(1)}, u32[]{:S(2)}, u32[]{:S(2)}) collective-permute-start(bf16[24,512]{1,0:T(8,128)(2,1)S(1)} %get-tuple-element.14.own_ref), channel_id=1, source_target_pairs={{0,3},{1,0},{2,1},{3,2},{4,7},{5,4},{6,5},{7,6},{8,11},{9,8},{10,9... | collective-permute-start | bytes 73736 | tf_op jit(solution)/shard_map/ppermute | solution.py:276
  7.6 4.2 %collective-permute-start.1 = (bf16[24,512]{1,0:T(8,128)(2,1)S(1)}, bf16[24,512]{1,0:T(8,128)(2,1)S(1)}, u32[]{:S(2)}, u32[]{:S(2)}) collective-permute-start(bf16[24,512]{1,0:T(8,128)(2,1)S(1)} %get-tuple-element.14.own_ref), channel_id=1, source_target_pairs={{0,2},{1,3},{2,0},{3,1},{4,6},{5,7},{6,4},{7,5},{8,10},{9,11},{10,... | collective-permute-start | bytes 73736 | tf_op jit(solution)/shard_map/ppermute | solution.py:276
  7.9 4.1 %collective-permute-start = (bf16[24,512]{1,0:T(8,128)(2,1)S(1)}, bf16[24,512]{1,0:T(8,128)(2,1)S(1)}, u32[]{:S(2)}, u32[]{:S(2)}) collective-permute-start(bf16[24,512]{1,0:T(8,128)(2,1)S(1)} %get-tuple-element.14.own_ref), channel_id=1, source_target_pairs={{0,1},{1,2},{2,3},{3,0},{4,5},{5,6},{6,7},{7,4},{8,9},{9,10},{10,1... | collective-permute-start | bytes 73736 | tf_op jit(solution)/shard_map/ppermute | solution.py:276
  13.3 3.3 %collective-permute-start.3 = (bf16[768,128]{1,0:T(8,128)(2,1)S(1)}, bf16[768,128]{1,0:T(8,128)(2,1)S(1)}, u32[]{:S(2)}, u32[]{:S(2)}) collective-permute-start(bf16[768,128]{1,0:T(8,128)(2,1)S(1)} %get-tuple-element.19), channel_id=1, source_target_pairs={{0,4},{4,0},{1,5},{5,1},{2,6},{6,2},{3,7},{7,3},{8,12},{12,8},{9,1... | collective-permute-start | bytes 589832 | tf_op jit(solution)/shard_map/ppermute | solution.py:334
  16.7 3.7 %collective-permute-start.6 = (bf16[192,128]{1,0:T(8,128)(2,1)S(1)}, bf16[192,128]{1,0:T(8,128)(2,1)S(1)}, u32[]{:S(2)}, u32[]{:S(2)}) collective-permute-start(bf16[192,128]{1,0:T(8,128)(2,1)S(1)} %get-tuple-element.24), channel_id=1, source_target_pairs={{0,192},{64,0},{128,64},{192,128},{1,193},{65,1},{129,65},{193,129... | collective-permute-start | bytes 147464 | tf_op jit(solution)/shard_map/ppermute | solution.py:276
  19.3 4.5 %collective-permute-start.5 = (bf16[192,128]{1,0:T(8,128)(2,1)S(1)}, bf16[192,128]{1,0:T(8,128)(2,1)S(1)}, u32[]{:S(2)}, u32[]{:S(2)}) collective-permute-start(bf16[192,128]{1,0:T(8,128)(2,1)S(1)} %get-tuple-element.25), channel_id=1, source_target_pairs={{0,128},{64,192},{128,0},{192,64},{1,129},{65,193},{129,1},{193,65... | collective-permute-start | bytes 147464 | tf_op jit(solution)/shard_map/ppermute | solution.py:276
  19.8 4.4 %collective-permute-start.4 = (bf16[192,128]{1,0:T(8,128)(2,1)S(1)}, bf16[192,128]{1,0:T(8,128)(2,1)S(1)}, u32[]{:S(2)}, u32[]{:S(2)}) collective-permute-start(bf16[192,128]{1,0:T(8,128)(2,1)S(1)} %get-tuple-element.26), channel_id=1, source_target_pairs={{0,64},{64,128},{128,192},{192,0},{1,65},{65,129},{129,193},{193,1... | collective-permute-start | bytes 147464 | tf_op jit(solution)/shard_map/ppermute | solution.py:276
  51.7 5.4 %collective-permute-start.7 = (bf16[16,48,128]{2,1,0:T(8,128)(2,1)S(1)}, bf16[16,48,128]{2,1,0:T(8,128)(2,1)S(1)}, u32[]{:S(2)}, u32[]{:S(2)}) collective-permute-start(bf16[16,48,128]{2,1,0:T(8,128)(2,1)S(1)} %all_to_all.11.own_ref), channel_id=1, source_target_pairs={{0,4},{4,0},{1,5},{5,1},{2,6},{6,2},{3,7},{7,3},{8,12},{12,8},{9,1... | collective-permute-start | bytes 589832 | tf_op jit(solution)/shard_map/ppermute | solution.py:354

commit v5 on v4

--- a/solution.py
+++ b/solution.py
@@ -37,6 +37,28 @@
 
 def nt(a, b):
     return lax.dot_general(a, b, (((1,), (1,)), ((), ())), preferred_element_type=F32)
+
+
+def half_here():
+    z = lax.axis_index("z")
+    x = lax.axis_index("x")
+    flips = jnp.where(z >= NZ // 2, 1, 0) + jnp.where(x >= NX // 2, 1, 0)
+    return lax.rem(lax.axis_index("core") + flips, CORES)
+
+
+def flip_x(x):
+    return x // (NX // 2)
+
+
+def flip_z(z):
+    return z // (NZ // 2)
+
+
+Z_GROUPS = [[z * CORES + (g + flip_z(z)) % CORES for z in range(NZ)] for g in range(CORES)]
+X_GROUPS = [
+    [(q * NX + x) * CORES + (g + flip_x(x)) % CORES for q in range(OWNERS) for x in range(NX)]
+    for g in range(CORES)
+]
 
 
 def lanes(shape):
@@ -175,7 +197,7 @@
     coupling_ref, spread, left, coulomb, main, rest, staged,
 ):
     here = lax.axis_index("pair")
-    core = lax.axis_index("core")
+    core = half_here()
     along = lax.axis_index("x")
     total = (own_ref[...].astype(F32) + two_ref[...].astype(F32)) + (
         one_ref[...].astype(F32) + three_ref[...].astype(F32)
@@ -253,29 +275,46 @@
 
 def place_kernel(place_ref, own_ref, other_ref, fock_ref, gram_ref):
     core = lax.axis_index("core")
+    held = half_here()
     along = lax.axis_index("x")
     table = place_ref[...]
     for n, ref in enumerate((own_ref, other_ref)):
-        which = core if n == 0 else 1 - core
+        which = held if n == 0 else 1 - held
         for x in range(NX):
             pieces = jnp.concatenate([ref[q * NX + x, 0:32, :] for q in range(OWNERS)], axis=0)
             placed = jnp.dot(table, pieces, preferred_element_type=F32)
             for rank in range(8):
                 row = pl.multiple_of(rank * BW + 32 * x + 16 * which, 16)
                 fock_ref[pl.ds(row, 16), :] = placed[16 * rank : 16 * (rank + 1)]
-    for q in range(OWNERS):
-        gram = own_ref[q * NX + along, 32:48, :].astype(F32)
-        gram_ref[:, q * BW : (q + 1) * BW] = gram[0:9]
-        if q == 0:
-            gram_ref[0:7, 4 * BW : PAIRS] = gram[9:16, 0 : BW // 2]
-            gram_ref[7:9, 4 * BW : PAIRS] = gram[9:11, BW // 2 : BW]
-
-
-def from_others(x, axis="pair"):
+    for same, ref in ((True, own_ref), (False, other_ref)):
+
+        @pl.when((held == core) == same)
+        def _(ref=ref):
+            for q in range(OWNERS):
+                gram = ref[q * NX + along, 32:48, :].astype(F32)
+                gram_ref[:, q * BW : (q + 1) * BW] = gram[0:9]
+                if q == 0:
+                    gram_ref[0:7, 4 * BW : PAIRS] = gram[9:16, 0 : BW // 2]
+                    gram_ref[7:9, 4 * BW : PAIRS] = gram[9:11, BW // 2 : BW]
+
+
+def from_others(x):
     return [
-        lax.ppermute(x if axis == "pair" else x[s], axis, [(i, (i + s) % 4) for i in range(4)])
-        for s in range(1, 4)
+        lax.ppermute(x, "pair", [(i, (i + s) % OWNERS) for i in range(OWNERS)])
+        for s in range(1, OWNERS)
     ]
+
+
+def along(pieces):
+    moved = []
+    for s in range(1, NX):
+        pairs = []
+        for x in range(NX):
+            to = (x + s) % NX
+            for c in range(CORES):
+                pairs.append((x * CORES + c, to * CORES + (c + flip_x(x) + flip_x(to)) % CORES))
+        moved.append(lax.ppermute(pieces[s], ("x", "core"), pairs))
+    return moved
 
 
 def shards(three_centre, block_mask, block_owner, block_index, active_orbitals, inactive_orbitals):
@@ -332,7 +371,7 @@
     )(message, one, two, three, blocks, keep_mask, pick_mask)
     swap = [(0, 1), (1, 0)]
     chip_sum = (keep + lax.ppermute(send, "core", swap).astype(F32)).reshape(NX, NZ * MSG, BW)
-    one, two, three = from_others(chip_sum.astype(BF16), "x")
+    one, two, three = along(chip_sum.astype(BF16))
     pieces = pl.pallas_call(
         along_x_kernel,
         out_shape=pltpu.VMEM((NZ, 80, BW), BF16),
@@ -341,7 +380,9 @@
         compiler_params=limit(4096),
         name="along_x",
     )(chip_sum[0], one, two, three)
-    along_z = lax.all_to_all(pieces, "z", 0, 0, tiled=True)
+    along_z = lax.all_to_all(
+        pieces, ("z", "core"), 0, 0, tiled=True, axis_index_groups=Z_GROUPS
+    )
     pieces = pl.pallas_call(
         route_kernel,
         out_shape=pltpu.VMEM((OWNERS * NX, 48, BW), BF16),
@@ -350,7 +391,9 @@
         compiler_params=limit(4096),
         name="route",
     )(routes, along_z)
-    received = lax.all_to_all(pieces, ("pair", "x"), 0, 0, tiled=True)
+    received = lax.all_to_all(
+        pieces, ("pair", "x", "core"), 0, 0, tiled=True, axis_index_groups=X_GROUPS
+    )
     partner = lax.ppermute(received, "core", swap)
     fock, integrals = pl.pallas_call(
         place_kernel,

time: 58.3 us -> 58.5 us (level)
  starting transfers between devices: 15 us -> 11.3 us
  blocking collectives: 27.3 us -> 29.9 us
  waiting for transfers between devices: 9.38 us -> 10.6 us
    ppermute x1, starting transfers between devices: 4.37 us -> 0.11 us  [shards(): partner = lax.ppermute(received, 'core', swap)]
    all_to_all x2, blocking collectives: 27.3 us -> 29.9 us  [the longest x1 18.5 us: shards(): lax.all_to_all(pieces, ('z', 'core'), 0, 0, tiled=True, axis_index_groups...]
    ppermute x6, waiting for transfers between devices: 7.24 us -> 8.17 us  [the longest x3 4.77 us: along(): moved.append(lax.ppermute(pieces[s], ('x', 'core'), pairs))]
where the time goes in v5:
time: 58.5 us; the launch traced here: 58.3 us
  blocking collectives  29.9 us (51%)
  starting transfers between devices  11.3 us (19%)
  waiting for transfers between devices  10.6 us (18%)
  Pallas kernels  5.84 us (10%)
  between operations  0.68 us (1%)
    all_to_all x1, blocking collectives, shards(): lax.all_to_all(pieces, ('z', 'core'), 0, 0, tiled=True, axis_index_groups...  18.5 us
    all_to_all x1, blocking collectives, shards(): lax.all_to_all(pieces, ('pair', 'x', 'core'), 0, 0, tiled=True, axis_inde...  11.4 us
    ppermute x3, waiting for transfers between devices, along(): moved.append(lax.ppermute(pieces[s], ('x', 'core'), pairs))  4.77 us
    ppermute x3, starting transfers between devices, from_others(): lax.ppermute(x, 'pair', [(i, (i + s) % OWNERS) for i in range(OWNERS)])  4.67 us
    ppermute x3, starting transfers between devices, along(): moved.append(lax.ppermute(pieces[s], ('x', 'core'), pairs))  4.23 us
    ppermute x3, waiting for transfers between devices, from_others(): lax.ppermute(x, 'pair', [(i, (i + s) % OWNERS) for i in range(OWNERS)])  3.4 us
    pallas_call x1, Pallas kernels, shards(): pl.pallas_call(contract_kernel, out_shape=[pltpu.VMEM((ACT, GROUPS * BW),...  3.29 us
    ppermute x1, starting transfers between devices, shards(): lax.ppermute(send, 'core', swap).astype(F32)  2.26 us
  transfers between devices with their start and end apart: 8, of which 6 were waited for; matrix products, arithmetic and copies ran while one was open for 0% of the time, Pallas kernels for 0%

profile of v5, /device:TPU:1, one launch (start us, length us, event | category | flops | bytes accessed | tf_op | source)
XLA Modules:
  0.0 58.3 jit_solution(6705774349062705303)
XLA Ops:
  0.6 3.3 %contract.1 = (bf16[24,512]{1,0:T(8,128)(2,1)S(1)}, bf16[4,20,128,128]{3,2,1,0:T(8,128)(2,1)S(1)}, bf16[128,128]{1,0:T(8,128)(2,1)S(1)}, bf16[128,128]{1,0:T(8,1...) custom-call(s32[16]{0:T(128)} %mask_hbm.1, s32[16]{0:T(128)} %owner_hbm.1, s32[2,16]{1,0:T(2,128)} %index_hbm.1, ...), custom_call_target="tpu_custom_call" | custom-call | tf_op jit(solution)/shard_map/contract/pallas_call | solution.py:326
  3.9 3.6 %collective-permute-start.2 = (bf16[24,512]{1,0:T(8,128)(2,1)S(1)}, bf16[24,512]{1,0:T(8,128)(2,1)S(1)}, u32[]{:S(2)}, u32[]{:S(2)}) collective-permute-start(bf16[24,512]{1,0:T(8,128)(2,1)S(1)} %get-tuple-element.14.own_ref), channel_id=1, source_target_pairs={{0,3},{1,0},{2,1},{3,2},{4,7},{5,4},{6,5},{7,6},{8,11},{9,8},{10,9... | collective-permute-start | bytes 73736 | tf_op jit(solution)/shard_map/ppermute | solution.py:303
  7.6 0.4 collective-permute-start.1
  7.9 0.7 %collective-permute-start = (bf16[24,512]{1,0:T(8,128)(2,1)S(1)}, bf16[24,512]{1,0:T(8,128)(2,1)S(1)}, u32[]{:S(2)}, u32[]{:S(2)}) collective-permute-start(bf16[24,512]{1,0:T(8,128)(2,1)S(1)} %get-tuple-element.14.own_ref), channel_id=1, source_target_pairs={{0,1},{1,2},{2,3},{3,0},{4,5},{5,6},{6,7},{7,4},{8,9},{9,10},{10,1... | collective-permute-start | bytes 73736 | tf_op jit(solution)/shard_map/ppermute | solution.py:303
  8.6 0.0 collective-permute-done.2.three_ref
  8.6 3.2 %collective-permute-done.1.two_ref = bf16[24,512]{1,0:T(8,128)(2,1)S(1)} collective-permute-done((bf16[24,512]{1,0:T(8,128)(2,1)S(1)}, bf16[24,512]{1,0:T(8,128)(2,1)S(1)}, u32[]{:S(2)}, u32[]{:S(2)}) %collective-permute-start.1) | collective-permute-done | bytes 24608 | tf_op jit(solution)/shard_map/ppermute | solution.py:303
  11.8 0.2 collective-permute-done.one_ref
  12.0 1.3 %expand.1 = (f32[768,128]{1,0:T(8,128)S(1)}, bf16[768,128]{1,0:T(8,128)(2,1)S(1)}) custom-call(bf16[24,512]{1,0:T(8,128)(2,1)S(1)} %get-tuple-element.14.own_ref, bf16[24,512]{1,0:T(8,128)(2,1)S(1)} %collective-permute-done.one_ref, bf16[24,512]{1,0:T(8,128)(2,1)S(1)} %collective-permute-done.1.two_ref, ...), custom_call_target="tpu_custom_call" | custom-call | tf_op jit(solution)/shard_map/expand/pallas_call | solution.py:355
  13.3 2.3 %collective-permute-start.3 = (bf16[768,128]{1,0:T(8,128)(2,1)S(1)}, bf16[768,128]{1,0:T(8,128)(2,1)S(1)}, u32[]{:S(2)}, u32[]{:S(2)}) collective-permute-start(bf16[768,128]{1,0:T(8,128)(2,1)S(1)} %get-tuple-element.19), channel_id=1, source_target_pairs={{0,4},{4,0},{1,5},{5,1},{2,6},{6,2},{3,7},{7,3},{8,12},{12,8},{9,1... | collective-permute-start | bytes 589832 | tf_op jit(solution)/shard_map/ppermute | solution.py:373
  15.6 1.1 %collective-permute-done.3 = bf16[768,128]{1,0:T(8,128)(2,1)S(1)} collective-permute-done((bf16[768,128]{1,0:T(8,128)(2,1)S(1)}, bf16[768,128]{1,0:T(8,128)(2,1)S(1)}, u32[]{:S(2)}, u32[]{:S(2)}) %collective-permute-start.3) | collective-permute-done | bytes 196640 | tf_op jit(solution)/shard_map/ppermute | solution.py:373
  16.7 0.1 fusion
  16.7 2.8 %collective-permute-start.6 = (bf16[192,128]{1,0:T(8,128)(2,1)S(1)}, bf16[192,128]{1,0:T(8,128)(2,1)S(1)}, u32[]{:S(2)}, u32[]{:S(2)}) collective-permute-start(bf16[192,128]{1,0:T(8,128)(2,1)S(1)} %get-tuple-element.24), channel_id=1, source_target_pairs={{0,196},{4,192},{64,0},{68,4},{128,68},{132,64},{192,128},{196,132... | collective-permute-start | bytes 147464 | tf_op jit(solution)/shard_map/ppermute | solution.py:316
  19.6 0.5 collective-permute-start.5
  20.1 0.9 %collective-permute-start.4 = (bf16[192,128]{1,0:T(8,128)(2,1)S(1)}, bf16[192,128]{1,0:T(8,128)(2,1)S(1)}, u32[]{:S(2)}, u32[]{:S(2)}) collective-permute-start(bf16[192,128]{1,0:T(8,128)(2,1)S(1)} %get-tuple-element.26), channel_id=1, source_target_pairs={{0,64},{4,68},{64,132},{68,128},{128,192},{132,196},{192,4},{196,0... | collective-permute-start | bytes 147464 | tf_op jit(solution)/shard_map/ppermute | solution.py:316
  21.0 0.0 collective-permute-done.6.three_ref
  21.0 4.1 %collective-permute-done.5.two_ref = bf16[192,128]{1,0:T(8,128)(2,1)S(1)} collective-permute-done((bf16[192,128]{1,0:T(8,128)(2,1)S(1)}, bf16[192,128]{1,0:T(8,128)(2,1)S(1)}, u32[]{:S(2)}, u32[]{:S(2)}) %collective-permute-start.5) | collective-permute-done | bytes 49184 | tf_op jit(solution)/shard_map/ppermute | solution.py:316
  25.1 0.7 %collective-permute-done.4.one_ref = bf16[192,128]{1,0:T(8,128)(2,1)S(1)} collective-permute-done((bf16[192,128]{1,0:T(8,128)(2,1)S(1)}, bf16[192,128]{1,0:T(8,128)(2,1)S(1)}, u32[]{:S(2)}, u32[]{:S(2)}) %collective-permute-start.4) | collective-permute-done | bytes 49184 | tf_op jit(solution)/shard_map/ppermute | solution.py:316
  25.8 18.5 %all_to_all.10.parts_ref = bf16[8,80,128]{2,1,0:T(8,128)(2,1)S(1)} all-to-all(bf16[8,80,128]{2,1,0:T(8,128)(2,1)S(1)} %along_x.1), channel_id=1, replica_groups={{0,8,16,24,36,44,52,60},{4,12,20,28,32,40,48,56},{1,9,17,25,37,45,53,61..., dimensions={0} | all-to-all | bytes 327680 | tf_op jit(solution)/shard_map/all_to_all | solution.py:383
  44.3 0.1 route.1
  44.4 11.4 %all_to_all.11.own_ref = bf16[16,48,128]{2,1,0:T(8,128)(2,1)S(1)} all-to-all(bf16[16,48,128]{2,1,0:T(8,128)(2,1)S(1)} %route.1), channel_id=1, replica_groups={{0,64,132,196,1,65,133,197,2,66,134,198,3,67,135,199},{4,68,128,192,5,6..., dimensions={0} | all-to-all | bytes 393216 | tf_op jit(solution)/shard_map/all_to_all | solution.py:394
  55.8 0.1 collective-permute-start.7
  55.9 1.3 %collective-permute-done.7.other_ref = bf16[16,48,128]{2,1,0:T(8,128)(2,1)S(1)} collective-permute-done((bf16[16,48,128]{2,1,0:T(8,128)(2,1)S(1)}, bf16[16,48,128]{2,1,0:T(8,128)(2,1)S(1)}, u32[]{:S(2)}, u32[]{:S(2)}) %collective-permute-start.7) | collective-permute-done | bytes 196640 | tf_op jit(solution)/shard_map/ppermute | solution.py:397
  57.3 1.1 %place.1 = (f32[1024,128]{1,0:T(8,128)}, f32[9,576]{1,0:T(8,128)}) custom-call(bf16[128,128]{1,0:T(8,128)(2,1)S(1)} %get-tuple-element.12.place_ref, bf16[16,48,128]{2,1,0:T(8,128)(2,1)S(1)} %all_to_all.11.own_ref, bf16[16,48,128]{2,1,0:T(8,128)(2,1)S(1)} %collective-permute-done.7.other_ref), custom_call_target="tpu_custom_call" | custom-call | tf_op jit(solution)/shard_map/place/pallas_call | solution.py:398
  (3 shorter events, 0.0 us)
Async XLA Ops:
  3.9 4.7 %collective-permute-start.2 = (bf16[24,512]{1,0:T(8,128)(2,1)S(1)}, bf16[24,512]{1,0:T(8,128)(2,1)S(1)}, u32[]{:S(2)}, u32[]{:S(2)}) collective-permute-start(bf16[24,512]{1,0:T(8,128)(2,1)S(1)} %get-tuple-element.14.own_ref), channel_id=1, source_target_pairs={{0,3},{1,0},{2,1},{3,2},{4,7},{5,4},{6,5},{7,6},{8,11},{9,8},{10,9... | collective-permute-start | bytes 73736 | tf_op jit(solution)/shard_map/ppermute | solution.py:303
  7.6 4.2 %collective-permute-start.1 = (bf16[24,512]{1,0:T(8,128)(2,1)S(1)}, bf16[24,512]{1,0:T(8,128)(2,1)S(1)}, u32[]{:S(2)}, u32[]{:S(2)}) collective-permute-start(bf16[24,512]{1,0:T(8,128)(2,1)S(1)} %get-tuple-element.14.own_ref), channel_id=1, source_target_pairs={{0,2},{1,3},{2,0},{3,1},{4,6},{5,7},{6,4},{7,5},{8,10},{9,11},{10,... | collective-permute-start | bytes 73736 | tf_op jit(solution)/shard_map/ppermute | solution.py:303
  7.9 4.1 %collective-permute-start = (bf16[24,512]{1,0:T(8,128)(2,1)S(1)}, bf16[24,512]{1,0:T(8,128)(2,1)S(1)}, u32[]{:S(2)}, u32[]{:S(2)}) collective-permute-start(bf16[24,512]{1,0:T(8,128)(2,1)S(1)} %get-tuple-element.14.own_ref), channel_id=1, source_target_pairs={{0,1},{1,2},{2,3},{3,0},{4,5},{5,6},{6,7},{7,4},{8,9},{9,10},{10,1... | collective-permute-start | bytes 73736 | tf_op jit(solution)/shard_map/ppermute | solution.py:303
  13.3 3.3 %collective-permute-start.3 = (bf16[768,128]{1,0:T(8,128)(2,1)S(1)}, bf16[768,128]{1,0:T(8,128)(2,1)S(1)}, u32[]{:S(2)}, u32[]{:S(2)}) collective-permute-start(bf16[768,128]{1,0:T(8,128)(2,1)S(1)} %get-tuple-element.19), channel_id=1, source_target_pairs={{0,4},{4,0},{1,5},{5,1},{2,6},{6,2},{3,7},{7,3},{8,12},{12,8},{9,1... | collective-permute-start | bytes 589832 | tf_op jit(solution)/shard_map/ppermute | solution.py:373
  16.7 4.2 %collective-permute-start.6 = (bf16[192,128]{1,0:T(8,128)(2,1)S(1)}, bf16[192,128]{1,0:T(8,128)(2,1)S(1)}, u32[]{:S(2)}, u32[]{:S(2)}) collective-permute-start(bf16[192,128]{1,0:T(8,128)(2,1)S(1)} %get-tuple-element.24), channel_id=1, source_target_pairs={{0,196},{4,192},{64,0},{68,4},{128,68},{132,64},{192,128},{196,132... | collective-permute-start | bytes 147464 | tf_op jit(solution)/shard_map/ppermute | solution.py:316
  19.6 5.5 %collective-permute-start.5 = (bf16[192,128]{1,0:T(8,128)(2,1)S(1)}, bf16[192,128]{1,0:T(8,128)(2,1)S(1)}, u32[]{:S(2)}, u32[]{:S(2)}) collective-permute-start(bf16[192,128]{1,0:T(8,128)(2,1)S(1)} %get-tuple-element.25), channel_id=1, source_target_pairs={{0,132},{4,128},{64,196},{68,192},{128,4},{132,0},{192,68},{196,64... | collective-permute-start | bytes 147464 | tf_op jit(solution)/shard_map/ppermute | solution.py:316
  20.1 5.7 %collective-permute-start.4 = (bf16[192,128]{1,0:T(8,128)(2,1)S(1)}, bf16[192,128]{1,0:T(8,128)(2,1)S(1)}, u32[]{:S(2)}, u32[]{:S(2)}) collective-permute-start(bf16[192,128]{1,0:T(8,128)(2,1)S(1)} %get-tuple-element.26), channel_id=1, source_target_pairs={{0,64},{4,68},{64,132},{68,128},{128,192},{132,196},{192,4},{196,0... | collective-permute-start | bytes 147464 | tf_op jit(solution)/shard_map/ppermute | solution.py:316
  55.8 1.4 %collective-permute-start.7 = (bf16[16,48,128]{2,1,0:T(8,128)(2,1)S(1)}, bf16[16,48,128]{2,1,0:T(8,128)(2,1)S(1)}, u32[]{:S(2)}, u32[]{:S(2)}) collective-permute-start(bf16[16,48,128]{2,1,0:T(8,128)(2,1)S(1)} %all_to_all.11.own_ref), channel_id=1, source_target_pairs={{0,4},{4,0},{1,5},{5,1},{2,6},{6,2},{3,7},{7,3},{8,12},{12,8},{9,1... | collective-permute-start | bytes 589832 | tf_op jit(solution)/shard_map/ppermute | solution.py:397

commit v6 on v5

--- a/solution.py
+++ b/solution.py
@@ -40,9 +40,7 @@
 
 
 def half_here():
-    z = lax.axis_index("z")
-    x = lax.axis_index("x")
-    flips = jnp.where(z >= NZ // 2, 1, 0) + jnp.where(x >= NX // 2, 1, 0)
+    flips = jnp.where(lax.axis_index("x") >= NX // 2, 1, 0)
     return lax.rem(lax.axis_index("core") + flips, CORES)
 
 
@@ -50,11 +48,6 @@
     return x // (NX // 2)
 
 
-def flip_z(z):
-    return z // (NZ // 2)
-
-
-Z_GROUPS = [[z * CORES + (g + flip_z(z)) % CORES for z in range(NZ)] for g in range(CORES)]
 X_GROUPS = [
     [(q * NX + x) * CORES + (g + flip_x(x)) % CORES for q in range(OWNERS) for x in range(NX)]
     for g in range(CORES)
@@ -273,7 +266,7 @@
             out_ref[o * NX + x, 32:48, :] = gram
 
 
-def place_kernel(place_ref, own_ref, other_ref, fock_ref, gram_ref):
+def place_kernel(place_ref, own_ref, other_ref, fock_out, gram_ref, fock_ref, out_sem):
     core = lax.axis_index("core")
     held = half_here()
     along = lax.axis_index("x")
@@ -286,6 +279,12 @@
             for rank in range(8):
                 row = pl.multiple_of(rank * BW + 32 * x + 16 * which, 16)
                 fock_ref[pl.ds(row, 16), :] = placed[16 * rank : 16 * (rank + 1)]
+    copies = [
+        pltpu.make_async_copy(
+            fock_ref.at[pl.ds(rank * BW, BW)], fock_out.at[pl.ds(rank * BW, BW)], out_sem.at[rank]
+        )
+        for rank in range(8)
+    ]
     for same, ref in ((True, own_ref), (False, other_ref)):
 
         @pl.when((held == core) == same)
@@ -296,6 +295,10 @@
                 if q == 0:
                     gram_ref[0:7, 4 * BW : PAIRS] = gram[9:16, 0 : BW // 2]
                     gram_ref[7:9, 4 * BW : PAIRS] = gram[9:11, BW // 2 : BW]
+    for rank, c in enumerate(copies):
+        c.start(priority=rank % 2)
+    for c in copies:
+        c.wait()
 
 
 def from_others(x):
@@ -380,9 +383,7 @@
         compiler_params=limit(4096),
         name="along_x",
     )(chip_sum[0], one, two, three)
-    along_z = lax.all_to_all(
-        pieces, ("z", "core"), 0, 0, tiled=True, axis_index_groups=Z_GROUPS
-    )
+    along_z = lax.all_to_all(pieces, "z", 0, 0, tiled=True)
     pieces = pl.pallas_call(
         route_kernel,
         out_shape=pltpu.VMEM((OWNERS * NX, 48, BW), BF16),
@@ -402,7 +403,8 @@
             jax.ShapeDtypeStruct((9, PAIRS), F32),
         ],
         in_specs=[VMEM] * 3,
-        out_specs=[VMEM, VMEM],
+        out_specs=[HBM, VMEM],
+        scratch_shapes=[pltpu.VMEM((8 * BW, BW), F32), dma((8,))],
         compiler_params=limit(4096),
         name="place",
     )(places, received, partner)

time: 58.5 us -> 59 us (level)
  Pallas kernels: 5.84 us -> 6.51 us
    all_to_all x1, blocking collectives: 18.5 us -> 16.6 us  [shards(): along_z = lax.all_to_all(pieces, 'z', 0, 0, tiled=True)]
    all_to_all x1, blocking collectives: 11.4 us -> 13.1 us  [shards(): lax.all_to_all(pieces, ('pair', 'x', 'core'), 0, 0, tiled=True, axis_inde...]
    pallas_call x1, Pallas kernels: 1.06 us -> 1.72 us  [shards(): pl.pallas_call(place_kernel, out_shape=[jax.ShapeDtypeStruct((8 * BW, BW)...]
where the time goes in v6:
time: 59 us; the launch traced here: 58.8 us
  blocking collectives  29.7 us (50%)
  starting transfers between devices  11.2 us (19%)
  waiting for transfers between devices  10.6 us (18%)
  Pallas kernels  6.51 us (11%)
  between operations  0.68 us (1%)
    all_to_all x1, blocking collectives, shards(): along_z = lax.all_to_all(pieces, 'z', 0, 0, tiled=True)  16.6 us
    all_to_all x1, blocking collectives, shards(): lax.all_to_all(pieces, ('pair', 'x', 'core'), 0, 0, tiled=True, axis_inde...  13.1 us
    ppermute x3, waiting for transfers between devices, along(): moved.append(lax.ppermute(pieces[s], ('x', 'core'), pairs))  4.77 us
    ppermute x3, starting transfers between devices, from_others(): lax.ppermute(x, 'pair', [(i, (i + s) % OWNERS) for i in range(OWNERS)])  4.67 us
    ppermute x3, starting transfers between devices, along(): moved.append(lax.ppermute(pieces[s], ('x', 'core'), pairs))  4.23 us
    ppermute x3, waiting for transfers between devices, from_others(): lax.ppermute(x, 'pair', [(i, (i + s) % OWNERS) for i in range(OWNERS)])  3.4 us
    pallas_call x1, Pallas kernels, shards(): pl.pallas_call(contract_kernel, out_shape=[pltpu.VMEM((ACT, GROUPS * BW),...  3.29 us
    ppermute x1, starting transfers between devices, shards(): lax.ppermute(send, 'core', swap).astype(F32)  2.27 us
  transfers between devices with their start and end apart: 8, of which 6 were waited for; matrix products, arithmetic and copies ran while one was open for 0% of the time, Pallas kernels for 0%

profile of v6, /device:TPU:1, one launch (start us, length us, event | category | flops | bytes accessed | tf_op | source)
XLA Modules:
  0.0 58.8 jit_solution(1766317781471151435)
XLA Ops:
  0.6 3.3 %contract.1 = (bf16[24,512]{1,0:T(8,128)(2,1)S(1)}, bf16[4,20,128,128]{3,2,1,0:T(8,128)(2,1)S(1)}, bf16[128,128]{1,0:T(8,128)(2,1)S(1)}, bf16[128,128]{1,0:T(8,1...) custom-call(s32[16]{0:T(128)} %mask_hbm.1, s32[16]{0:T(128)} %owner_hbm.1, s32[2,16]{1,0:T(2,128)} %index_hbm.1, ...), custom_call_target="tpu_custom_call" | custom-call | tf_op jit(solution)/shard_map/contract/pallas_call | solution.py:329
  3.9 3.6 %collective-permute-start.2 = (bf16[24,512]{1,0:T(8,128)(2,1)S(1)}, bf16[24,512]{1,0:T(8,128)(2,1)S(1)}, u32[]{:S(2)}, u32[]{:S(2)}) collective-permute-start(bf16[24,512]{1,0:T(8,128)(2,1)S(1)} %get-tuple-element.14.own_ref), channel_id=1, source_target_pairs={{0,3},{1,0},{2,1},{3,2},{4,7},{5,4},{6,5},{7,6},{8,11},{9,8},{10,9... | collective-permute-start | bytes 73736 | tf_op jit(solution)/shard_map/ppermute | solution.py:306
  7.6 0.4 collective-permute-start.1
  7.9 0.7 %collective-permute-start = (bf16[24,512]{1,0:T(8,128)(2,1)S(1)}, bf16[24,512]{1,0:T(8,128)(2,1)S(1)}, u32[]{:S(2)}, u32[]{:S(2)}) collective-permute-start(bf16[24,512]{1,0:T(8,128)(2,1)S(1)} %get-tuple-element.14.own_ref), channel_id=1, source_target_pairs={{0,1},{1,2},{2,3},{3,0},{4,5},{5,6},{6,7},{7,4},{8,9},{9,10},{10,1... | collective-permute-start | bytes 73736 | tf_op jit(solution)/shard_map/ppermute | solution.py:306
  8.6 0.0 collective-permute-done.2.three_ref
  8.6 3.2 %collective-permute-done.1.two_ref = bf16[24,512]{1,0:T(8,128)(2,1)S(1)} collective-permute-done((bf16[24,512]{1,0:T(8,128)(2,1)S(1)}, bf16[24,512]{1,0:T(8,128)(2,1)S(1)}, u32[]{:S(2)}, u32[]{:S(2)}) %collective-permute-start.1) | collective-permute-done | bytes 24608 | tf_op jit(solution)/shard_map/ppermute | solution.py:306
  11.8 0.2 collective-permute-done.one_ref
  12.0 1.3 %expand.1 = (f32[768,128]{1,0:T(8,128)S(1)}, bf16[768,128]{1,0:T(8,128)(2,1)S(1)}) custom-call(bf16[24,512]{1,0:T(8,128)(2,1)S(1)} %get-tuple-element.14.own_ref, bf16[24,512]{1,0:T(8,128)(2,1)S(1)} %collective-permute-done.one_ref, bf16[24,512]{1,0:T(8,128)(2,1)S(1)} %collective-permute-done.1.two_ref, ...), custom_call_target="tpu_custom_call" | custom-call | tf_op jit(solution)/shard_map/expand/pallas_call | solution.py:358
  13.3 2.3 %collective-permute-start.3 = (bf16[768,128]{1,0:T(8,128)(2,1)S(1)}, bf16[768,128]{1,0:T(8,128)(2,1)S(1)}, u32[]{:S(2)}, u32[]{:S(2)}) collective-permute-start(bf16[768,128]{1,0:T(8,128)(2,1)S(1)} %get-tuple-element.19), channel_id=1, source_target_pairs={{0,4},{4,0},{1,5},{5,1},{2,6},{6,2},{3,7},{7,3},{8,12},{12,8},{9,1... | collective-permute-start | bytes 589832 | tf_op jit(solution)/shard_map/ppermute | solution.py:376
  15.6 1.1 %collective-permute-done.3 = bf16[768,128]{1,0:T(8,128)(2,1)S(1)} collective-permute-done((bf16[768,128]{1,0:T(8,128)(2,1)S(1)}, bf16[768,128]{1,0:T(8,128)(2,1)S(1)}, u32[]{:S(2)}, u32[]{:S(2)}) %collective-permute-start.3) | collective-permute-done | bytes 196640 | tf_op jit(solution)/shard_map/ppermute | solution.py:376
  16.7 0.1 fusion
  16.7 2.8 %collective-permute-start.6 = (bf16[192,128]{1,0:T(8,128)(2,1)S(1)}, bf16[192,128]{1,0:T(8,128)(2,1)S(1)}, u32[]{:S(2)}, u32[]{:S(2)}) collective-permute-start(bf16[192,128]{1,0:T(8,128)(2,1)S(1)} %get-tuple-element.24), channel_id=1, source_target_pairs={{0,196},{4,192},{64,0},{68,4},{128,68},{132,64},{192,128},{196,132... | collective-permute-start | bytes 147464 | tf_op jit(solution)/shard_map/ppermute | solution.py:319
  19.6 0.5 collective-permute-start.5
  20.1 0.9 %collective-permute-start.4 = (bf16[192,128]{1,0:T(8,128)(2,1)S(1)}, bf16[192,128]{1,0:T(8,128)(2,1)S(1)}, u32[]{:S(2)}, u32[]{:S(2)}) collective-permute-start(bf16[192,128]{1,0:T(8,128)(2,1)S(1)} %get-tuple-element.26), channel_id=1, source_target_pairs={{0,64},{4,68},{64,132},{68,128},{128,192},{132,196},{192,4},{196,0... | collective-permute-start | bytes 147464 | tf_op jit(solution)/shard_map/ppermute | solution.py:319
  21.0 0.0 collective-permute-done.6.three_ref
  21.0 4.1 %collective-permute-done.5.two_ref = bf16[192,128]{1,0:T(8,128)(2,1)S(1)} collective-permute-done((bf16[192,128]{1,0:T(8,128)(2,1)S(1)}, bf16[192,128]{1,0:T(8,128)(2,1)S(1)}, u32[]{:S(2)}, u32[]{:S(2)}) %collective-permute-start.5) | collective-permute-done | bytes 49184 | tf_op jit(solution)/shard_map/ppermute | solution.py:319
  25.1 0.7 %collective-permute-done.4.one_ref = bf16[192,128]{1,0:T(8,128)(2,1)S(1)} collective-permute-done((bf16[192,128]{1,0:T(8,128)(2,1)S(1)}, bf16[192,128]{1,0:T(8,128)(2,1)S(1)}, u32[]{:S(2)}, u32[]{:S(2)}) %collective-permute-start.4) | collective-permute-done | bytes 49184 | tf_op jit(solution)/shard_map/ppermute | solution.py:319
  25.8 16.6 %all_to_all.10.parts_ref = bf16[8,80,128]{2,1,0:T(8,128)(2,1)S(1)} all-to-all(bf16[8,80,128]{2,1,0:T(8,128)(2,1)S(1)} %along_x.1), channel_id=1, replica_groups=mesh['x'=4,'z'=8,'core'=2,'pair'=4] {'z'}, dimensions={0} | all-to-all | bytes 327680 | tf_op jit(solution)/shard_map/all_to_all | solution.py:386
  42.4 0.1 route.1
  42.6 13.1 %all_to_all.11.own_ref = bf16[16,48,128]{2,1,0:T(8,128)(2,1)S(1)} all-to-all(bf16[16,48,128]{2,1,0:T(8,128)(2,1)S(1)} %route.1), channel_id=1, replica_groups={{0,64,132,196,1,65,133,197,2,66,134,198,3,67,135,199},{4,68,128,192,5,6..., dimensions={0} | all-to-all | bytes 393216 | tf_op jit(solution)/shard_map/all_to_all | solution.py:395
  55.7 0.1 collective-permute-start.7
  55.7 1.4 %collective-permute-done.7.other_ref = bf16[16,48,128]{2,1,0:T(8,128)(2,1)S(1)} collective-permute-done((bf16[16,48,128]{2,1,0:T(8,128)(2,1)S(1)}, bf16[16,48,128]{2,1,0:T(8,128)(2,1)S(1)}, u32[]{:S(2)}, u32[]{:S(2)}) %collective-permute-start.7) | collective-permute-done | bytes 196640 | tf_op jit(solution)/shard_map/ppermute | solution.py:398
  57.1 1.7 %place.1 = (f32[1024,128]{1,0:T(8,128)}, f32[9,576]{1,0:T(8,128)}) custom-call(bf16[128,128]{1,0:T(8,128)(2,1)S(1)} %get-tuple-element.12.place_ref, bf16[16,48,128]{2,1,0:T(8,128)(2,1)S(1)} %all_to_all.11.own_ref, bf16[16,48,128]{2,1,0:T(8,128)(2,1)S(1)} %collective-permute-done.7.other_ref), custom_call_target="tpu_custom_call" | custom-call | tf_op jit(solution)/shard_map/place/pallas_call | solution.py:399
  (3 shorter events, 0.0 us)
Async XLA Ops:
  3.9 4.7 %collective-permute-start.2 = (bf16[24,512]{1,0:T(8,128)(2,1)S(1)}, bf16[24,512]{1,0:T(8,128)(2,1)S(1)}, u32[]{:S(2)}, u32[]{:S(2)}) collective-permute-start(bf16[24,512]{1,0:T(8,128)(2,1)S(1)} %get-tuple-element.14.own_ref), channel_id=1, source_target_pairs={{0,3},{1,0},{2,1},{3,2},{4,7},{5,4},{6,5},{7,6},{8,11},{9,8},{10,9... | collective-permute-start | bytes 73736 | tf_op jit(solution)/shard_map/ppermute | solution.py:306
  7.6 4.2 %collective-permute-start.1 = (bf16[24,512]{1,0:T(8,128)(2,1)S(1)}, bf16[24,512]{1,0:T(8,128)(2,1)S(1)}, u32[]{:S(2)}, u32[]{:S(2)}) collective-permute-start(bf16[24,512]{1,0:T(8,128)(2,1)S(1)} %get-tuple-element.14.own_ref), channel_id=1, source_target_pairs={{0,2},{1,3},{2,0},{3,1},{4,6},{5,7},{6,4},{7,5},{8,10},{9,11},{10,... | collective-permute-start | bytes 73736 | tf_op jit(solution)/shard_map/ppermute | solution.py:306
  7.9 4.1 %collective-permute-start = (bf16[24,512]{1,0:T(8,128)(2,1)S(1)}, bf16[24,512]{1,0:T(8,128)(2,1)S(1)}, u32[]{:S(2)}, u32[]{:S(2)}) collective-permute-start(bf16[24,512]{1,0:T(8,128)(2,1)S(1)} %get-tuple-element.14.own_ref), channel_id=1, source_target_pairs={{0,1},{1,2},{2,3},{3,0},{4,5},{5,6},{6,7},{7,4},{8,9},{9,10},{10,1... | collective-permute-start | bytes 73736 | tf_op jit(solution)/shard_map/ppermute | solution.py:306
  13.3 3.3 %collective-permute-start.3 = (bf16[768,128]{1,0:T(8,128)(2,1)S(1)}, bf16[768,128]{1,0:T(8,128)(2,1)S(1)}, u32[]{:S(2)}, u32[]{:S(2)}) collective-permute-start(bf16[768,128]{1,0:T(8,128)(2,1)S(1)} %get-tuple-element.19), channel_id=1, source_target_pairs={{0,4},{4,0},{1,5},{5,1},{2,6},{6,2},{3,7},{7,3},{8,12},{12,8},{9,1... | collective-permute-start | bytes 589832 | tf_op jit(solution)/shard_map/ppermute | solution.py:376
  16.7 4.2 %collective-permute-start.6 = (bf16[192,128]{1,0:T(8,128)(2,1)S(1)}, bf16[192,128]{1,0:T(8,128)(2,1)S(1)}, u32[]{:S(2)}, u32[]{:S(2)}) collective-permute-start(bf16[192,128]{1,0:T(8,128)(2,1)S(1)} %get-tuple-element.24), channel_id=1, source_target_pairs={{0,196},{4,192},{64,0},{68,4},{128,68},{132,64},{192,128},{196,132... | collective-permute-start | bytes 147464 | tf_op jit(solution)/shard_map/ppermute | solution.py:319
  19.6 5.5 %collective-permute-start.5 = (bf16[192,128]{1,0:T(8,128)(2,1)S(1)}, bf16[192,128]{1,0:T(8,128)(2,1)S(1)}, u32[]{:S(2)}, u32[]{:S(2)}) collective-permute-start(bf16[192,128]{1,0:T(8,128)(2,1)S(1)} %get-tuple-element.25), channel_id=1, source_target_pairs={{0,132},{4,128},{64,196},{68,192},{128,4},{132,0},{192,68},{196,64... | collective-permute-start | bytes 147464 | tf_op jit(solution)/shard_map/ppermute | solution.py:319
  20.1 5.7 %collective-permute-start.4 = (bf16[192,128]{1,0:T(8,128)(2,1)S(1)}, bf16[192,128]{1,0:T(8,128)(2,1)S(1)}, u32[]{:S(2)}, u32[]{:S(2)}) collective-permute-start(bf16[192,128]{1,0:T(8,128)(2,1)S(1)} %get-tuple-element.26), channel_id=1, source_target_pairs={{0,64},{4,68},{64,132},{68,128},{128,192},{132,196},{192,4},{196,0... | collective-permute-start | bytes 147464 | tf_op jit(solution)/shard_map/ppermute | solution.py:319
  55.7 1.4 %collective-permute-start.7 = (bf16[16,48,128]{2,1,0:T(8,128)(2,1)S(1)}, bf16[16,48,128]{2,1,0:T(8,128)(2,1)S(1)}, u32[]{:S(2)}, u32[]{:S(2)}) collective-permute-start(bf16[16,48,128]{2,1,0:T(8,128)(2,1)S(1)} %all_to_all.11.own_ref), channel_id=1, source_target_pairs={{0,4},{4,0},{1,5},{5,1},{2,6},{6,2},{3,7},{7,3},{8,12},{12,8},{9,1... | collective-permute-start | bytes 589832 | tf_op jit(solution)/shard_map/ppermute | solution.py:398

commit v7 on v4

--- a/solution.py
+++ b/solution.py
@@ -171,7 +171,7 @@
 
 
 def expand_kernel(
-    own_ref, one_ref, two_ref, three_ref, blocks, keep_mask, pick_mask, keep_ref, send_ref,
+    own_ref, one_ref, three_ref, two_ref, blocks, keep_mask, pick_mask, keep_ref, send_ref,
     coupling_ref, spread, left, coulomb, main, rest, staged,
 ):
     here = lax.axis_index("pair")
@@ -228,7 +228,7 @@
     send_ref[...] = staged[...].astype(BF16)
 
 
-def along_x_kernel(own_ref, one_ref, two_ref, three_ref, out_ref):
+def along_x_kernel(own_ref, one_ref, three_ref, two_ref, out_ref):
     total = own_ref[...]
     for ref in (one_ref, two_ref, three_ref):
         total = total + ref[...].astype(F32)
@@ -272,10 +272,11 @@
 
 
 def from_others(x, axis="pair"):
-    return [
-        lax.ppermute(x if axis == "pair" else x[s], axis, [(i, (i + s) % 4) for i in range(4)])
-        for s in range(1, 4)
-    ]
+    moved = {
+        s: lax.ppermute(x if axis == "pair" else x[s], axis, [(i, (i + s) % 4) for i in range(4)])
+        for s in (1, 3, 2)
+    }
+    return [moved[s] for s in range(1, 4)]
 
 
 def shards(three_centre, block_mask, block_owner, block_index, active_orbitals, inactive_orbitals):
@@ -329,7 +330,7 @@
         ],
         compiler_params=limit(8192),
         name="expand",
-    )(message, one, two, three, blocks, keep_mask, pick_mask)
+    )(message, one, three, two, blocks, keep_mask, pick_mask)
     swap = [(0, 1), (1, 0)]
     chip_sum = (keep + lax.ppermute(send, "core", swap).astype(F32)).reshape(NX, NZ * MSG, BW)
     one, two, three = from_others(chip_sum.astype(BF16), "x")
@@ -340,7 +341,7 @@
         out_specs=VMEM,
         compiler_params=limit(4096),
         name="along_x",
-    )(chip_sum[0], one, two, three)
+    )(chip_sum[0], one, three, two)
     along_z = lax.all_to_all(pieces, "z", 0, 0, tiled=True)
     pieces = pl.pallas_call(
         route_kernel,

time: 58.3 us -> 58.4 us (level)
  starting transfers between devices: 15 us -> 16.6 us
  blocking collectives: 27.3 us -> 26.1 us
    ppermute x6, starting transfers between devices: 8.35 us -> 9.58 us  [from_others(): lax.ppermute(x if axis == 'pair' else x[s], axis, [(i, (i + s) % 4) for i...]
    all_to_all x1, blocking collectives: 10.9 us -> 9.78 us  [shards(): received = lax.all_to_all(pieces, ('pair', 'x'), 0, 0, tiled=True)]
  transfers between devices with their start and end apart: 8 -> 8, of which waited for: 6 -> 7; matrix products, arithmetic and copies ran while one was open for 0% -> 0% of each run, Pallas kernels for 0% -> 0%
where the time goes in v7:
time: 58.4 us; the launch traced here: 58.2 us
  blocking collectives  26.1 us (45%)
  starting transfers between devices  16.6 us (28%)
  waiting for transfers between devices  8.88 us (15%)
  Pallas kernels  5.8 us (10%)
  between operations  0.68 us (1%)
    all_to_all x1, blocking collectives, shards(): along_z = lax.all_to_all(pieces, 'z', 0, 0, tiled=True)  16.4 us
    all_to_all x1, blocking collectives, shards(): received = lax.all_to_all(pieces, ('pair', 'x'), 0, 0, tiled=True)  9.78 us
    ppermute x6, starting transfers between devices, from_others(): lax.ppermute(x if axis == 'pair' else x[s], axis, [(i, (i + s) % 4) for i...  9.58 us
    ppermute x6, waiting for transfers between devices, from_others(): lax.ppermute(x if axis == 'pair' else x[s], axis, [(i, (i + s) % 4) for i...  6.74 us
    ppermute x1, starting transfers between devices, shards(): partner = lax.ppermute(received, 'core', swap)  4.56 us
    pallas_call x1, Pallas kernels, shards(): pl.pallas_call(contract_kernel, out_shape=[pltpu.VMEM((ACT, GROUPS * BW),...  3.29 us
    ppermute x1, starting transfers between devices, shards(): lax.ppermute(send, 'core', swap).astype(F32)  2.47 us
    pallas_call x1, Pallas kernels, shards(): pl.pallas_call(expand_kernel, out_shape=[pltpu.VMEM((rows, BW), F32), plt...  1.33 us
  transfers between devices with their start and end apart: 8, of which 7 were waited for; matrix products, arithmetic and copies ran while one was open for 0% of the time, Pallas kernels for 0%

profile of v7, /device:TPU:1, one launch (start us, length us, event | category | flops | bytes accessed | tf_op | source)
XLA Modules:
  0.0 58.2 jit_solution(7456143970119487838)
XLA Ops:
  0.6 3.3 %contract.1 = (bf16[24,512]{1,0:T(8,128)(2,1)S(1)}, bf16[4,20,128,128]{3,2,1,0:T(8,128)(2,1)S(1)}, bf16[128,128]{1,0:T(8,128)(2,1)S(1)}, bf16[128,128]{1,0:T(8,1...) custom-call(s32[16]{0:T(128)} %mask_hbm.1, s32[16]{0:T(128)} %owner_hbm.1, s32[2,16]{1,0:T(2,128)} %index_hbm.1, ...), custom_call_target="tpu_custom_call" | custom-call | tf_op jit(solution)/shard_map/contract/pallas_call | solution.py:288
  3.9 3.8 %collective-permute-start.2 = (bf16[24,512]{1,0:T(8,128)(2,1)S(1)}, bf16[24,512]{1,0:T(8,128)(2,1)S(1)}, u32[]{:S(2)}, u32[]{:S(2)}) collective-permute-start(bf16[24,512]{1,0:T(8,128)(2,1)S(1)} %get-tuple-element.14.own_ref), channel_id=1, source_target_pairs={{0,2},{1,3},{2,0},{3,1},{4,6},{5,7},{6,4},{7,5},{8,10},{9,11},{10,... | collective-permute-start | bytes 73736 | tf_op jit(solution)/shard_map/ppermute | solution.py:276
  7.7 0.8 %collective-permute-start.1 = (bf16[24,512]{1,0:T(8,128)(2,1)S(1)}, bf16[24,512]{1,0:T(8,128)(2,1)S(1)}, u32[]{:S(2)}, u32[]{:S(2)}) collective-permute-start(bf16[24,512]{1,0:T(8,128)(2,1)S(1)} %get-tuple-element.14.own_ref), channel_id=1, source_target_pairs={{0,3},{1,0},{2,1},{3,2},{4,7},{5,4},{6,5},{7,6},{8,11},{9,8},{10,9... | collective-permute-start | bytes 73736 | tf_op jit(solution)/shard_map/ppermute | solution.py:276
  8.5 0.7 %collective-permute-start = (bf16[24,512]{1,0:T(8,128)(2,1)S(1)}, bf16[24,512]{1,0:T(8,128)(2,1)S(1)}, u32[]{:S(2)}, u32[]{:S(2)}) collective-permute-start(bf16[24,512]{1,0:T(8,128)(2,1)S(1)} %get-tuple-element.14.own_ref), channel_id=1, source_target_pairs={{0,1},{1,2},{2,3},{3,0},{4,5},{5,6},{6,7},{7,4},{8,9},{9,10},{10,1... | collective-permute-start | bytes 73736 | tf_op jit(solution)/shard_map/ppermute | solution.py:276
  9.2 0.0 collective-permute-done.2.two_ref
  9.2 1.4 %collective-permute-done.1.three_ref = bf16[24,512]{1,0:T(8,128)(2,1)S(1)} collective-permute-done((bf16[24,512]{1,0:T(8,128)(2,1)S(1)}, bf16[24,512]{1,0:T(8,128)(2,1)S(1)}, u32[]{:S(2)}, u32[]{:S(2)}) %collective-permute-start.1) | collective-permute-done | bytes 24608 | tf_op jit(solution)/shard_map/ppermute | solution.py:276
  10.6 1.8 %collective-permute-done.one_ref = bf16[24,512]{1,0:T(8,128)(2,1)S(1)} collective-permute-done((bf16[24,512]{1,0:T(8,128)(2,1)S(1)}, bf16[24,512]{1,0:T(8,128)(2,1)S(1)}, u32[]{:S(2)}, u32[]{:S(2)}) %collective-permute-start) | collective-permute-done | bytes 24608 | tf_op jit(solution)/shard_map/ppermute | solution.py:276
  12.4 1.3 %expand.1 = (f32[768,128]{1,0:T(8,128)S(1)}, bf16[768,128]{1,0:T(8,128)(2,1)S(1)}) custom-call(bf16[24,512]{1,0:T(8,128)(2,1)S(1)} %get-tuple-element.14.own_ref, bf16[24,512]{1,0:T(8,128)(2,1)S(1)} %collective-permute-done.one_ref, bf16[24,512]{1,0:T(8,128)(2,1)S(1)} %collective-permute-done.1.three_ref, ...), custom_call_target="tpu_custom_call" | custom-call | tf_op jit(solution)/shard_map/expand/pallas_call | solution.py:317
  13.7 2.5 %collective-permute-start.3 = (bf16[768,128]{1,0:T(8,128)(2,1)S(1)}, bf16[768,128]{1,0:T(8,128)(2,1)S(1)}, u32[]{:S(2)}, u32[]{:S(2)}) collective-permute-start(bf16[768,128]{1,0:T(8,128)(2,1)S(1)} %get-tuple-element.19), channel_id=1, source_target_pairs={{0,4},{4,0},{1,5},{5,1},{2,6},{6,2},{3,7},{7,3},{8,12},{12,8},{9,1... | collective-permute-start | bytes 589832 | tf_op jit(solution)/shard_map/ppermute | solution.py:335
  16.2 1.1 %collective-permute-done.3 = bf16[768,128]{1,0:T(8,128)(2,1)S(1)} collective-permute-done((bf16[768,128]{1,0:T(8,128)(2,1)S(1)}, bf16[768,128]{1,0:T(8,128)(2,1)S(1)}, u32[]{:S(2)}, u32[]{:S(2)}) %collective-permute-start.3) | collective-permute-done | bytes 196640 | tf_op jit(solution)/shard_map/ppermute | solution.py:335
  17.3 0.1 fusion
  17.4 2.8 %collective-permute-start.6 = (bf16[192,128]{1,0:T(8,128)(2,1)S(1)}, bf16[192,128]{1,0:T(8,128)(2,1)S(1)}, u32[]{:S(2)}, u32[]{:S(2)}) collective-permute-start(bf16[192,128]{1,0:T(8,128)(2,1)S(1)} %get-tuple-element.24), channel_id=1, source_target_pairs={{0,128},{64,192},{128,0},{192,64},{1,129},{65,193},{129,1},{193,65... | collective-permute-start | bytes 147464 | tf_op jit(solution)/shard_map/ppermute | solution.py:276
  20.2 0.9 %collective-permute-start.5 = (bf16[192,128]{1,0:T(8,128)(2,1)S(1)}, bf16[192,128]{1,0:T(8,128)(2,1)S(1)}, u32[]{:S(2)}, u32[]{:S(2)}) collective-permute-start(bf16[192,128]{1,0:T(8,128)(2,1)S(1)} %get-tuple-element.25), channel_id=1, source_target_pairs={{0,192},{64,0},{128,64},{192,128},{1,193},{65,1},{129,65},{193,129... | collective-permute-start | bytes 147464 | tf_op jit(solution)/shard_map/ppermute | solution.py:276
  21.1 0.6 %collective-permute-start.4 = (bf16[192,128]{1,0:T(8,128)(2,1)S(1)}, bf16[192,128]{1,0:T(8,128)(2,1)S(1)}, u32[]{:S(2)}, u32[]{:S(2)}) collective-permute-start(bf16[192,128]{1,0:T(8,128)(2,1)S(1)} %get-tuple-element.26), channel_id=1, source_target_pairs={{0,64},{64,128},{128,192},{192,0},{1,65},{65,129},{129,193},{193,1... | collective-permute-start | bytes 147464 | tf_op jit(solution)/shard_map/ppermute | solution.py:276
  21.7 0.2 collective-permute-done.6.two_ref
  21.9 1.4 %collective-permute-done.5.three_ref = bf16[192,128]{1,0:T(8,128)(2,1)S(1)} collective-permute-done((bf16[192,128]{1,0:T(8,128)(2,1)S(1)}, bf16[192,128]{1,0:T(8,128)(2,1)S(1)}, u32[]{:S(2)}, u32[]{:S(2)}) %collective-permute-start.5) | collective-permute-done | bytes 49184 | tf_op jit(solution)/shard_map/ppermute | solution.py:276
  23.3 1.9 %collective-permute-done.4.one_ref = bf16[192,128]{1,0:T(8,128)(2,1)S(1)} collective-permute-done((bf16[192,128]{1,0:T(8,128)(2,1)S(1)}, bf16[192,128]{1,0:T(8,128)(2,1)S(1)}, u32[]{:S(2)}, u32[]{:S(2)}) %collective-permute-start.4) | collective-permute-done | bytes 49184 | tf_op jit(solution)/shard_map/ppermute | solution.py:276
  25.2 16.4 %all_to_all.10.parts_ref = bf16[8,80,128]{2,1,0:T(8,128)(2,1)S(1)} all-to-all(bf16[8,80,128]{2,1,0:T(8,128)(2,1)S(1)} %along_x.1), channel_id=1, replica_groups=mesh['x'=4,'z'=8,'core'=2,'pair'=4] {'z'}, dimensions={0} | all-to-all | bytes 327680 | tf_op jit(solution)/shard_map/all_to_all | solution.py:345
  41.6 0.1 route.1
  41.8 9.8 %all_to_all.11.own_ref = bf16[16,48,128]{2,1,0:T(8,128)(2,1)S(1)} all-to-all(bf16[16,48,128]{2,1,0:T(8,128)(2,1)S(1)} %route.1), channel_id=1, replica_groups=mesh['x'=4,'z'=8,'core'=2,'pair'=4] {'pair','x'}, dimensions={0} | all-to-all | bytes 393216 | tf_op jit(solution)/shard_map/all_to_all | solution.py:354
  51.5 4.6 %collective-permute-start.7 = (bf16[16,48,128]{2,1,0:T(8,128)(2,1)S(1)}, bf16[16,48,128]{2,1,0:T(8,128)(2,1)S(1)}, u32[]{:S(2)}, u32[]{:S(2)}) collective-permute-start(bf16[16,48,128]{2,1,0:T(8,128)(2,1)S(1)} %all_to_all.11.own_ref), channel_id=1, source_target_pairs={{0,4},{4,0},{1,5},{5,1},{2,6},{6,2},{3,7},{7,3},{8,12},{12,8},{9,1... | collective-permute-start | bytes 589832 | tf_op jit(solution)/shard_map/ppermute | solution.py:355
  56.1 1.1 %collective-permute-done.7.other_ref = bf16[16,48,128]{2,1,0:T(8,128)(2,1)S(1)} collective-permute-done((bf16[16,48,128]{2,1,0:T(8,128)(2,1)S(1)}, bf16[16,48,128]{2,1,0:T(8,128)(2,1)S(1)}, u32[]{:S(2)}, u32[]{:S(2)}) %collective-permute-start.7) | collective-permute-done | bytes 196640 | tf_op jit(solution)/shard_map/ppermute | solution.py:355
  57.2 1.0 %place.1 = (f32[1024,128]{1,0:T(8,128)}, f32[9,576]{1,0:T(8,128)}) custom-call(bf16[128,128]{1,0:T(8,128)(2,1)S(1)} %get-tuple-element.12.place_ref, bf16[16,48,128]{2,1,0:T(8,128)(2,1)S(1)} %all_to_all.11.own_ref, bf16[16,48,128]{2,1,0:T(8,128)(2,1)S(1)} %collective-permute-done.7.other_ref), custom_call_target="tpu_custom_call" | custom-call | tf_op jit(solution)/shard_map/place/pallas_call | solution.py:356
  (3 shorter events, 0.0 us)
Async XLA Ops:
  3.9 5.3 %collective-permute-start.2 = (bf16[24,512]{1,0:T(8,128)(2,1)S(1)}, bf16[24,512]{1,0:T(8,128)(2,1)S(1)}, u32[]{:S(2)}, u32[]{:S(2)}) collective-permute-start(bf16[24,512]{1,0:T(8,128)(2,1)S(1)} %get-tuple-element.14.own_ref), channel_id=1, source_target_pairs={{0,2},{1,3},{2,0},{3,1},{4,6},{5,7},{6,4},{7,5},{8,10},{9,11},{10,... | collective-permute-start | bytes 73736 | tf_op jit(solution)/shard_map/ppermute | solution.py:276
  7.7 2.9 %collective-permute-start.1 = (bf16[24,512]{1,0:T(8,128)(2,1)S(1)}, bf16[24,512]{1,0:T(8,128)(2,1)S(1)}, u32[]{:S(2)}, u32[]{:S(2)}) collective-permute-start(bf16[24,512]{1,0:T(8,128)(2,1)S(1)} %get-tuple-element.14.own_ref), channel_id=1, source_target_pairs={{0,3},{1,0},{2,1},{3,2},{4,7},{5,4},{6,5},{7,6},{8,11},{9,8},{10,9... | collective-permute-start | bytes 73736 | tf_op jit(solution)/shard_map/ppermute | solution.py:276
  8.5 3.9 %collective-permute-start = (bf16[24,512]{1,0:T(8,128)(2,1)S(1)}, bf16[24,512]{1,0:T(8,128)(2,1)S(1)}, u32[]{:S(2)}, u32[]{:S(2)}) collective-permute-start(bf16[24,512]{1,0:T(8,128)(2,1)S(1)} %get-tuple-element.14.own_ref), channel_id=1, source_target_pairs={{0,1},{1,2},{2,3},{3,0},{4,5},{5,6},{6,7},{7,4},{8,9},{9,10},{10,1... | collective-permute-start | bytes 73736 | tf_op jit(solution)/shard_map/ppermute | solution.py:276
  13.7 3.5 %collective-permute-start.3 = (bf16[768,128]{1,0:T(8,128)(2,1)S(1)}, bf16[768,128]{1,0:T(8,128)(2,1)S(1)}, u32[]{:S(2)}, u32[]{:S(2)}) collective-permute-start(bf16[768,128]{1,0:T(8,128)(2,1)S(1)} %get-tuple-element.19), channel_id=1, source_target_pairs={{0,4},{4,0},{1,5},{5,1},{2,6},{6,2},{3,7},{7,3},{8,12},{12,8},{9,1... | collective-permute-start | bytes 589832 | tf_op jit(solution)/shard_map/ppermute | solution.py:335
  17.4 4.5 %collective-permute-start.6 = (bf16[192,128]{1,0:T(8,128)(2,1)S(1)}, bf16[192,128]{1,0:T(8,128)(2,1)S(1)}, u32[]{:S(2)}, u32[]{:S(2)}) collective-permute-start(bf16[192,128]{1,0:T(8,128)(2,1)S(1)} %get-tuple-element.24), channel_id=1, source_target_pairs={{0,128},{64,192},{128,0},{192,64},{1,129},{65,193},{129,1},{193,65... | collective-permute-start | bytes 147464 | tf_op jit(solution)/shard_map/ppermute | solution.py:276
  20.2 3.1 %collective-permute-start.5 = (bf16[192,128]{1,0:T(8,128)(2,1)S(1)}, bf16[192,128]{1,0:T(8,128)(2,1)S(1)}, u32[]{:S(2)}, u32[]{:S(2)}) collective-permute-start(bf16[192,128]{1,0:T(8,128)(2,1)S(1)} %get-tuple-element.25), channel_id=1, source_target_pairs={{0,192},{64,0},{128,64},{192,128},{1,193},{65,1},{129,65},{193,129... | collective-permute-start | bytes 147464 | tf_op jit(solution)/shard_map/ppermute | solution.py:276
  21.1 4.2 %collective-permute-start.4 = (bf16[192,128]{1,0:T(8,128)(2,1)S(1)}, bf16[192,128]{1,0:T(8,128)(2,1)S(1)}, u32[]{:S(2)}, u32[]{:S(2)}) collective-permute-start(bf16[192,128]{1,0:T(8,128)(2,1)S(1)} %get-tuple-element.26), channel_id=1, source_target_pairs={{0,64},{64,128},{128,192},{192,0},{1,65},{65,129},{129,193},{193,1... | collective-permute-start | bytes 147464 | tf_op jit(solution)/shard_map/ppermute | solution.py:276
  51.5 5.6 %collective-permute-start.7 = (bf16[16,48,128]{2,1,0:T(8,128)(2,1)S(1)}, bf16[16,48,128]{2,1,0:T(8,128)(2,1)S(1)}, u32[]{:S(2)}, u32[]{:S(2)}) collective-permute-start(bf16[16,48,128]{2,1,0:T(8,128)(2,1)S(1)} %all_to_all.11.own_ref), channel_id=1, source_target_pairs={{0,4},{4,0},{1,5},{5,1},{2,6},{6,2},{3,7},{7,3},{8,12},{12,8},{9,1... | collective-permute-start | bytes 589832 | tf_op jit(solution)/shard_map/ppermute | solution.py:355

commit v8 on v4

--- a/solution.py
+++ b/solution.py
@@ -247,24 +247,27 @@
     chosen = jnp.dot(route_ref[...], scaled, preferred_element_type=F32).astype(BF16)
     for o in range(OWNERS):
         for x in range(NX):
-            out_ref[o * NX + x, 0:32, :] = chosen[32 * o : 32 * (o + 1)]
-            out_ref[o * NX + x, 32:48, :] = gram
-
-
-def place_kernel(place_ref, own_ref, other_ref, fock_ref, gram_ref):
+            for c in range(CORES):
+                to = (o * NX + x) * CORES + c
+                out_ref[to, 0:32, :] = chosen[32 * o : 32 * (o + 1)]
+                out_ref[to, 32:48, :] = gram
+
+
+def place_kernel(place_ref, ref, fock_ref, gram_ref):
     core = lax.axis_index("core")
     along = lax.axis_index("x")
     table = place_ref[...]
-    for n, ref in enumerate((own_ref, other_ref)):
-        which = core if n == 0 else 1 - core
+    for c in range(CORES):
         for x in range(NX):
-            pieces = jnp.concatenate([ref[q * NX + x, 0:32, :] for q in range(OWNERS)], axis=0)
+            pieces = jnp.concatenate(
+                [ref[(q * NX + x) * CORES + c, 0:32, :] for q in range(OWNERS)], axis=0
+            )
             placed = jnp.dot(table, pieces, preferred_element_type=F32)
             for rank in range(8):
-                row = pl.multiple_of(rank * BW + 32 * x + 16 * which, 16)
-                fock_ref[pl.ds(row, 16), :] = placed[16 * rank : 16 * (rank + 1)]
+                row = rank * BW + 32 * x + 16 * c
+                fock_ref[row : row + 16, :] = placed[16 * rank : 16 * (rank + 1)]
     for q in range(OWNERS):
-        gram = own_ref[q * NX + along, 32:48, :].astype(F32)
+        gram = ref[(q * NX + along) * CORES + core, 32:48, :].astype(F32)
         gram_ref[:, q * BW : (q + 1) * BW] = gram[0:9]
         if q == 0:
             gram_ref[0:7, 4 * BW : PAIRS] = gram[9:16, 0 : BW // 2]
@@ -344,25 +347,24 @@
     along_z = lax.all_to_all(pieces, "z", 0, 0, tiled=True)
     pieces = pl.pallas_call(
         route_kernel,
-        out_shape=pltpu.VMEM((OWNERS * NX, 48, BW), BF16),
+        out_shape=pltpu.VMEM((OWNERS * NX * CORES, 48, BW), BF16),
         in_specs=[VMEM] * 2,
         out_specs=VMEM,
         compiler_params=limit(4096),
         name="route",
     )(routes, along_z)
-    received = lax.all_to_all(pieces, ("pair", "x"), 0, 0, tiled=True)
-    partner = lax.ppermute(received, "core", swap)
+    received = lax.all_to_all(pieces, ("pair", "x", "core"), 0, 0, tiled=True)
     fock, integrals = pl.pallas_call(
         place_kernel,
         out_shape=[
             jax.ShapeDtypeStruct((8 * BW, BW), F32),
             jax.ShapeDtypeStruct((9, PAIRS), F32),
         ],
-        in_specs=[VMEM] * 3,
+        in_specs=[VMEM] * 2,
         out_specs=[VMEM, VMEM],
         compiler_params=limit(4096),
         name="place",
-    )(places, received, partner)
+    )(places, received)
     return (fock.reshape(8, BW, BW), integrals)
 
 

time: 58.3 us -> 59.1 us (1.014)
  blocking collectives: 27.3 us -> 33.5 us
  starting transfers between devices: 15 us -> 10.6 us
  waiting for transfers between devices: 9.38 us -> 8.3 us
    all_to_all x1, blocking collectives: 10.9 us -> 17.1 us  [shards(): received = lax.all_to_all(pieces, ('pair', 'x', 'core'), 0, 0, tiled=True)]
    ppermute x1 -> x0, starting transfers between devices: 4.37 us -> none  [shards(): partner = lax.ppermute(received, 'core', swap)]
    ppermute x1 -> x0, waiting for transfers between devices: 1.07 us -> none  [shards(): partner = lax.ppermute(received, 'core', swap)]
  transfers between devices with their start and end apart: 8 -> 7, of which waited for: 6 -> 5; matrix products, arithmetic and copies ran while one was open for 0% -> 0% of each run, Pallas kernels for 0% -> 0%
where the time goes in v8:
time: 59.1 us; the launch traced here: 59 us
  blocking collectives  33.5 us (57%)
  starting transfers between devices  10.6 us (18%)
  waiting for transfers between devices  8.3 us (14%)
  Pallas kernels  5.81 us (10%)
  between operations  0.68 us (1%)
    all_to_all x1, blocking collectives, shards(): received = lax.all_to_all(pieces, ('pair', 'x', 'core'), 0, 0, tiled=True)  17.1 us
    all_to_all x1, blocking collectives, shards(): along_z = lax.all_to_all(pieces, 'z', 0, 0, tiled=True)  16.4 us
    ppermute x6, starting transfers between devices, from_others(): lax.ppermute(x if axis == 'pair' else x[s], axis, [(i, (i + s) % 4) for i...  8.35 us
    ppermute x6, waiting for transfers between devices, from_others(): lax.ppermute(x if axis == 'pair' else x[s], axis, [(i, (i + s) % 4) for i...  7.23 us
    pallas_call x1, Pallas kernels, shards(): pl.pallas_call(contract_kernel, out_shape=[pltpu.VMEM((ACT, GROUPS * BW),...  3.29 us
    ppermute x1, starting transfers between devices, shards(): lax.ppermute(send, 'core', swap).astype(F32)  2.27 us
    pallas_call x1, Pallas kernels, shards(): pl.pallas_call(expand_kernel, out_shape=[pltpu.VMEM((rows, BW), F32), plt...  1.33 us
  transfers between devices with their start and end apart: 7, of which 5 were waited for; matrix products, arithmetic and copies ran while one was open for 0% of the time, Pallas kernels for 0%

profile of v8, /device:TPU:1, one launch (start us, length us, event | category | flops | bytes accessed | tf_op | source)
XLA Modules:
  0.0 59.0 jit_solution(3306531845653582733)
XLA Ops:
  0.6 3.3 %contract.1 = (bf16[24,512]{1,0:T(8,128)(2,1)S(1)}, bf16[4,20,128,128]{3,2,1,0:T(8,128)(2,1)S(1)}, bf16[128,128]{1,0:T(8,128)(2,1)S(1)}, bf16[128,128]{1,0:T(8,1...) custom-call(s32[16]{0:T(128)} %mask_hbm.1, s32[16]{0:T(128)} %owner_hbm.1, s32[2,16]{1,0:T(2,128)} %index_hbm.1, ...), custom_call_target="tpu_custom_call" | custom-call | tf_op jit(solution)/shard_map/contract/pallas_call | solution.py:290
  3.9 3.6 %collective-permute-start.2 = (bf16[24,512]{1,0:T(8,128)(2,1)S(1)}, bf16[24,512]{1,0:T(8,128)(2,1)S(1)}, u32[]{:S(2)}, u32[]{:S(2)}) collective-permute-start(bf16[24,512]{1,0:T(8,128)(2,1)S(1)} %get-tuple-element.14.own_ref), channel_id=1, source_target_pairs={{0,3},{1,0},{2,1},{3,2},{4,7},{5,4},{6,5},{7,6},{8,11},{9,8},{10,9... | collective-permute-start | bytes 73736 | tf_op jit(solution)/shard_map/ppermute | solution.py:279
  7.6 0.4 collective-permute-start.1
  7.9 0.7 %collective-permute-start = (bf16[24,512]{1,0:T(8,128)(2,1)S(1)}, bf16[24,512]{1,0:T(8,128)(2,1)S(1)}, u32[]{:S(2)}, u32[]{:S(2)}) collective-permute-start(bf16[24,512]{1,0:T(8,128)(2,1)S(1)} %get-tuple-element.14.own_ref), channel_id=1, source_target_pairs={{0,1},{1,2},{2,3},{3,0},{4,5},{5,6},{6,7},{7,4},{8,9},{9,10},{10,1... | collective-permute-start | bytes 73736 | tf_op jit(solution)/shard_map/ppermute | solution.py:279
  8.6 0.0 collective-permute-done.2.three_ref
  8.6 3.1 %collective-permute-done.1.two_ref = bf16[24,512]{1,0:T(8,128)(2,1)S(1)} collective-permute-done((bf16[24,512]{1,0:T(8,128)(2,1)S(1)}, bf16[24,512]{1,0:T(8,128)(2,1)S(1)}, u32[]{:S(2)}, u32[]{:S(2)}) %collective-permute-start.1) | collective-permute-done | bytes 24608 | tf_op jit(solution)/shard_map/ppermute | solution.py:279
  11.8 0.2 collective-permute-done.one_ref
  12.0 1.3 %expand.1 = (f32[768,128]{1,0:T(8,128)S(1)}, bf16[768,128]{1,0:T(8,128)(2,1)S(1)}) custom-call(bf16[24,512]{1,0:T(8,128)(2,1)S(1)} %get-tuple-element.14.own_ref, bf16[24,512]{1,0:T(8,128)(2,1)S(1)} %collective-permute-done.one_ref, bf16[24,512]{1,0:T(8,128)(2,1)S(1)} %collective-permute-done.1.two_ref, ...), custom_call_target="tpu_custom_call" | custom-call | tf_op jit(solution)/shard_map/expand/pallas_call | solution.py:319
  13.3 2.3 %collective-permute-start.3 = (bf16[768,128]{1,0:T(8,128)(2,1)S(1)}, bf16[768,128]{1,0:T(8,128)(2,1)S(1)}, u32[]{:S(2)}, u32[]{:S(2)}) collective-permute-start(bf16[768,128]{1,0:T(8,128)(2,1)S(1)} %get-tuple-element.19), channel_id=1, source_target_pairs={{0,4},{4,0},{1,5},{5,1},{2,6},{6,2},{3,7},{7,3},{8,12},{12,8},{9,1... | collective-permute-start | bytes 589832 | tf_op jit(solution)/shard_map/ppermute | solution.py:337
  15.6 1.1 %collective-permute-done.3 = bf16[768,128]{1,0:T(8,128)(2,1)S(1)} collective-permute-done((bf16[768,128]{1,0:T(8,128)(2,1)S(1)}, bf16[768,128]{1,0:T(8,128)(2,1)S(1)}, u32[]{:S(2)}, u32[]{:S(2)}) %collective-permute-start.3) | collective-permute-done | bytes 196640 | tf_op jit(solution)/shard_map/ppermute | solution.py:337
  16.7 0.1 fusion
  16.7 2.6 %collective-permute-start.6 = (bf16[192,128]{1,0:T(8,128)(2,1)S(1)}, bf16[192,128]{1,0:T(8,128)(2,1)S(1)}, u32[]{:S(2)}, u32[]{:S(2)}) collective-permute-start(bf16[192,128]{1,0:T(8,128)(2,1)S(1)} %get-tuple-element.24), channel_id=1, source_target_pairs={{0,192},{64,0},{128,64},{192,128},{1,193},{65,1},{129,65},{193,129... | collective-permute-start | bytes 147464 | tf_op jit(solution)/shard_map/ppermute | solution.py:279
  19.3 0.5 collective-permute-start.5
  19.8 0.6 %collective-permute-start.4 = (bf16[192,128]{1,0:T(8,128)(2,1)S(1)}, bf16[192,128]{1,0:T(8,128)(2,1)S(1)}, u32[]{:S(2)}, u32[]{:S(2)}) collective-permute-start(bf16[192,128]{1,0:T(8,128)(2,1)S(1)} %get-tuple-element.26), channel_id=1, source_target_pairs={{0,64},{64,128},{128,192},{192,0},{1,65},{65,129},{129,193},{193,1... | collective-permute-start | bytes 147464 | tf_op jit(solution)/shard_map/ppermute | solution.py:279
  20.4 0.0 collective-permute-done.6.three_ref
  20.5 3.3 %collective-permute-done.5.two_ref = bf16[192,128]{1,0:T(8,128)(2,1)S(1)} collective-permute-done((bf16[192,128]{1,0:T(8,128)(2,1)S(1)}, bf16[192,128]{1,0:T(8,128)(2,1)S(1)}, u32[]{:S(2)}, u32[]{:S(2)}) %collective-permute-start.5) | collective-permute-done | bytes 49184 | tf_op jit(solution)/shard_map/ppermute | solution.py:279
  23.8 0.5 collective-permute-done.4.one_ref
  24.3 16.4 %all_to_all.10.parts_ref = bf16[8,80,128]{2,1,0:T(8,128)(2,1)S(1)} all-to-all(bf16[8,80,128]{2,1,0:T(8,128)(2,1)S(1)} %along_x.1), channel_id=1, replica_groups=mesh['x'=4,'z'=8,'core'=2,'pair'=4] {'z'}, dimensions={0} | all-to-all | bytes 327680 | tf_op jit(solution)/shard_map/all_to_all | solution.py:347
  40.7 0.2 route.1
  40.8 17.1 %all_to_all.11.ref = bf16[32,48,128]{2,1,0:T(8,128)(2,1)S(1)} all-to-all(bf16[32,48,128]{2,1,0:T(8,128)(2,1)S(1)} %route.1), channel_id=1, replica_groups=mesh['x'=4,'z'=8,'core'=2,'pair'=4] {'pair','x','core'}, dimensions={0} | all-to-all | bytes 786432 | tf_op jit(solution)/shard_map/all_to_all | solution.py:356
  58.0 1.0 %place.1 = (f32[1024,128]{1,0:T(8,128)}, f32[9,576]{1,0:T(8,128)}) custom-call(bf16[128,128]{1,0:T(8,128)(2,1)S(1)} %get-tuple-element.12.place_ref, bf16[32,48,128]{2,1,0:T(8,128)(2,1)S(1)} %all_to_all.11.ref), custom_call_target="tpu_custom_call" | custom-call | tf_op jit(solution)/shard_map/place/pallas_call | solution.py:357
  (3 shorter events, 0.0 us)
Async XLA Ops:
  3.9 4.7 %collective-permute-start.2 = (bf16[24,512]{1,0:T(8,128)(2,1)S(1)}, bf16[24,512]{1,0:T(8,128)(2,1)S(1)}, u32[]{:S(2)}, u32[]{:S(2)}) collective-permute-start(bf16[24,512]{1,0:T(8,128)(2,1)S(1)} %get-tuple-element.14.own_ref), channel_id=1, source_target_pairs={{0,3},{1,0},{2,1},{3,2},{4,7},{5,4},{6,5},{7,6},{8,11},{9,8},{10,9... | collective-permute-start | bytes 73736 | tf_op jit(solution)/shard_map/ppermute | solution.py:279
  7.6 4.2 %collective-permute-start.1 = (bf16[24,512]{1,0:T(8,128)(2,1)S(1)}, bf16[24,512]{1,0:T(8,128)(2,1)S(1)}, u32[]{:S(2)}, u32[]{:S(2)}) collective-permute-start(bf16[24,512]{1,0:T(8,128)(2,1)S(1)} %get-tuple-element.14.own_ref), channel_id=1, source_target_pairs={{0,2},{1,3},{2,0},{3,1},{4,6},{5,7},{6,4},{7,5},{8,10},{9,11},{10,... | collective-permute-start | bytes 73736 | tf_op jit(solution)/shard_map/ppermute | solution.py:279
  7.9 4.1 %collective-permute-start = (bf16[24,512]{1,0:T(8,128)(2,1)S(1)}, bf16[24,512]{1,0:T(8,128)(2,1)S(1)}, u32[]{:S(2)}, u32[]{:S(2)}) collective-permute-start(bf16[24,512]{1,0:T(8,128)(2,1)S(1)} %get-tuple-element.14.own_ref), channel_id=1, source_target_pairs={{0,1},{1,2},{2,3},{3,0},{4,5},{5,6},{6,7},{7,4},{8,9},{9,10},{10,1... | collective-permute-start | bytes 73736 | tf_op jit(solution)/shard_map/ppermute | solution.py:279
  13.3 3.3 %collective-permute-start.3 = (bf16[768,128]{1,0:T(8,128)(2,1)S(1)}, bf16[768,128]{1,0:T(8,128)(2,1)S(1)}, u32[]{:S(2)}, u32[]{:S(2)}) collective-permute-start(bf16[768,128]{1,0:T(8,128)(2,1)S(1)} %get-tuple-element.19), channel_id=1, source_target_pairs={{0,4},{4,0},{1,5},{5,1},{2,6},{6,2},{3,7},{7,3},{8,12},{12,8},{9,1... | collective-permute-start | bytes 589832 | tf_op jit(solution)/shard_map/ppermute | solution.py:337
  16.7 3.7 %collective-permute-start.6 = (bf16[192,128]{1,0:T(8,128)(2,1)S(1)}, bf16[192,128]{1,0:T(8,128)(2,1)S(1)}, u32[]{:S(2)}, u32[]{:S(2)}) collective-permute-start(bf16[192,128]{1,0:T(8,128)(2,1)S(1)} %get-tuple-element.24), channel_id=1, source_target_pairs={{0,192},{64,0},{128,64},{192,128},{1,193},{65,1},{129,65},{193,129... | collective-permute-start | bytes 147464 | tf_op jit(solution)/shard_map/ppermute | solution.py:279
  19.3 4.5 %collective-permute-start.5 = (bf16[192,128]{1,0:T(8,128)(2,1)S(1)}, bf16[192,128]{1,0:T(8,128)(2,1)S(1)}, u32[]{:S(2)}, u32[]{:S(2)}) collective-permute-start(bf16[192,128]{1,0:T(8,128)(2,1)S(1)} %get-tuple-element.25), channel_id=1, source_target_pairs={{0,128},{64,192},{128,0},{192,64},{1,129},{65,193},{129,1},{193,65... | collective-permute-start | bytes 147464 | tf_op jit(solution)/shard_map/ppermute | solution.py:279
  19.8 4.5 %collective-permute-start.4 = (bf16[192,128]{1,0:T(8,128)(2,1)S(1)}, bf16[192,128]{1,0:T(8,128)(2,1)S(1)}, u32[]{:S(2)}, u32[]{:S(2)}) collective-permute-start(bf16[192,128]{1,0:T(8,128)(2,1)S(1)} %get-tuple-element.26), channel_id=1, source_target_pairs={{0,64},{64,128},{128,192},{192,0},{1,65},{65,129},{129,193},{193,1... | collective-permute-start | bytes 147464 | tf_op jit(solution)/shard_map/ppermute | solution.py:279

commit v9 on v4

--- a/solution.py
+++ b/solution.py
@@ -331,8 +331,10 @@
         name="expand",
     )(message, one, two, three, blocks, keep_mask, pick_mask)
     swap = [(0, 1), (1, 0)]
-    chip_sum = (keep + lax.ppermute(send, "core", swap).astype(F32)).reshape(NX, NZ * MSG, BW)
-    one, two, three = from_others(chip_sum.astype(BF16), "x")
+    kept = keep.reshape(NX, NZ * MSG, BW)
+    taken = lax.ppermute(send, "core", swap).reshape(NX, NZ * MSG, BW)
+    sums = [kept[s] + taken[s].astype(F32) for s in range(NX)]
+    one, two, three = from_others([v.astype(BF16) for v in sums], "x")
     pieces = pl.pallas_call(
         along_x_kernel,
         out_shape=pltpu.VMEM((NZ, 80, BW), BF16),
@@ -340,7 +342,7 @@
         out_specs=VMEM,
         compiler_params=limit(4096),
         name="along_x",
-    )(chip_sum[0], one, two, three)
+    )(sums[0], one, two, three)
     along_z = lax.all_to_all(pieces, "z", 0, 0, tiled=True)
     pieces = pl.pallas_call(
         route_kernel,

time: 58.3 us -> 58.3 us (level)
  transfers between devices with their start and end apart: 8 -> 8, of which waited for: 6 -> 7; matrix products, arithmetic and copies ran while one was open for 0% -> 0% of each run, Pallas kernels for 0% -> 0%
where the time goes in v9:
time: 58.3 us; the launch traced here: 58.2 us
  blocking collectives  27.3 us (47%)
  starting transfers between devices  15 us (26%)
  waiting for transfers between devices  9.38 us (16%)
  Pallas kernels  5.81 us (10%)
  between operations  0.67 us (1%)
    all_to_all x1, blocking collectives, shards(): along_z = lax.all_to_all(pieces, 'z', 0, 0, tiled=True)  16.4 us
    all_to_all x1, blocking collectives, shards(): received = lax.all_to_all(pieces, ('pair', 'x'), 0, 0, tiled=True)  10.9 us
    ppermute x6, starting transfers between devices, from_others(): lax.ppermute(x if axis == 'pair' else x[s], axis, [(i, (i + s) % 4) for i...  8.35 us
    ppermute x6, waiting for transfers between devices, from_others(): lax.ppermute(x if axis == 'pair' else x[s], axis, [(i, (i + s) % 4) for i...  7.24 us
    ppermute x1, starting transfers between devices, shards(): partner = lax.ppermute(received, 'core', swap)  4.37 us
    pallas_call x1, Pallas kernels, shards(): pl.pallas_call(contract_kernel, out_shape=[pltpu.VMEM((ACT, GROUPS * BW),...  3.29 us
    ppermute x1, starting transfers between devices, shards(): taken = lax.ppermute(send, 'core', swap).reshape(NX, NZ * MSG, BW)  2.27 us
    pallas_call x1, Pallas kernels, shards(): pl.pallas_call(expand_kernel, out_shape=[pltpu.VMEM((rows, BW), F32), plt...  1.33 us
  transfers between devices with their start and end apart: 8, of which 7 were waited for; matrix products, arithmetic and copies ran while one was open for 0% of the time, Pallas kernels for 0%

profile of v9, /device:TPU:1, one launch (start us, length us, event | category | flops | bytes accessed | tf_op | source)
XLA Modules:
  0.0 58.2 jit_solution(15622820916146531479)
XLA Ops:
  0.6 3.3 %contract.1 = (bf16[24,512]{1,0:T(8,128)(2,1)S(1)}, bf16[4,20,128,128]{3,2,1,0:T(8,128)(2,1)S(1)}, bf16[128,128]{1,0:T(8,128)(2,1)S(1)}, bf16[128,128]{1,0:T(8,1...) custom-call(s32[16]{0:T(128)} %mask_hbm.1, s32[16]{0:T(128)} %owner_hbm.1, s32[2,16]{1,0:T(2,128)} %index_hbm.1, ...), custom_call_target="tpu_custom_call" | custom-call | tf_op jit(solution)/shard_map/contract/pallas_call | solution.py:287
  3.9 3.6 %collective-permute-start.2 = (bf16[24,512]{1,0:T(8,128)(2,1)S(1)}, bf16[24,512]{1,0:T(8,128)(2,1)S(1)}, u32[]{:S(2)}, u32[]{:S(2)}) collective-permute-start(bf16[24,512]{1,0:T(8,128)(2,1)S(1)} %get-tuple-element.14.own_ref), channel_id=1, source_target_pairs={{0,3},{1,0},{2,1},{3,2},{4,7},{5,4},{6,5},{7,6},{8,11},{9,8},{10,9... | collective-permute-start | bytes 73736 | tf_op jit(solution)/shard_map/ppermute | solution.py:276
  7.6 0.4 collective-permute-start.1
  7.9 0.7 %collective-permute-start = (bf16[24,512]{1,0:T(8,128)(2,1)S(1)}, bf16[24,512]{1,0:T(8,128)(2,1)S(1)}, u32[]{:S(2)}, u32[]{:S(2)}) collective-permute-start(bf16[24,512]{1,0:T(8,128)(2,1)S(1)} %get-tuple-element.14.own_ref), channel_id=1, source_target_pairs={{0,1},{1,2},{2,3},{3,0},{4,5},{5,6},{6,7},{7,4},{8,9},{9,10},{10,1... | collective-permute-start | bytes 73736 | tf_op jit(solution)/shard_map/ppermute | solution.py:276
  8.6 0.0 collective-permute-done.2.three_ref
  8.6 3.1 %collective-permute-done.1.two_ref = bf16[24,512]{1,0:T(8,128)(2,1)S(1)} collective-permute-done((bf16[24,512]{1,0:T(8,128)(2,1)S(1)}, bf16[24,512]{1,0:T(8,128)(2,1)S(1)}, u32[]{:S(2)}, u32[]{:S(2)}) %collective-permute-start.1) | collective-permute-done | bytes 24608 | tf_op jit(solution)/shard_map/ppermute | solution.py:276
  11.7 0.2 collective-permute-done.one_ref
  12.0 1.3 %expand.1 = (f32[768,128]{1,0:T(8,128)S(1)}, bf16[768,128]{1,0:T(8,128)(2,1)S(1)}) custom-call(bf16[24,512]{1,0:T(8,128)(2,1)S(1)} %get-tuple-element.14.own_ref, bf16[24,512]{1,0:T(8,128)(2,1)S(1)} %collective-permute-done.one_ref, bf16[24,512]{1,0:T(8,128)(2,1)S(1)} %collective-permute-done.1.two_ref, ...), custom_call_target="tpu_custom_call" | custom-call | tf_op jit(solution)/shard_map/expand/pallas_call | solution.py:316
  13.3 2.3 %collective-permute-start.3 = (bf16[768,128]{1,0:T(8,128)(2,1)S(1)}, bf16[768,128]{1,0:T(8,128)(2,1)S(1)}, u32[]{:S(2)}, u32[]{:S(2)}) collective-permute-start(bf16[768,128]{1,0:T(8,128)(2,1)S(1)} %get-tuple-element.19), channel_id=1, source_target_pairs={{0,4},{4,0},{1,5},{5,1},{2,6},{6,2},{3,7},{7,3},{8,12},{12,8},{9,1... | collective-permute-start | bytes 589832 | tf_op jit(solution)/shard_map/ppermute | solution.py:335
  15.6 1.1 %collective-permute-done.3 = bf16[768,128]{1,0:T(8,128)(2,1)S(1)} collective-permute-done((bf16[768,128]{1,0:T(8,128)(2,1)S(1)}, bf16[768,128]{1,0:T(8,128)(2,1)S(1)}, u32[]{:S(2)}, u32[]{:S(2)}) %collective-permute-start.3) | collective-permute-done | bytes 196640 | tf_op jit(solution)/shard_map/ppermute | solution.py:335
  16.7 2.6 %collective-permute-start.6 = (bf16[192,128]{1,0:T(8,128)(2,1)S(1)}, bf16[192,128]{1,0:T(8,128)(2,1)S(1)}, u32[]{:S(2)}, u32[]{:S(2)}) collective-permute-start(bf16[192,128]{1,0:T(8,128)(2,1)S(1)} %get-tuple-element.22), channel_id=1, source_target_pairs={{0,192},{64,0},{128,64},{192,128},{1,193},{65,1},{129,65},{193,129... | collective-permute-start | bytes 147464 | tf_op jit(solution)/shard_map/ppermute | solution.py:276
  19.3 0.5 collective-permute-start.5
  19.8 0.6 %collective-permute-start.4 = (bf16[192,128]{1,0:T(8,128)(2,1)S(1)}, bf16[192,128]{1,0:T(8,128)(2,1)S(1)}, u32[]{:S(2)}, u32[]{:S(2)}) collective-permute-start(bf16[192,128]{1,0:T(8,128)(2,1)S(1)} %get-tuple-element.24), channel_id=1, source_target_pairs={{0,64},{64,128},{128,192},{192,0},{1,65},{65,129},{129,193},{193,1... | collective-permute-start | bytes 147464 | tf_op jit(solution)/shard_map/ppermute | solution.py:276
  20.4 0.1 collective-permute-done.6.three_ref
  20.5 3.3 %collective-permute-done.5.two_ref = bf16[192,128]{1,0:T(8,128)(2,1)S(1)} collective-permute-done((bf16[192,128]{1,0:T(8,128)(2,1)S(1)}, bf16[192,128]{1,0:T(8,128)(2,1)S(1)}, u32[]{:S(2)}, u32[]{:S(2)}) %collective-permute-start.5) | collective-permute-done | bytes 49184 | tf_op jit(solution)/shard_map/ppermute | solution.py:276
  23.7 0.5 collective-permute-done.4.one_ref
  24.3 16.4 %all_to_all.10.parts_ref = bf16[8,80,128]{2,1,0:T(8,128)(2,1)S(1)} all-to-all(bf16[8,80,128]{2,1,0:T(8,128)(2,1)S(1)} %along_x.1), channel_id=1, replica_groups=mesh['x'=4,'z'=8,'core'=2,'pair'=4] {'z'}, dimensions={0} | all-to-all | bytes 327680 | tf_op jit(solution)/shard_map/all_to_all | solution.py:346
  40.6 0.1 route.1
  40.8 10.9 %all_to_all.11.own_ref = bf16[16,48,128]{2,1,0:T(8,128)(2,1)S(1)} all-to-all(bf16[16,48,128]{2,1,0:T(8,128)(2,1)S(1)} %route.1), channel_id=1, replica_groups=mesh['x'=4,'z'=8,'core'=2,'pair'=4] {'pair','x'}, dimensions={0} | all-to-all | bytes 393216 | tf_op jit(solution)/shard_map/all_to_all | solution.py:355
  51.7 4.4 %collective-permute-start.7 = (bf16[16,48,128]{2,1,0:T(8,128)(2,1)S(1)}, bf16[16,48,128]{2,1,0:T(8,128)(2,1)S(1)}, u32[]{:S(2)}, u32[]{:S(2)}) collective-permute-start(bf16[16,48,128]{2,1,0:T(8,128)(2,1)S(1)} %all_to_all.11.own_ref), channel_id=1, source_target_pairs={{0,4},{4,0},{1,5},{5,1},{2,6},{6,2},{3,7},{7,3},{8,12},{12,8},{9,1... | collective-permute-start | bytes 589832 | tf_op jit(solution)/shard_map/ppermute | solution.py:356
  56.1 1.1 %collective-permute-done.7.other_ref = bf16[16,48,128]{2,1,0:T(8,128)(2,1)S(1)} collective-permute-done((bf16[16,48,128]{2,1,0:T(8,128)(2,1)S(1)}, bf16[16,48,128]{2,1,0:T(8,128)(2,1)S(1)}, u32[]{:S(2)}, u32[]{:S(2)}) %collective-permute-start.7) | collective-permute-done | bytes 196640 | tf_op jit(solution)/shard_map/ppermute | solution.py:356
  57.1 1.0 %place.1 = (f32[1024,128]{1,0:T(8,128)}, f32[9,576]{1,0:T(8,128)}) custom-call(bf16[128,128]{1,0:T(8,128)(2,1)S(1)} %get-tuple-element.12.place_ref, bf16[16,48,128]{2,1,0:T(8,128)(2,1)S(1)} %all_to_all.11.own_ref, bf16[16,48,128]{2,1,0:T(8,128)(2,1)S(1)} %collective-permute-done.7.other_ref), custom_call_target="tpu_custom_call" | custom-call | tf_op jit(solution)/shard_map/place/pallas_call | solution.py:357
  (2 shorter events, 0.1 us)
Async XLA Ops:
  3.9 4.7 %collective-permute-start.2 = (bf16[24,512]{1,0:T(8,128)(2,1)S(1)}, bf16[24,512]{1,0:T(8,128)(2,1)S(1)}, u32[]{:S(2)}, u32[]{:S(2)}) collective-permute-start(bf16[24,512]{1,0:T(8,128)(2,1)S(1)} %get-tuple-element.14.own_ref), channel_id=1, source_target_pairs={{0,3},{1,0},{2,1},{3,2},{4,7},{5,4},{6,5},{7,6},{8,11},{9,8},{10,9... | collective-permute-start | bytes 73736 | tf_op jit(solution)/shard_map/ppermute | solution.py:276
  7.6 4.2 %collective-permute-start.1 = (bf16[24,512]{1,0:T(8,128)(2,1)S(1)}, bf16[24,512]{1,0:T(8,128)(2,1)S(1)}, u32[]{:S(2)}, u32[]{:S(2)}) collective-permute-start(bf16[24,512]{1,0:T(8,128)(2,1)S(1)} %get-tuple-element.14.own_ref), channel_id=1, source_target_pairs={{0,2},{1,3},{2,0},{3,1},{4,6},{5,7},{6,4},{7,5},{8,10},{9,11},{10,... | collective-permute-start | bytes 73736 | tf_op jit(solution)/shard_map/ppermute | solution.py:276
  7.9 4.1 %collective-permute-start = (bf16[24,512]{1,0:T(8,128)(2,1)S(1)}, bf16[24,512]{1,0:T(8,128)(2,1)S(1)}, u32[]{:S(2)}, u32[]{:S(2)}) collective-permute-start(bf16[24,512]{1,0:T(8,128)(2,1)S(1)} %get-tuple-element.14.own_ref), channel_id=1, source_target_pairs={{0,1},{1,2},{2,3},{3,0},{4,5},{5,6},{6,7},{7,4},{8,9},{9,10},{10,1... | collective-permute-start | bytes 73736 | tf_op jit(solution)/shard_map/ppermute | solution.py:276
  13.3 3.3 %collective-permute-start.3 = (bf16[768,128]{1,0:T(8,128)(2,1)S(1)}, bf16[768,128]{1,0:T(8,128)(2,1)S(1)}, u32[]{:S(2)}, u32[]{:S(2)}) collective-permute-start(bf16[768,128]{1,0:T(8,128)(2,1)S(1)} %get-tuple-element.19), channel_id=1, source_target_pairs={{0,4},{4,0},{1,5},{5,1},{2,6},{6,2},{3,7},{7,3},{8,12},{12,8},{9,1... | collective-permute-start | bytes 589832 | tf_op jit(solution)/shard_map/ppermute | solution.py:335
  16.7 3.7 %collective-permute-start.6 = (bf16[192,128]{1,0:T(8,128)(2,1)S(1)}, bf16[192,128]{1,0:T(8,128)(2,1)S(1)}, u32[]{:S(2)}, u32[]{:S(2)}) collective-permute-start(bf16[192,128]{1,0:T(8,128)(2,1)S(1)} %get-tuple-element.22), channel_id=1, source_target_pairs={{0,192},{64,0},{128,64},{192,128},{1,193},{65,1},{129,65},{193,129... | collective-permute-start | bytes 147464 | tf_op jit(solution)/shard_map/ppermute | solution.py:276
  19.3 4.5 %collective-permute-start.5 = (bf16[192,128]{1,0:T(8,128)(2,1)S(1)}, bf16[192,128]{1,0:T(8,128)(2,1)S(1)}, u32[]{:S(2)}, u32[]{:S(2)}) collective-permute-start(bf16[192,128]{1,0:T(8,128)(2,1)S(1)} %get-tuple-element.23), channel_id=1, source_target_pairs={{0,128},{64,192},{128,0},{192,64},{1,129},{65,193},{129,1},{193,65... | collective-permute-start | bytes 147464 | tf_op jit(solution)/shard_map/ppermute | solution.py:276
  19.8 4.5 %collective-permute-start.4 = (bf16[192,128]{1,0:T(8,128)(2,1)S(1)}, bf16[192,128]{1,0:T(8,128)(2,1)S(1)}, u32[]{:S(2)}, u32[]{:S(2)}) collective-permute-start(bf16[192,128]{1,0:T(8,128)(2,1)S(1)} %get-tuple-element.24), channel_id=1, source_target_pairs={{0,64},{64,128},{128,192},{192,0},{1,65},{65,129},{129,193},{193,1... | collective-permute-start | bytes 147464 | tf_op jit(solution)/shard_map/ppermute | solution.py:276
  51.7 5.4 %collective-permute-start.7 = (bf16[16,48,128]{2,1,0:T(8,128)(2,1)S(1)}, bf16[16,48,128]{2,1,0:T(8,128)(2,1)S(1)}, u32[]{:S(2)}, u32[]{:S(2)}) collective-permute-start(bf16[16,48,128]{2,1,0:T(8,128)(2,1)S(1)} %all_to_all.11.own_ref), channel_id=1, source_target_pairs={{0,4},{4,0},{1,5},{5,1},{2,6},{6,2},{3,7},{7,3},{8,12},{12,8},{9,1... | collective-permute-start | bytes 589832 | tf_op jit(solution)/shard_map/ppermute | solution.py:356
